TPU v7x, 512 devices: a whole 4x8x8 slice. The times are simulated.
512 devices in a mesh: group: 16 (over y, core), slab: 32 (over z, x).
Axes of the slice: x: 4, y: 8, z: 8, core: 2. Of those that a mesh axis runs over, the one named last changes fastest.
Arguments:
- state: float32 [32, 256, 32, 256], P('group', 'slab'), may hold values from -3 to 3
- theta: float32 [32, 128, 16, 128], P('group', 'slab'), may hold values from -2.5 to 2.5
- forcing: float32 [256, 32, 256], P('slab'), may hold values from -6 to 6
- boxes: int32 [6, 16384], replicated, may hold values from 0 to 256, as said below
- observed: float32 [16384], P('slab'), may hold values from -6 to 6
- noise_var: float32 [16384], P('slab'), may hold values from 0.05 to 0.5
- perturb: float32 [32, 16384], P('group', 'slab'), may hold values from -6 to 6
Outputs:
- final_state: float32 [32, 256, 32, 256], P('group', 'slab')
- theta_new: float32 [32, 128, 16, 128], P('group', 'slab')
Inputs may be any that keep to these rules, and one draw needn't show every extreme that they name: `boxes`: for every observation z0 < z1 <= 256, y0 < y1 <= 8, x0 < x1 <= 64; a box spans at most 16 planes, 4 tiles along the second dimension and 8 along the third (fewer where the grid is narrower), and these most are reached.
All inputs are finite; a program needn't handle non-finite values.
Results may differ from a plain program's by a relative error of at most 0.00019.
Values sent between devices are 32-bit elements; how exact they have to be, the bound alone decides.
No kernel may reach another device: no remote copies, remote signals or barrier semaphores. Data moves between devices by JAX's collectives and lax.ppermute only.
A program may use at most 64 MiB of HBM per device.

v0:
```python
import jax
import jax.numpy as jnp
from jax import lax
from jax.sharding import PartitionSpec as P

STEP_SIZE = 0.1


def extended(cells, sides, width):
    for axis, dim in sides:
        count = lax.axis_size(axis)
        ends = count - 1
        head = lax.slice_in_dim(cells, 0, width, axis=dim)
        tail = lax.slice_in_dim(cells, cells.shape[dim] - width, cells.shape[dim], axis=dim)
        cells = jnp.concatenate(
            [
                lax.ppermute(tail, axis, [(i, (i + 1) % count) for i in range(ends)]),
                cells,
                lax.ppermute(head, axis, [((i + 1) % count, i) for i in range(ends)]),
            ],
            axis=dim,
        )
    return cells


def split_up(shard, dim, peers):
    shape = shard.shape
    parts = shard.reshape(*shape[:dim], peers, shape[dim] // peers, *shape[dim + 1 :])
    return jnp.moveaxis(parts, dim, 0)


def sum_at_owner(shard, axis, dim):
    parts = split_up(shard, dim, lax.axis_size(axis))
    arrived = lax.all_to_all(parts, axis, split_axis=0, concat_axis=0, tiled=True)
    return arrived.sum(axis=0)


def sent_together(arrays, axis, dim, along):
    both = jnp.concatenate(arrays, axis=along)
    filled, at, outs = (lax.all_gather(both, axis, axis=dim, tiled=True), 0, [])
    for a in arrays:
        outs.append(lax.slice_in_dim(filled, at, at + a.shape[along], axis=along))
        at += a.shape[along]
    return tuple(outs)


def sent_to_all(shard, axis):
    copies = jnp.broadcast_to(shard, (lax.axis_size(axis), *shard.shape))
    return lax.all_to_all(copies, axis, split_axis=0, concat_axis=0, tiled=True)


def of_everyone(shard, axis):
    everything = sent_to_all(shard, axis)
    return jnp.sum(everything, axis=0)


def in_one(arrays, axis):
    ends = [0]
    for a in arrays:
        ends.append(ends[-1] + a.size)
    running = of_everyone(jnp.concatenate([a.ravel() for a in arrays]), axis)
    return tuple((running[b:e].reshape(a.shape) for a, b, e in zip(arrays, ends, ends[1:])))


def advance(padded, diffusivity, forcing):
    center = padded[:, 1:-1]
    side_pad = jnp.pad(center, ((0, 0), (0, 0), (1, 1), (1, 1)))
    beside_all = padded[:, 2:] + padded[:, :-2]
    beside_all = beside_all + side_pad[:, :, 2:, 1:-1] + side_pad[:, :, :-2, 1:-1]
    beside_all = beside_all + side_pad[:, :, 1:-1, 2:] + side_pad[:, :, 1:-1, :-2]
    change = (
        diffusivity * (beside_all - 6.0 * center) + 0.5 * center * (1.0 - center * center) + forcing
    )
    return center + STEP_SIZE * change


def upsample(params):
    return jnp.repeat(jnp.repeat(jnp.repeat(params, 2, axis=1), 2, axis=2), 2, axis=3)


def local(state, theta, forcing, boxes, observed, noise_var, perturb):
    mem_local, planes, rows_y, rows_x = state.shape
    slab_index = lax.axis_index("slab")
    diffusivity = 0.5 * jnp.exp(upsample(theta))
    current = state
    for sweep in range(2):
        padded = extended(current, (("slab", 1),), 1)
        current = advance(padded, diffusivity, forcing[None])
    tiles_y = rows_y // 4
    tiles_x = rows_x // 4
    tiles = current.reshape(mem_local, planes, tiles_y, 4, tiles_x, 4).sum(axis=(3, 5))
    tile_rows = tiles.reshape(mem_local * planes * tiles_y, tiles_x)
    obs_total = boxes.shape[1]
    width = 2048
    box_blocks = jnp.moveaxis(boxes.reshape(6, obs_total // width, width), 1, 0)
    plane_global = slab_index * planes + jnp.arange(planes, dtype=jnp.int32)
    index_y = jnp.arange(tiles_y, dtype=jnp.int32)
    index_x = jnp.arange(tiles_x, dtype=jnp.int32)

    def observe(block):
        in_x = ((index_x[:, None] >= block[4][None]) & (index_x[:, None] < block[5][None])).astype(
            jnp.float32
        )
        in_y = ((index_y[:, None] >= block[2][None]) & (index_y[:, None] < block[3][None])).astype(
            jnp.float32
        )
        in_z = (
            (plane_global[:, None] >= block[0][None]) & (plane_global[:, None] < block[1][None])
        ).astype(jnp.float32)
        count = ((block[1] - block[0]) * (block[3] - block[2]) * (block[5] - block[4]) * 16).astype(
            jnp.float32
        )
        along_x = jnp.dot(tile_rows, in_x, precision=lax.Precision.HIGHEST)
        along_x = along_x.reshape(mem_local, planes, tiles_y, width)
        weight = in_z[:, None, :] * in_y[None, :, :] / count[None, None, :]
        return jnp.sum(along_x * weight[None], axis=(1, 2))

    partial_value = lax.map(observe, box_blocks)
    partial_value = jnp.moveaxis(partial_value, 0, 1).reshape(mem_local, obs_total)
    pred_share = sum_at_owner(partial_value, "slab", 1)
    predicted, perturbs = sent_together((pred_share, perturb), "group", 0, 1)
    members = predicted.shape[0]
    scale = jnp.sqrt(jnp.float32(members - 1))
    anomaly = (predicted - jnp.mean(predicted, axis=0, keepdims=True)) / scale
    misfit = observed[None] + jnp.sqrt(noise_var)[None] * perturbs - predicted
    weighted = anomaly / noise_var[None]
    inner_part = jnp.dot(weighted, anomaly.T, precision=lax.Precision.HIGHEST)
    cross_part = jnp.dot(weighted, misfit.T, precision=lax.Precision.HIGHEST)
    inner, cross = in_one((inner_part, cross_part), "slab")
    identity = jnp.eye(members, dtype=jnp.float32)
    factor = jnp.linalg.cholesky(identity + inner)
    gain = jax.scipy.linalg.cho_solve((factor, True), cross)
    mixing = identity + (gain - jnp.mean(gain, axis=0, keepdims=True)) / scale
    flat_theta = theta.reshape(mem_local, -1)
    regrouped = lax.all_to_all(flat_theta, "group", split_axis=1, concat_axis=0, tiled=True)
    blended = jnp.dot(mixing.T, regrouped, precision=lax.Precision.HIGHEST)
    updated = lax.all_to_all(blended, "group", split_axis=0, concat_axis=1, tiled=True)
    return (current, updated.reshape(theta.shape))


def solution(mesh):
    return jax.shard_map(
        local,
        mesh=mesh,
        in_specs=(
            P("group", "slab", None, None),
            P("group", "slab", None, None),
            P("slab", None, None),
            P(),
            P("slab"),
            P("slab"),
            P("group", "slab"),
        ),
        out_specs=(P("group", "slab", None, None), P("group", "slab", None, None)),
        check_vma=False,
    )
```

profile of v0, /device:TPU:1, one launch (start us, length us, event | category | flops | bytes accessed | tf_op | source)
XLA Modules:
  0.0 145.7 jit_solution(4196204752132657275)
XLA Ops:
  0.6 1.6 %fusion.63 = (f32[2,1,32,256]{3,2,1,0:T(8,128)}, f32[2,1,32,256]{3,2,1,0:T(8,128)}) fusion(f32[2,8,32,256]{3,2,1,0:T(8,128)} %param.9), kind=kLoop, calls=%fused_computation.103 | loop fusion | bytes 262144 | tf_op jit(solution)/shard_map/slice | solution.py:13
  2.2 1.3 collective-permute-start
  3.5 4.6 %collective-permute-start.1 = (f32[2,1,32,256]{3,2,1,0:T(8,128)}, f32[2,1,32,256]{3,2,1,0:T(8,128)S(1)}, u32[]{:S(2)}, u32[]{:S(2)}) collective-permute-start(f32[2,1,32,256]{3,2,1,0:T(8,128)} %get-tuple-element.116), channel_id=1, source_target_pairs={{0,1},{1,2},{2,3},{3,4},{4,5},{5,6},{6,7},{7,8},{8,9},{9,10},{10,1... | collective-permute-start | bytes 196616 | tf_op jit(solution)/shard_map/ppermute | solution.py:17
  10.3 3.1 %fusion.22 = f32[2,8,32,256]{3,2,1,0:T(8,128)S(1)} fusion(f32[2,8,32,256]{3,2,1,0:T(8,128)} %param.9, f32[2,8,32,256]{3,2,1,0:T(8,128)S(1)} %copy.152, f32[2,1,32,256]{3,2,1,0:T(8,128)S(1)} %collective-permute-done.1, f32[2,1,32,256]{3,2,1,0:T(8,128)S(1)} %collective-permute-done, f32[8,32,256]{2,1,0:T(8,128)} %param.11), kind=kLoop, calls=%fused_computation.42 | loop fusion | flops 2359296 | bytes 1966080 | tf_op jit(solution)/shard_map/add | solution.py:74
  13.4 1.3 collective-permute-start.2
  14.7 4.0 %collective-permute-start.3 = (f32[2,1,32,256]{3,2,1,0:T(8,128)S(1)}, f32[2,1,32,256]{3,2,1,0:T(8,128)S(1)}, u32[]{:S(2)}, u32[]{:S(2)}) collective-permute-start(f32[2,1,32,256]{3,2,1,0:T(8,128)S(1)} %get-tuple-element.114), channel_id=1, source_target_pairs={{0,1},{1,2},{2,3},{3,4},{4,5},{5,6},{6,7},{7,8},{8,9},{9,10},{10,1... | collective-permute-start | bytes 196616 | tf_op jit(solution)/shard_map/ppermute | solution.py:17
  18.7 1.3 collective-permute-done.3
  20.4 4.6 %copy.154 = f32[2,8,32,256]{1,3,2,0:T(8,128)} copy(f32[2,8,32,256]{3,2,1,0:T(8,128)S(1)} %fusion.32) | data formatting | bytes 1048576 | tf_op jit(solution)/shard_map/add | solution.py:74
  25.0 6.2 %reduce_sum.54 = f32[2,8,8,64]{1,3,2,0:T(8,128)S(1)} reduce(f32[2,8,8,4,64,4]{1,5,4,3,2,0:T(4,128)} %bitcast.69, f32[]{:T(128)} %constant.79.clone.1), dimensions={3,5}, to_apply=%region_0.1 | reduce | flops 122880 | bytes 557060 | tf_op jit(solution)/shard_map/reduce_sum | solution.py:91
  31.4 16.0 %while.12 = (s32[]{:T(128)}, f32[8,2,2048]{2,1,0:T(2,128)S(1)}, s32[8,6,2048]{2,1,0:T(8,128)}, f32[128,64]{1,0:T(8,128)S(1)}, s32[]{:T(128)}, /*index=5*/s32[]{:...) while((s32[]{:T(128)}, f32[8,2,2048]{2,1,0:T(2,128)S(1)}, ...), condition=%wide.region_3.4_spmd.clone.clone, body=%wide.region_1.3_spmd.clone.clone.sunk | while | flops 202647568 | bytes 1556753 | solution.py:118
  35.4 1.2 multiply_convert_fusion.2
  39.4 1.2 multiply_convert_fusion.2
  41.4 1.2 multiply_convert_fusion.2
  43.4 1.2 multiply_convert_fusion.2
  45.4 1.2 multiply_convert_fusion.2
  48.3 19.2 %all-to-all-start = ((f32[32,2,512]{2,1,0:T(2,128)}), f32[32,2,512]{2,1,0:T(2,128)S(1)}, u32[]{:S(2)}, u32[]{:S(2)}) async-start(f32[32,2,512]{2,1,0:T(2,128)} %copy.157), calls=%async_computation | async-start | bytes 262144 | tf_op jit(solution)/shard_map/all_to_all | solution.py:34
  68.2 8.6 %all-to-all-done = f32[32,2,512]{2,1,0:T(2,128)S(1)} async-done(((f32[32,2,512]{2,1,0:T(2,128)}), f32[32,2,512]{2,1,0:T(2,128)S(1)}, u32[]{:S(2)}, u32[]{:S(2)}) %all-to-all-start) | async-done | bytes 131104 | tf_op jit(solution)/shard_map/all_to_all | solution.py:34
  76.8 11.4 %all-to-all-start.2 = ((f32[2,16,512]{2,0,1:T(2,128)}), f32[2,16,512]{2,0,1:T(2,128)S(1)}, u32[]{:S(2)}, u32[]{:S(2)}) async-start(f32[2,16,512]{2,0,1:T(2,128)} %copy.161), calls=%async_computation.2 | async-start | bytes 131072 | tf_op jit(solution)/shard_map/all_to_all | solution.py:135
  88.2 17.5 %all-gather = f32[16,2,1024]{2,1,0:T(2,128)S(1)} all-gather(f32[1,2,1024]{2,1,0:T(2,128)S(1)} %maximum_bitcast_fusion), channel_id=1, replica_groups=mesh['group'=16,'slab'=32] {'group'}, dimensions={0}, use_global_device_ids=true | all-gather | bytes 139264 | tf_op jit(solution)/shard_map/all_gather | solution.py:40
  107.3 3.9 %all-to-all-start.1 = ((f32[32,1,2048]{2,1,0:T(1,128)}), f32[32,1,2048]{2,1,0:T(1,128)S(1)}, u32[]{:S(2)}, u32[]{:S(2)}) async-start(f32[32,1,2048]{2,1,0:T(1,128)} %broadcast_in_dim.29), calls=%async_computation.1 | async-start | bytes 524288 | tf_op jit(solution)/shard_map/all_to_all | solution.py:49
  111.3 12.0 %all-to-all-done.1 = f32[32,1,2048]{2,1,0:T(1,128)S(1)} async-done(((f32[32,1,2048]{2,1,0:T(1,128)}), f32[32,1,2048]{2,1,0:T(1,128)S(1)}, u32[]{:S(2)}, u32[]{:S(2)}) %all-to-all-start.1) | async-done | bytes 262176 | tf_op jit(solution)/shard_map/all_to_all | solution.py:49
  123.6 2.9 %cholesky.14 = f32[32,32]{1,0:T(8,128)S(1)} custom-call(f32[32,32]{1,0:T(8,128)S(1)} %fusion.57), custom_call_target="Cholesky" | custom-call | tf_op jit(solution)/shard_map/jit(cholesky)/cholesky | solution.py:131
  127.9 2.4 %custom-call.10 = f32[1,32,32]{1,2,0:T(8,128)S(1)} custom-call(f32[1,32,32]{2,1,0:T(8,128)S(1)} %fusion.52), custom_call_target="InvertDiagBlocksLowerTriangular" | custom-call | tf_op jit(solution)/shard_map/jit(_cho_solve)/triangular_solve | solution.py:132
  131.1 14.0 %all_to_all.43 = f32[16,2,512]{2,1,0:T(2,128)S(1)} all-to-all(f32[16,2,512]{2,1,0:T(2,128)S(1)} %copy.163), channel_id=1, replica_groups=mesh['group'=16,'slab'=32] {'group'}, dimensions={0} | all-to-all | bytes 131072 | tf_op jit(solution)/shard_map/all_to_all | solution.py:137
  (107 shorter events, 18.9 us)
Async XLA Ops:
  0.6 19.4 %copy-start.1 = (f32[8,32,256]{2,1,0:T(8,128)S(1)}, f32[8,32,256]{2,1,0:T(8,128)}, u32[]{:S(2)}) copy-start(f32[8,32,256]{2,1,0:T(8,128)} %param.11) | copy-start | bytes 786436
  2.2 8.0 %collective-permute-start = (f32[2,1,32,256]{3,2,1,0:T(8,128)}, f32[2,1,32,256]{3,2,1,0:T(8,128)S(1)}, u32[]{:S(2)}, u32[]{:S(2)}) collective-permute-start(f32[2,1,32,256]{3,2,1,0:T(8,128)} %get-tuple-element.115), channel_id=1, source_target_pairs={{1,0},{2,1},{3,2},{4,3},{5,4},{6,5},{7,6},{8,7},{9,8},{10,9},{11,1... | collective-permute-start | bytes 196616 | tf_op jit(solution)/shard_map/ppermute | solution.py:19
  3.5 6.8 %collective-permute-start.1 = (f32[2,1,32,256]{3,2,1,0:T(8,128)}, f32[2,1,32,256]{3,2,1,0:T(8,128)S(1)}, u32[]{:S(2)}, u32[]{:S(2)}) collective-permute-start(f32[2,1,32,256]{3,2,1,0:T(8,128)} %get-tuple-element.116), channel_id=1, source_target_pairs={{0,1},{1,2},{2,3},{3,4},{4,5},{5,6},{6,7},{7,8},{8,9},{9,10},{10,1... | collective-permute-start | bytes 196616 | tf_op jit(solution)/shard_map/ppermute | solution.py:17
  13.4 5.3 %collective-permute-start.2 = (f32[2,1,32,256]{3,2,1,0:T(8,128)S(1)}, f32[2,1,32,256]{3,2,1,0:T(8,128)S(1)}, u32[]{:S(2)}, u32[]{:S(2)}) collective-permute-start(f32[2,1,32,256]{3,2,1,0:T(8,128)S(1)} %get-tuple-element.113), channel_id=1, source_target_pairs={{1,0},{2,1},{3,2},{4,3},{5,4},{6,5},{7,6},{8,7},{9,8},{10,9},{11,1... | collective-permute-start | bytes 196616 | tf_op jit(solution)/shard_map/ppermute | solution.py:19
  14.7 5.3 %collective-permute-start.3 = (f32[2,1,32,256]{3,2,1,0:T(8,128)S(1)}, f32[2,1,32,256]{3,2,1,0:T(8,128)S(1)}, u32[]{:S(2)}, u32[]{:S(2)}) collective-permute-start(f32[2,1,32,256]{3,2,1,0:T(8,128)S(1)} %get-tuple-element.114), channel_id=1, source_target_pairs={{0,1},{1,2},{2,3},{3,4},{4,5},{5,6},{6,7},{7,8},{8,9},{9,10},{10,1... | collective-permute-start | bytes 196616 | tf_op jit(solution)/shard_map/ppermute | solution.py:17
  20.4 10.8 %copy-start = (f32[2,8,32,256]{3,2,1,0:T(8,128)}, f32[2,8,32,256]{3,2,1,0:T(8,128)S(1)}, u32[]{:S(2)}) copy-start(f32[2,8,32,256]{3,2,1,0:T(8,128)S(1)} %fusion.32) | copy-start | bytes 1572868
  25.0 42.4 %copy-start.2 = (f32[2,4,16,128]{3,2,1,0:T(8,128)S(1)}, f32[2,4,16,128]{3,2,1,0:T(8,128)}, u32[]{:S(2)}) copy-start(f32[2,4,16,128]{3,2,1,0:T(8,128)} %param.10) | copy-start | bytes 196612
  25.0 42.4 %copy-start.4 = (f32[512]{0:T(512)S(1)}, f32[512]{0:T(512)}, u32[]{:S(2)}) copy-start(f32[512]{0:T(512)} %param.14) | copy-start | bytes 6148
  25.0 63.2 %copy-start.3 = (f32[2,512]{1,0:T(2,128)S(1)}, f32[2,512]{1,0:T(2,128)}, u32[]{:S(2)}) copy-start(f32[2,512]{1,0:T(2,128)} %param.15) | copy-start | bytes 12292
  25.0 80.9 %copy-start.5 = (f32[512]{0:T(512)S(1)}, f32[512]{0:T(512)}, u32[]{:S(2)}) copy-start(f32[512]{0:T(512)} %param.13) | copy-start | bytes 6148
  48.3 28.5 %all-to-all-start = ((f32[32,2,512]{2,1,0:T(2,128)}), f32[32,2,512]{2,1,0:T(2,128)S(1)}, u32[]{:S(2)}, u32[]{:S(2)}) async-start(f32[32,2,512]{2,1,0:T(2,128)} %copy.157), calls=%async_computation | async-start | bytes 262144 | tf_op jit(solution)/shard_map/all_to_all | solution.py:34
  76.8 29.7 %all-to-all-start.2 = ((f32[2,16,512]{2,0,1:T(2,128)}), f32[2,16,512]{2,0,1:T(2,128)S(1)}, u32[]{:S(2)}, u32[]{:S(2)}) async-start(f32[2,16,512]{2,0,1:T(2,128)} %copy.161), calls=%async_computation.2 | async-start | bytes 131072 | tf_op jit(solution)/shard_map/all_to_all | solution.py:135
  107.3 15.9 %all-to-all-start.1 = ((f32[32,1,2048]{2,1,0:T(1,128)}), f32[32,1,2048]{2,1,0:T(1,128)S(1)}, u32[]{:S(2)}, u32[]{:S(2)}) async-start(f32[32,1,2048]{2,1,0:T(1,128)} %broadcast_in_dim.29), calls=%async_computation.1 | async-start | bytes 524288 | tf_op jit(solution)/shard_map/all_to_all | solution.py:49
where the time goes:
time: 147 us; the launch traced here: 146 us
  starting transfers between devices  45.5 us (31%)
  blocking collectives  31.5 us (21%)
  other arithmetic  27.8 us (19%)
  waiting for transfers between devices  21.9 us (15%)
  local copies, waits for them, and re-layouts  11.5 us (8%)
  matrix products  6.19 us (4%)
    all_to_all x1, starting transfers between devices, sum_at_owner(): lax.all_to_all(parts, axis, split_axis=0, concat_axis=0, tiled=True)  19.2 us
    all_gather x1, blocking collectives, sent_together(): filled, at, outs = (lax.all_gather(both, axis, axis=dim, tiled=True), 0, [])  17.5 us
    all_to_all x1, blocking collectives, local(): lax.all_to_all(blended, 'group', split_axis=0, concat_axis=1, tiled=True)  14 us
    all_to_all x1, waiting for transfers between devices, sent_to_all(): return lax.all_to_all(copies, axis, split_axis=0, concat_axis=0, tiled=True)  12 us
    all_to_all x1, starting transfers between devices, local(): lax.all_to_all(flat_theta, 'group', split_axis=1, concat_axis=0, tiled=True)  11.4 us
    convert_element_type x8, other arithmetic, observe(): ((block[1] - block[0]) * (block[3] - block[2]) * (block[5] - block[4]) *...  9.21 us
    all_to_all x1, waiting for transfers between devices, sum_at_owner(): lax.all_to_all(parts, axis, split_axis=0, concat_axis=0, tiled=True)  8.61 us
    ppermute x2, starting transfers between devices, extended(): lax.ppermute(tail, axis, [(i, (i + 1) % count) for i in range(ends)])  8.55 us
  transfers between devices with their start and end apart: 7, of which 3 were waited for; matrix products, arithmetic and copies ran while one was open for 2% of the time, Pallas kernels for 0%

commit v1 on v0

v1 whole, which is shorter than its diff:
```python
import functools

import jax
import jax.numpy as jnp
from jax import lax
from jax.experimental import pallas as pl
from jax.experimental.pallas import tpu as pltpu
from jax.sharding import PartitionSpec as P

STEP_SIZE = 0.1
F32 = jnp.float32
BF16 = jnp.bfloat16

LOCAL = 2
PLANES = 8
ROWS = 32
COLS = 256
COARSE = 4
SLABS = 32
GROUPS = 16
MEMBERS = 32
BLOCK = 512
HALO_ROWS = 176


def split3(value):
    a = value.astype(BF16)
    rest = value - a.astype(F32)
    b = rest.astype(BF16)
    c = (rest - b.astype(F32)).astype(BF16)
    return a, b, c


def pack_kernel(state, theta, forcing, first, last, sems):
    copies = []

    def copy(src, dst):
        copies.append(pltpu.make_async_copy(src, dst, sems.at[len(copies)]))

    for out, plane, coarse, force in ((first, 0, 0, 0), (last, PLANES - 2, COARSE - 1, PLANES - 1)):
        for m in range(LOCAL):
            for p in range(2):
                at = (m * 2 + p) * ROWS
                copy(state.at[m, plane + p], out.at[pl.ds(at, ROWS), :])
            copy(theta.at[m, coarse], out.at[pl.ds(160, 16), pl.ds(m * 128, 128)])
        copy(forcing.at[force], out.at[pl.ds(128, ROWS), :])
    for c in copies:
        c.start()
    for c in copies:
        c.wait()


def pack(state, theta, forcing):
    shape = jax.ShapeDtypeStruct((HALO_ROWS, COLS), F32)
    anywhere = pl.BlockSpec(memory_space=pl.ANY)
    return pl.pallas_call(
        pack_kernel,
        out_shape=(shape, shape),
        in_specs=[anywhere] * 3,
        out_specs=(anywhere, anywhere),
        scratch_shapes=[pltpu.SemaphoreType.DMA((14,))],
        name="pack",
    )(state, theta, forcing)


def window_kernel(slab, state, theta, forcing, low, high, boxes, final, part, count, diff, mid, done):
    s = slab[0]
    keep_low = jnp.where(s > 0, 0.5, 0.0).astype(F32)
    keep_high = jnp.where(s < SLABS - 1, 0.5, 0.0).astype(F32)
    pieces = []
    for m in range(LOCAL):
        pieces.append(keep_low * jnp.exp(low[160:176, m * 128 : (m + 1) * 128]))
        for c in range(COARSE):
            pieces.append(0.5 * jnp.exp(theta[m, c]))
        pieces.append(keep_high * jnp.exp(high[160:176, m * 128 : (m + 1) * 128]))
    coarse = jnp.concatenate(pieces, axis=0)
    up = (
        lax.broadcasted_iota(jnp.int32, (128, COLS), 1) // 2
        == lax.broadcasted_iota(jnp.int32, (128, COLS), 0)
    ).astype(F32).astype(BF16)
    wide = sum(jnp.dot(part_, up, preferred_element_type=F32) for part_ in split3(coarse))
    rows = LOCAL * (COARSE + 2) * 16
    for h in range(2):
        diff[h, pl.ds(0, rows, stride=2), :] = wide[:, h * 128 : (h + 1) * 128]
        diff[h, pl.ds(1, rows, stride=2), :] = wide[:, h * 128 : (h + 1) * 128]

    row = lax.broadcasted_iota(jnp.int32, (ROWS, COLS), 0)
    col = lax.broadcasted_iota(jnp.int32, (ROWS, COLS), 1)

    def step(below, center, above, d, f):
        beside = above + below
        beside = beside + jnp.where(row == ROWS - 1, 0.0, pltpu.roll(center, ROWS - 1, 0))
        beside = beside + jnp.where(row == 0, 0.0, pltpu.roll(center, 1, 0))
        beside = beside + jnp.where(col == COLS - 1, 0.0, pltpu.roll(center, COLS - 1, 1))
        beside = beside + jnp.where(col == 0, 0.0, pltpu.roll(center, 1, 1))
        change = d * (beside - 6.0 * center) + 0.5 * center * (1.0 - center * center) + f
        return center + STEP_SIZE * change

    def plane(m, p):
        if p < 0:
            at = (m * 2 + p + 2) * ROWS
            return low[at : at + ROWS, :]
        if p >= PLANES:
            at = (m * 2 + p - PLANES) * ROWS
            return high[at : at + ROWS, :]
        return state[m, p]

    def force(p):
        if p < 0:
            return low[128:160, :]
        if p >= PLANES:
            return high[128:160, :]
        return forcing[p]

    def diffusivity(m, p):
        at = (m * (COARSE + 2) + (p + 2) // 2) * ROWS
        return jnp.concatenate([diff[h, at : at + ROWS, :] for h in range(2)], axis=1)

    for m in range(LOCAL):
        for p in range(-1, PLANES + 1):
            mid[m * (PLANES + 2) + p + 1] = step(
                plane(m, p - 1), plane(m, p), plane(m, p + 1), diffusivity(m, p), force(p)
            )
        for p in range(PLANES):
            at = m * (PLANES + 2) + p
            new = step(mid[at], mid[at + 1], mid[at + 2], diffusivity(m, p), forcing[p])
            final[m, p] = new
            to = (m * PLANES + p) * ROWS
            for h in range(2):
                done[h, to : to + ROWS, :] = new[:, h * 128 : (h + 1) * 128]

    tall = LOCAL * PLANES * 8
    sums = jnp.concatenate(
        [sum(done[h, pl.ds(q, tall, stride=4), :] for q in range(4)) for h in range(2)], axis=1
    )
    fold = (
        lax.broadcasted_iota(jnp.int32, (COLS, 128), 0) // 4
        == lax.broadcasted_iota(jnp.int32, (COLS, 128), 1) % 64
    ).astype(F32).astype(BF16)
    tiles = sum(jnp.dot(part_, fold, preferred_element_type=F32) for part_ in split3(sums))
    top = tiles.astype(BF16).astype(F32)
    lane = lax.broadcasted_iota(jnp.int32, (tall, 128), 1)
    left = jnp.where(lane < 64, top, tiles - top).astype(BF16)

    iota_x = lax.broadcasted_iota(jnp.int32, (64, BLOCK), 0)
    iota_y = lax.broadcasted_iota(jnp.int32, (8, BLOCK), 0)

    def observe(d, carry):
        here = pl.ds(pl.multiple_of(d * BLOCK, BLOCK), BLOCK)
        b = boxes[:, here]
        in_x = ((iota_x >= b[4:5]) & (iota_x < b[5:6])).astype(F32).astype(BF16)
        along = jnp.dot(left, jnp.concatenate([in_x, in_x], axis=0), preferred_element_type=F32)
        z0 = jnp.broadcast_to(b[0:1], (8, BLOCK)) - s * PLANES
        z1 = jnp.broadcast_to(b[1:2], (8, BLOCK)) - s * PLANES
        in_y = (iota_y >= b[2:3]) & (iota_y < b[3:4])
        sums = [jnp.zeros((8, BLOCK), F32) for m in range(LOCAL)]
        for z in range(PLANES):
            in_z = (z0 <= z) & (z1 > z)
            for m in range(LOCAL):
                at = (m * PLANES + z) * 8
                sums[m] = sums[m] + jnp.where(in_z, along[at : at + 8], 0.0)
        for m in range(LOCAL):
            total = jnp.sum(jnp.where(in_y, sums[m], 0.0), axis=0, keepdims=True)
            for q in range(4):
                part[d, m * 4 + q : m * 4 + q + 1, :] = total[:, q * 128 : (q + 1) * 128]
        return carry

    lax.fori_loop(0, SLABS, observe, 0)

    b = boxes[:, pl.ds(pl.multiple_of(s * BLOCK, BLOCK), BLOCK)]
    cells = ((b[1:2] - b[0:1]) * (b[3:4] - b[2:3]) * (b[5:6] - b[4:5]) * 16).astype(F32)
    for m in range(LOCAL):
        for q in range(4):
            count[m * 4 + q : m * 4 + q + 1, :] = cells[:, q * 128 : (q + 1) * 128]


def window(slab, state, theta, forcing, low, high, boxes):
    vmem = pl.BlockSpec(memory_space=pltpu.VMEM)
    return pl.pallas_call(
        window_kernel,
        out_shape=(
            jax.ShapeDtypeStruct(state.shape, F32),
            jax.ShapeDtypeStruct((SLABS, 8, 128), F32),
            jax.ShapeDtypeStruct((8, 128), F32),
        ),
        in_specs=[pl.BlockSpec(memory_space=pltpu.SMEM)] + [vmem] * 6,
        out_specs=(vmem, vmem, vmem),
        scratch_shapes=[
            pltpu.VMEM((2, LOCAL * (COARSE + 2) * ROWS, 128), F32),
            pltpu.VMEM((LOCAL * (PLANES + 2), ROWS, COLS), F32),
            pltpu.VMEM((2, LOCAL * PLANES * ROWS, 128), F32),
        ],
        name="window",
    )(slab, state, theta, forcing, low, high, boxes)


def gather_kernel(arrived, count, copies, own):
    pred = jnp.sum(arrived[...], axis=0) / count[...]
    own[...] = pred
    for g in range(GROUPS):
        copies[g] = pred


def own_predictions(arrived, count):
    return pl.pallas_call(
        gather_kernel,
        out_shape=(
            jax.ShapeDtypeStruct((GROUPS, 8, 128), F32),
            jax.ShapeDtypeStruct((8, 128), F32),
        ),
        name="own_predictions",
    )(arrived, count)


def moments_kernel(preds, own, observed, noise, perturb, out):
    scale = 1.0 / (float(MEMBERS - 1) ** 0.5)
    everyone = jnp.concatenate(
        [preds[pl.ds(q, MEMBERS, stride=4), :] for q in range(4)], axis=1
    )
    mine = jnp.concatenate([own[pl.ds(q, LOCAL, stride=4), :] for q in range(4)], axis=1)
    anomaly = (everyone - jnp.mean(everyone, axis=0, keepdims=True)) * scale
    var = noise[...]
    misfit = observed[...] + jnp.sqrt(var) * perturb[...] - mine
    weighted = anomaly / var
    left = jnp.concatenate([anomaly, misfit, jnp.zeros((6, BLOCK), F32)], axis=0)
    right = jnp.concatenate(
        [
            weighted,
            weighted[8:],
            weighted[16:],
            weighted[24:],
            weighted,
            jnp.zeros((16, BLOCK), F32),
        ],
        axis=0,
    )
    product = lax.dot_general(
        left, right, (((1,), (1,)), ((), ())), precision=lax.Precision.HIGHEST,
        preferred_element_type=F32,
    )
    lane = lax.broadcasted_iota(jnp.int32, (8, 128), 1)
    packed = product[0:8]
    for start, at in ((32, 8), (56, 16), (72, 24), (80, 32)):
        packed = jnp.where(lane >= start, product[at : at + 8], packed)
    for d in range(SLABS):
        out[d] = packed


def moments(preds, own, observed, noise, perturb):
    return pl.pallas_call(
        moments_kernel,
        out_shape=jax.ShapeDtypeStruct((SLABS, 8, 128), F32),
        name="moments",
    )(preds, own, observed, noise, perturb)


def update_kernel(group, arrived, theta, out):
    packed = jnp.sum(arrived[...], axis=0)
    lane8 = lax.broadcasted_iota(jnp.int32, (8, 128), 1)
    blocks = []
    for c, start in enumerate((0, 32, 56, 72)):
        moved = pltpu.roll(packed, (8 * c - start) % 128, 1)
        blocks.append(jnp.where((lane8 >= 8 * c) & (lane8 < 32), moved, 0.0))
    upper = jnp.concatenate(blocks + [jnp.zeros((96, 128), F32)], axis=0)
    mirrored = upper.T[0:MEMBERS]
    upper = upper[0:MEMBERS]
    row = lax.broadcasted_iota(jnp.int32, (MEMBERS, 128), 0)
    lane = lax.broadcasted_iota(jnp.int32, (MEMBERS, 128), 1)
    matrix = jnp.where(lane // 8 >= row // 8, upper, mirrored)
    matrix = jnp.where(row == lane, matrix + 1.0, matrix)
    cross_rows = jnp.where(lane8 < MEMBERS, pltpu.roll(packed, 128 - 80, 1), 0.0)
    cross = jnp.concatenate([cross_rows, jnp.zeros((120, 128), F32)], axis=0).T[0:MEMBERS]
    cross = pltpu.roll(cross, MEMBERS, 1)
    work = jnp.where((lane >= MEMBERS) & (lane < MEMBERS + LOCAL), cross, matrix)
    for k in range(MEMBERS):
        column = jnp.broadcast_to(work[:, k : k + 1], (MEMBERS, 128))
        pivot = column[k : k + 1, :]
        line = work[k : k + 1, :] / pivot
        work = jnp.where(row == k, line, work - column * line)
    gain = work
    mixing = (gain - jnp.mean(gain, axis=0, keepdims=True)) * (1.0 / float(MEMBERS - 1) ** 0.5)
    first = group[0] * LOCAL
    mixing = jnp.where(row - first == lane - MEMBERS, mixing + 1.0, mixing)
    columns = [
        jnp.broadcast_to(mixing[:, MEMBERS + j : MEMBERS + j + 1], (MEMBERS, 128))
        for j in range(LOCAL)
    ]
    totals = [jnp.zeros((64, 128), F32) for j in range(LOCAL)]
    for k in range(MEMBERS):
        field = theta[k]
        for j in range(LOCAL):
            totals[j] = totals[j] + columns[j][k : k + 1, :] * field
    for j in range(LOCAL):
        out[j] = totals[j]


def update(group, arrived, theta):
    vmem = pl.BlockSpec(memory_space=pltpu.VMEM)
    return pl.pallas_call(
        update_kernel,
        out_shape=jax.ShapeDtypeStruct((LOCAL, 64, 128), F32),
        in_specs=[pl.BlockSpec(memory_space=pltpu.SMEM), vmem, vmem],
        out_specs=vmem,
        name="update",
    )(group, arrived, theta)


def local(state, theta, forcing, boxes, observed, noise_var, perturb):
    slab = lax.axis_index("slab").astype(jnp.int32).reshape(1)
    group = lax.axis_index("group").astype(jnp.int32).reshape(1)
    first, last = pack(state, theta, forcing)
    low = lax.ppermute(last, "slab", [(i, i + 1) for i in range(SLABS - 1)])
    high = lax.ppermute(first, "slab", [(i + 1, i) for i in range(SLABS - 1)])
    field = theta.reshape(1, LOCAL, 64, 128)
    fields = lax.all_to_all(
        jnp.broadcast_to(field, (GROUPS, LOCAL, 64, 128)), "group", 0, 0, tiled=True
    ).reshape(MEMBERS, 64, 128)
    final, part, count = window(slab, state, theta, forcing, low, high, boxes)
    arrived = lax.all_to_all(part, "slab", 0, 0, tiled=True)
    copies, own = own_predictions(arrived, count)
    preds = lax.all_to_all(copies, "group", 0, 0, tiled=True).reshape(GROUPS * 8, 128)
    sums = moments(preds, own, observed.reshape(1, BLOCK), noise_var.reshape(1, BLOCK), perturb)
    sums = lax.all_to_all(sums, "slab", 0, 0, tiled=True)
    updated = update(group, sums, fields)
    return final, updated.reshape(theta.shape)


def solution(mesh):
    return jax.shard_map(
        local,
        mesh=mesh,
        in_specs=(
            P("group", "slab", None, None),
            P("group", "slab", None, None),
            P("slab", None, None),
            P(),
            P("slab"),
            P("slab"),
            P("group", "slab"),
        ),
        out_specs=(P("group", "slab", None, None), P("group", "slab", None, None)),
        check_vma=False,
    )
```

time: 147 us -> 136 us (0.925)
  starting transfers between devices: 45.5 us -> 10.3 us
  Pallas kernels: 0 us -> 30.6 us
  other arithmetic: 27.8 us -> 0 us
  blocking collectives: 31.5 us -> 58 us
  waiting for transfers between devices: 21.9 us -> 33.2 us
  local copies, waits for them, and re-layouts: 11.5 us -> 2.73 us
  matrix products: 6.19 us -> 0 us
    all_to_all x1 -> x3, blocking collectives: 14 us -> 58 us  [the longest x1 25.1 us: local(): arrived = lax.all_to_all(part, 'slab', 0, 0, tiled=True)]
    pallas_call x0 -> x5, Pallas kernels: none -> 30.6 us  [the longest x1 12.1 us: pack(): pl.pallas_call(pack_kernel, out_shape=(shape, shape), in_specs=[anywhere]...]
    all_to_all x3 -> x1, starting transfers between devices: 34.4 us -> 5.08 us  [local(): lax.all_to_all(jnp.broadcast_to(field, (GROUPS, LOCAL, 64, 128)), 'group'...]
    all_gather x1 -> x0, blocking collectives: 17.5 us -> none  [sent_together(): filled, at, outs = (lax.all_gather(both, axis, axis=dim, tiled=True), 0, [])]
    convert_element_type x16 -> x0, other arithmetic: 9.87 us -> none  [the longest x8 9.21 us: observe(): ((block[1] - block[0]) * (block[3] - block[2]) * (block[5] - block[4]) *...]
    all_to_all x3 -> x1, waiting for transfers between devices: 20.6 us -> 28 us  [local(): lax.all_to_all(jnp.broadcast_to(field, (GROUPS, LOCAL, 64, 128)), 'group'...]
    another operation x5 -> x0, other arithmetic: 6.68 us -> none  [the longest x3 3.59 us: local(): factor = jnp.linalg.cholesky(identity + inner)]
    reduce_sum x4 -> x0, other arithmetic: 6.43 us -> none  [the longest x1 6.18 us: local(): current.reshape(mem_local, planes, tiles_y, 4, tiles_x, 4).sum(axis=(3, 5))]
  transfers between devices with their start and end apart: 7 -> 3, of which waited for: 3 -> 3; matrix products, arithmetic and copies ran while one was open for 2% -> 0% of each run, Pallas kernels for 0% -> 0%
where the time goes in v1:
time: 136 us
  blocking collectives  58 us (43%)
  waiting for transfers between devices  33.2 us (24%)
  Pallas kernels  30.6 us (22%)
  starting transfers between devices  10.3 us (8%)
  local copies, waits for them, and re-layouts  2.73 us (2%)
    all_to_all x1, waiting for transfers between devices, local(): lax.all_to_all(jnp.broadcast_to(field, (GROUPS, LOCAL, 64, 128)), 'group'...  28 us
    all_to_all x1, blocking collectives, local(): arrived = lax.all_to_all(part, 'slab', 0, 0, tiled=True)  25.1 us
    all_to_all x1, blocking collectives, local(): lax.all_to_all(copies, 'group', 0, 0, tiled=True).reshape(GROUPS * 8, 128)  18.3 us
    all_to_all x1, blocking collectives, local(): sums = lax.all_to_all(sums, 'slab', 0, 0, tiled=True)  14.5 us
    pallas_call x1, Pallas kernels, pack(): pl.pallas_call(pack_kernel, out_shape=(shape, shape), in_specs=[anywhere]...  12.1 us
    pallas_call x1, Pallas kernels, window(): pl.pallas_call(window_kernel, out_shape=(jax.ShapeDtypeStruct(state.shape...  9.92 us
    pallas_call x1, Pallas kernels, update(): pl.pallas_call(update_kernel, out_shape=jax.ShapeDtypeStruct((LOCAL, 64,...  5.11 us
    all_to_all x1, starting transfers between devices, local(): lax.all_to_all(jnp.broadcast_to(field, (GROUPS, LOCAL, 64, 128)), 'group'...  5.08 us
  transfers between devices with their start and end apart: 3, of which 3 were waited for; matrix products, arithmetic and copies ran while one was open for 0% of the time, Pallas kernels for 0%

profile of v1, /device:TPU:1, one launch (start us, length us, event | category | flops | bytes accessed | tf_op | source)
XLA Modules:
  0.0 135.5 jit_solution(6477137530414663390)
XLA Ops:
  0.6 12.1 %pack.1 = (f32[176,256]{1,0:T(8,128)}, f32[176,256]{1,0:T(8,128)}) custom-call(f32[2,8,32,256]{3,2,1,0:T(8,128)} %state.3, f32[2,4,16,128]{3,2,1,0:T(8,128)} %theta.3, f32[8,32,256]{2,1,0:T(8,128)} %forcing.3), custom_call_target="tpu_custom_call" | custom-call | tf_op jit(solution)/shard_map/pack/pallas_call | solution.py:56
  12.8 3.9 %collective-permute-start = (f32[176,256]{1,0:T(8,128)}, f32[176,256]{1,0:T(8,128)S(1)}, u32[]{:S(2)}, u32[]{:S(2)}) collective-permute-start(f32[176,256]{1,0:T(8,128)} %get-tuple-element.9), channel_id=1, source_target_pairs={{0,1},{1,2},{2,3},{3,4},{4,5},{5,6},{6,7},{7,8},{8,9},{9,10},{10,1... | collective-permute-start | bytes 540680 | tf_op jit(solution)/shard_map/ppermute | solution.py:312
  16.7 1.3 collective-permute-start.1
  18.0 1.4 %collective-permute-done.low = f32[176,256]{1,0:T(8,128)S(1)} collective-permute-done((f32[176,256]{1,0:T(8,128)}, f32[176,256]{1,0:T(8,128)S(1)}, u32[]{:S(2)}, u32[]{:S(2)}) %collective-permute-start) | collective-permute-done | bytes 180256 | tf_op jit(solution)/shard_map/ppermute | solution.py:312
  19.5 0.0 copy-start.2
  19.5 3.7 %collective-permute-done.1.high = f32[176,256]{1,0:T(8,128)S(1)} collective-permute-done((f32[176,256]{1,0:T(8,128)}, f32[176,256]{1,0:T(8,128)S(1)}, u32[]{:S(2)}, u32[]{:S(2)}) %collective-permute-start.1) | collective-permute-done | bytes 180256 | tf_op jit(solution)/shard_map/ppermute | solution.py:313
  23.2 0.0 copy-start.3
  23.2 0.0 copy-done.2
  23.2 0.7 copy-done.3
  23.8 9.9 %window.1 = (f32[2,8,32,256]{3,2,1,0:T(8,128)}, f32[32,8,128]{2,1,0:T(8,128)}, f32[8,128]{1,0:T(8,128)}) custom-call(s32[1]{0:T(128)} %bitcast.slab, f32[2,8,32,256]{3,2,1,0:T(8,128)} %state.3, f32[2,4,16,128]{3,2,1,0:T(8,128)} %theta.3, f32[8,32,256]{2,1,0:T(8,128)} %forcing.3, f32[176,256]{1,0:T(8,128)} %copy-done.2, f32[176,256]{1,0:T(8,128)} %copy-done.3, ...), custom_call_target="tpu_custom_call" | custom-call | tf_op jit(solution)/shard_map/window/pallas_call | solution.py:179
  33.8 25.1 %all_to_all.20.arrived = f32[32,8,128]{2,1,0:T(8,128)} all-to-all(f32[32,8,128]{2,1,0:T(8,128)} %get-tuple-element.12), channel_id=1, replica_groups=mesh['group'=16,'slab'=32] {'slab'}, dimensions={0} | all-to-all | bytes 262144 | tf_op jit(solution)/shard_map/all_to_all | solution.py:319
  58.9 1.6 %own_predictions.1 = (f32[16,8,128]{2,1,0:T(8,128)}, f32[8,128]{1,0:T(8,128)}) custom-call(f32[32,8,128]{2,1,0:T(8,128)} %all_to_all.20.arrived, f32[8,128]{1,0:T(8,128)} %get-tuple-element.13.count), custom_call_target="tpu_custom_call" | custom-call | tf_op jit(solution)/shard_map/own_predictions/pallas_call | solution.py:205
  60.5 18.3 %all_to_all.21 = f32[16,8,128]{2,1,0:T(8,128)} all-to-all(f32[16,8,128]{2,1,0:T(8,128)} %get-tuple-element.14), channel_id=1, replica_groups=mesh['group'=16,'slab'=32] {'group'}, dimensions={0} | all-to-all | bytes 131072 | tf_op jit(solution)/shard_map/all_to_all | solution.py:321
  78.8 1.9 %moments.1 = f32[32,8,128]{2,1,0:T(8,128)} custom-call(f32[128,128]{1,0:T(8,128)} %bitcast.10, f32[8,128]{1,0:T(8,128)} %get-tuple-element.15.own, f32[1,512]{1,0:T(1,128)} %bitcast.12, f32[1,512]{1,0:T(1,128)} %bitcast.13, f32[2,512]{1,0:T(2,128)} %perturb.1), custom_call_target="tpu_custom_call" | custom-call | tf_op jit(solution)/shard_map/moments/pallas_call | solution.py:250
  80.7 0.0 copy-start.1
  80.7 14.5 %all_to_all.22.arrived = f32[32,8,128]{2,1,0:T(8,128)} all-to-all(f32[32,8,128]{2,1,0:T(8,128)} %moments.1), channel_id=1, replica_groups=mesh['group'=16,'slab'=32] {'slab'}, dimensions={0} | all-to-all | bytes 262144 | tf_op jit(solution)/shard_map/all_to_all | solution.py:323
  95.2 0.0 copy-done.1
  95.2 1.1 broadcast_in_dim.8
  96.3 5.1 %all-to-all-start.3 = ((f32[16,2,64,128]{3,2,1,0:T(8,128)}), f32[16,2,64,128]{3,2,1,0:T(8,128)S(1)}, u32[]{:S(2)}, u32[]{:S(2)}) async-start(f32[16,2,64,128]{3,2,1,0:T(8,128)} %broadcast_in_dim.8), calls=%async_computation.3 | async-start | bytes 2097152 | tf_op jit(solution)/shard_map/all_to_all | solution.py:315
  101.4 28.0 %all-to-all-done.3 = f32[16,2,64,128]{3,2,1,0:T(8,128)S(1)} async-done(((f32[16,2,64,128]{3,2,1,0:T(8,128)}), f32[16,2,64,128]{3,2,1,0:T(8,128)S(1)}, u32[]{:S(2)}, u32[]{:S(2)}) %all-to-all-start.3) | async-done | bytes 1048608 | tf_op jit(solution)/shard_map/all_to_all | solution.py:315
  129.4 0.0 copy-start
  129.4 1.0 copy-done
  130.4 5.1 %update.1 = f32[2,64,128]{2,1,0:T(8,128)} custom-call(s32[1]{0:T(128)} %bitcast.1.group, f32[32,8,128]{2,1,0:T(8,128)} %all_to_all.22.arrived, f32[32,64,128]{2,1,0:T(8,128)} %bitcast.8), custom_call_target="tpu_custom_call" | custom-call | tf_op jit(solution)/shard_map/update/pallas_call | solution.py:299
Async XLA Ops:
  12.8 6.7 %collective-permute-start = (f32[176,256]{1,0:T(8,128)}, f32[176,256]{1,0:T(8,128)S(1)}, u32[]{:S(2)}, u32[]{:S(2)}) collective-permute-start(f32[176,256]{1,0:T(8,128)} %get-tuple-element.9), channel_id=1, source_target_pairs={{0,1},{1,2},{2,3},{3,4},{4,5},{5,6},{6,7},{7,8},{8,9},{9,10},{10,1... | collective-permute-start | bytes 540680 | tf_op jit(solution)/shard_map/ppermute | solution.py:312
  16.7 6.4 %collective-permute-start.1 = (f32[176,256]{1,0:T(8,128)}, f32[176,256]{1,0:T(8,128)S(1)}, u32[]{:S(2)}, u32[]{:S(2)}) collective-permute-start(f32[176,256]{1,0:T(8,128)} %get-tuple-element.10), channel_id=1, source_target_pairs={{1,0},{2,1},{3,2},{4,3},{5,4},{6,5},{7,6},{8,7},{9,8},{10,9},{11,1... | collective-permute-start | bytes 540680 | tf_op jit(solution)/shard_map/ppermute | solution.py:313
  19.5 3.7 %copy-start.2 = (f32[176,256]{1,0:T(8,128)}, f32[176,256]{1,0:T(8,128)S(1)}, u32[]{:S(2)}) copy-start(f32[176,256]{1,0:T(8,128)S(1)} %collective-permute-done.low) | copy-start | bytes 540676
  23.2 0.7 copy-start.3
  80.7 14.5 %copy-start.1 = (f32[2,4,16,128]{3,2,1,0:T(8,128)S(1)}, f32[2,4,16,128]{3,2,1,0:T(8,128)}, u32[]{:S(2)}) copy-start(f32[2,4,16,128]{3,2,1,0:T(8,128)} %theta.3) | copy-start | bytes 196612
  96.3 33.1 %all-to-all-start.3 = ((f32[16,2,64,128]{3,2,1,0:T(8,128)}), f32[16,2,64,128]{3,2,1,0:T(8,128)S(1)}, u32[]{:S(2)}, u32[]{:S(2)}) async-start(f32[16,2,64,128]{3,2,1,0:T(8,128)} %broadcast_in_dim.8), calls=%async_computation.3 | async-start | bytes 2097152 | tf_op jit(solution)/shard_map/all_to_all | solution.py:315
  129.4 1.0 copy-start

commit v2 on v1

--- a/solution.py
+++ b/solution.py
@@ -1,11 +1,10 @@
-import functools
-
 import jax
 import jax.numpy as jnp
 from jax import lax
 from jax.experimental import pallas as pl
 from jax.experimental.pallas import tpu as pltpu
 from jax.sharding import PartitionSpec as P
+
 
 STEP_SIZE = 0.1
 F32 = jnp.float32
@@ -20,6 +19,7 @@
 GROUPS = 16
 MEMBERS = 32
 BLOCK = 512
+MIB = 1 << 20
 HALO_ROWS = 176
 
 
@@ -52,18 +52,19 @@
 
 def pack(state, theta, forcing):
     shape = jax.ShapeDtypeStruct((HALO_ROWS, COLS), F32)
-    anywhere = pl.BlockSpec(memory_space=pl.ANY)
+    vmem = pl.BlockSpec(memory_space=pltpu.VMEM)
     return pl.pallas_call(
         pack_kernel,
         out_shape=(shape, shape),
-        in_specs=[anywhere] * 3,
-        out_specs=(anywhere, anywhere),
+        in_specs=[pl.BlockSpec(memory_space=pltpu.HBM)] * 3,
+        out_specs=(vmem, vmem),
+        compiler_params=pltpu.CompilerParams(vmem_limit_bytes=2 * MIB),
         scratch_shapes=[pltpu.SemaphoreType.DMA((14,))],
         name="pack",
-    )(state, theta, forcing)
-
-
-def window_kernel(slab, state, theta, forcing, low, high, boxes, final, part, count, diff, mid, done):
+    )(*(pltpu.with_memory_space_constraint(a, pltpu.HBM) for a in (state, theta, forcing)))
+
+
+def window_kernel(slab, state, theta, forcing, low, high, boxes, final, part, count, diff, mid, fresh, done, sem):
     s = slab[0]
     keep_low = jnp.where(s > 0, 0.5, 0.0).astype(F32)
     keep_high = jnp.where(s < SLABS - 1, 0.5, 0.0).astype(F32)
@@ -124,10 +125,13 @@
         for p in range(PLANES):
             at = m * (PLANES + 2) + p
             new = step(mid[at], mid[at + 1], mid[at + 2], diffusivity(m, p), forcing[p])
-            final[m, p] = new
+            fresh[m, p] = new
             to = (m * PLANES + p) * ROWS
             for h in range(2):
                 done[h, to : to + ROWS, :] = new[:, h * 128 : (h + 1) * 128]
+
+    leave = pltpu.make_async_copy(fresh, final, sem)
+    leave.start()
 
     tall = LOCAL * PLANES * 8
     sums = jnp.concatenate(
@@ -153,7 +157,7 @@
         z0 = jnp.broadcast_to(b[0:1], (8, BLOCK)) - s * PLANES
         z1 = jnp.broadcast_to(b[1:2], (8, BLOCK)) - s * PLANES
         in_y = (iota_y >= b[2:3]) & (iota_y < b[3:4])
-        sums = [jnp.zeros((8, BLOCK), F32) for m in range(LOCAL)]
+        sums = [jnp.zeros((8, BLOCK), F32) for _ in range(LOCAL)]
         for z in range(PLANES):
             in_z = (z0 <= z) & (z1 > z)
             for m in range(LOCAL):
@@ -172,6 +176,7 @@
     for m in range(LOCAL):
         for q in range(4):
             count[m * 4 + q : m * 4 + q + 1, :] = cells[:, q * 128 : (q + 1) * 128]
+    leave.wait()
 
 
 def window(slab, state, theta, forcing, low, high, boxes):
@@ -184,11 +189,14 @@
             jax.ShapeDtypeStruct((8, 128), F32),
         ),
         in_specs=[pl.BlockSpec(memory_space=pltpu.SMEM)] + [vmem] * 6,
-        out_specs=(vmem, vmem, vmem),
+        out_specs=(pl.BlockSpec(memory_space=pltpu.HBM), vmem, vmem),
+        compiler_params=pltpu.CompilerParams(vmem_limit_bytes=12 * MIB),
         scratch_shapes=[
             pltpu.VMEM((2, LOCAL * (COARSE + 2) * ROWS, 128), F32),
             pltpu.VMEM((LOCAL * (PLANES + 2), ROWS, COLS), F32),
+            pltpu.VMEM((LOCAL, PLANES, ROWS, COLS), F32),
             pltpu.VMEM((2, LOCAL * PLANES * ROWS, 128), F32),
+            pltpu.SemaphoreType.DMA,
         ],
         name="window",
     )(slab, state, theta, forcing, low, high, boxes)
@@ -208,6 +216,7 @@
             jax.ShapeDtypeStruct((GROUPS, 8, 128), F32),
             jax.ShapeDtypeStruct((8, 128), F32),
         ),
+        compiler_params=pltpu.CompilerParams(vmem_limit_bytes=4 * MIB),
         name="own_predictions",
     )(arrived, count)
 
@@ -250,11 +259,12 @@
     return pl.pallas_call(
         moments_kernel,
         out_shape=jax.ShapeDtypeStruct((SLABS, 8, 128), F32),
+        compiler_params=pltpu.CompilerParams(vmem_limit_bytes=4 * MIB),
         name="moments",
     )(preds, own, observed, noise, perturb)
 
 
-def update_kernel(group, arrived, theta, out):
+def update_kernel(group, arrived, theta, others, out):
     packed = jnp.sum(arrived[...], axis=0)
     lane8 = lax.broadcasted_iota(jnp.int32, (8, 128), 1)
     blocks = []
@@ -281,28 +291,32 @@
     mixing = (gain - jnp.mean(gain, axis=0, keepdims=True)) * (1.0 / float(MEMBERS - 1) ** 0.5)
     first = group[0] * LOCAL
     mixing = jnp.where(row - first == lane - MEMBERS, mixing + 1.0, mixing)
-    columns = [
-        jnp.broadcast_to(mixing[:, MEMBERS + j : MEMBERS + j + 1], (MEMBERS, 128))
-        for j in range(LOCAL)
-    ]
-    totals = [jnp.zeros((64, 128), F32) for j in range(LOCAL)]
-    for k in range(MEMBERS):
-        field = theta[k]
-        for j in range(LOCAL):
-            totals[j] = totals[j] + columns[j][k : k + 1, :] * field
+    south = group[0] % 2 == 0
+    totals = [jnp.zeros((64, 128), F32) for _ in range(LOCAL)]
+    for j in range(LOCAL):
+        column = jnp.broadcast_to(mixing[:, MEMBERS + j : MEMBERS + j + 1], (MEMBERS, 128))
+        later = pltpu.roll(column, MEMBERS - 2, 0)
+        here = jnp.where(south, column, later)
+        there = jnp.where(south, later, column)
+        for y in range(GROUPS // 2):
+            for m in range(LOCAL):
+                at = 4 * y + m
+                totals[j] = totals[j] + here[at : at + 1, :] * theta[2 * y + m]
+                totals[j] = totals[j] + there[at : at + 1, :] * others[2 * y + m]
     for j in range(LOCAL):
         out[j] = totals[j]
 
 
-def update(group, arrived, theta):
+def update(group, arrived, theta, others):
     vmem = pl.BlockSpec(memory_space=pltpu.VMEM)
     return pl.pallas_call(
         update_kernel,
         out_shape=jax.ShapeDtypeStruct((LOCAL, 64, 128), F32),
-        in_specs=[pl.BlockSpec(memory_space=pltpu.SMEM), vmem, vmem],
+        in_specs=[pl.BlockSpec(memory_space=pltpu.SMEM)] + [vmem] * 3,
         out_specs=vmem,
+        compiler_params=pltpu.CompilerParams(vmem_limit_bytes=4 * MIB),
         name="update",
-    )(group, arrived, theta)
+    )(group, arrived, theta, others)
 
 
 def local(state, theta, forcing, boxes, observed, noise_var, perturb):
@@ -312,16 +326,18 @@
     low = lax.ppermute(last, "slab", [(i, i + 1) for i in range(SLABS - 1)])
     high = lax.ppermute(first, "slab", [(i + 1, i) for i in range(SLABS - 1)])
     field = theta.reshape(1, LOCAL, 64, 128)
-    fields = lax.all_to_all(
-        jnp.broadcast_to(field, (GROUPS, LOCAL, 64, 128)), "group", 0, 0, tiled=True
-    ).reshape(MEMBERS, 64, 128)
+    copies = jnp.broadcast_to(field, (GROUPS // 2, LOCAL, 64, 128))
+    sides = [list(range(core, GROUPS, 2)) for core in range(2)]
+    fields = lax.all_to_all(copies, "group", 0, 0, axis_index_groups=sides, tiled=True)
+    fields = fields.reshape(GROUPS, 64, 128)
+    others = lax.ppermute(fields, "group", [(i, i ^ 1) for i in range(GROUPS)])
     final, part, count = window(slab, state, theta, forcing, low, high, boxes)
     arrived = lax.all_to_all(part, "slab", 0, 0, tiled=True)
     copies, own = own_predictions(arrived, count)
     preds = lax.all_to_all(copies, "group", 0, 0, tiled=True).reshape(GROUPS * 8, 128)
     sums = moments(preds, own, observed.reshape(1, BLOCK), noise_var.reshape(1, BLOCK), perturb)
     sums = lax.all_to_all(sums, "slab", 0, 0, tiled=True)
-    updated = update(group, sums, fields)
+    updated = update(group, sums, fields, others)
     return final, updated.reshape(theta.shape)
 
 

time: 136 us -> 91.8 us (0.67)
  blocking collectives: 58 us -> 18.1 us
  starting transfers between devices: 10.3 us -> 35.2 us
  Pallas kernels: 30.6 us -> 14.4 us
  waiting for transfers between devices: 33.2 us -> 20.4 us
    all_to_all x2 -> x0, blocking collectives: 39.7 us -> none  [the longest x1 25.1 us: local(): arrived = lax.all_to_all(part, 'slab', 0, 0, tiled=True)]
    all_to_all x1 -> x3, starting transfers between devices: 5.08 us -> 26.5 us  [the longest x1 14.9 us: local(): arrived = lax.all_to_all(part, 'slab', 0, 0, tiled=True)]
    all_to_all x1 -> x3, waiting for transfers between devices: 28 us -> 14.9 us  [the longest x1 9.84 us: local(): sums = lax.all_to_all(sums, 'slab', 0, 0, tiled=True)]
    pallas_call x1, Pallas kernels: 12.1 us -> 1.12 us  [pack(): pl.pallas_call(pack_kernel, out_shape=(shape, shape), in_specs=[pl.BlockS...]
    ppermute x0 -> x1, starting transfers between devices: none -> 4.28 us  [local(): others = lax.ppermute(fields, 'group', [(i, i ^ 1) for i in range(GROUPS)])]
    pallas_call x1, Pallas kernels: 1.58 us -> 0.04 us  [own_predictions(): pl.pallas_call(gather_kernel, out_shape=(jax.ShapeDtypeStruct((GROUPS, 8,...]
    pallas_call x1, Pallas kernels: 9.92 us -> 8.46 us  [window(): pl.pallas_call(window_kernel, out_shape=(jax.ShapeDtypeStruct(state.shape...]
  transfers between devices with their start and end apart: 3 -> 6, of which waited for: 3 -> 4; matrix products, arithmetic and copies ran while one was open for 0% -> 0% of each run, Pallas kernels for 0% -> 12%
where the time goes in v2:
time: 91.8 us; the launch traced here: 91.2 us
  starting transfers between devices  35.2 us (38%)
  waiting for transfers between devices  20.4 us (22%)
  blocking collectives  18.1 us (20%)
  Pallas kernels  14.4 us (16%)
  local copies, waits for them, and re-layouts  2.42 us (3%)
    all_to_all x1, blocking collectives, local(): lax.all_to_all(copies, 'group', 0, 0, tiled=True).reshape(GROUPS * 8, 128)  18.1 us
    all_to_all x1, starting transfers between devices, local(): arrived = lax.all_to_all(part, 'slab', 0, 0, tiled=True)  14.9 us
    all_to_all x1, waiting for transfers between devices, local(): sums = lax.all_to_all(sums, 'slab', 0, 0, tiled=True)  9.84 us
    pallas_call x1, Pallas kernels, window(): pl.pallas_call(window_kernel, out_shape=(jax.ShapeDtypeStruct(state.shape...  8.46 us
    all_to_all x1, starting transfers between devices, local(): lax.all_to_all(copies, 'group', 0, 0, axis_index_groups=sides, tiled=True)  7.77 us
    all_to_all x1, waiting for transfers between devices, local(): arrived = lax.all_to_all(part, 'slab', 0, 0, tiled=True)  5.05 us
    ppermute x1, starting transfers between devices, local(): others = lax.ppermute(fields, 'group', [(i, i ^ 1) for i in range(GROUPS)])  4.28 us
    all_to_all x1, starting transfers between devices, local(): sums = lax.all_to_all(sums, 'slab', 0, 0, tiled=True)  3.85 us
  transfers between devices with their start and end apart: 6, of which 4 were waited for; matrix products, arithmetic and copies ran while one was open for 0% of the time, Pallas kernels for 12%

profile of v2, /device:TPU:1, one launch (start us, length us, event | category | flops | bytes accessed | tf_op | source)
XLA Modules:
  0.0 91.2 jit_solution(1851436799279615708)
XLA Ops:
  0.6 1.7 %broadcast_in_dim.8 = f32[8,2,64,128]{3,2,1,0:T(8,128)} broadcast(f32[2,64,128]{2,1,0:T(8,128)} %bitcast.10), dimensions={1,2,3} | broadcast | bytes 589824 | tf_op jit(solution)/shard_map/broadcast_in_dim | solution.py:329
  2.3 7.8 %all-to-all-start.3 = ((f32[8,2,64,128]{3,2,1,0:T(8,128)}), f32[8,2,64,128]{3,2,1,0:T(8,128)S(1)}, u32[]{:S(2)}, u32[]{:S(2)}) async-start(f32[8,2,64,128]{3,2,1,0:T(8,128)} %broadcast_in_dim.8), calls=%async_computation.3 | async-start | bytes 1048576 | tf_op jit(solution)/shard_map/all_to_all | solution.py:331
  10.1 0.0 copy-start.1
  10.1 0.0 copy-start.2
  10.1 1.1 %pack.1 = (f32[176,256]{1,0:T(8,128)S(1)}, f32[176,256]{1,0:T(8,128)S(1)}) custom-call(f32[2,8,32,256]{3,2,1,0:T(8,128)} %state.3, f32[2,4,16,128]{3,2,1,0:T(8,128)} %theta.3, f32[8,32,256]{2,1,0:T(8,128)} %forcing.3), custom_call_target="tpu_custom_call" | custom-call | tf_op jit(solution)/shard_map/pack/pallas_call | solution.py:56
  11.3 3.1 %collective-permute-start = (f32[176,256]{1,0:T(8,128)S(1)}, f32[176,256]{1,0:T(8,128)S(1)}, u32[]{:S(2)}, u32[]{:S(2)}) collective-permute-start(f32[176,256]{1,0:T(8,128)S(1)} %get-tuple-element.9), channel_id=1, source_target_pairs={{0,1},{1,2},{2,3},{3,4},{4,5},{5,6},{6,7},{7,8},{8,9},{9,10},{10,1... | collective-permute-start | bytes 540680 | tf_op jit(solution)/shard_map/ppermute | solution.py:326
  14.4 1.3 %collective-permute-start.1 = (f32[176,256]{1,0:T(8,128)S(1)}, f32[176,256]{1,0:T(8,128)S(1)}, u32[]{:S(2)}, u32[]{:S(2)}) collective-permute-start(f32[176,256]{1,0:T(8,128)S(1)} %get-tuple-element.10), channel_id=1, source_target_pairs={{1,0},{2,1},{3,2},{4,3},{5,4},{6,5},{7,6},{8,7},{9,8},{10,9},{11,1... | collective-permute-start | bytes 540680 | tf_op jit(solution)/shard_map/ppermute | solution.py:327
  15.7 1.6 %collective-permute-done.low = f32[176,256]{1,0:T(8,128)S(1)} collective-permute-done((f32[176,256]{1,0:T(8,128)S(1)}, f32[176,256]{1,0:T(8,128)S(1)}, u32[]{:S(2)}, u32[]{:S(2)}) %collective-permute-start) | collective-permute-done | bytes 180256 | tf_op jit(solution)/shard_map/ppermute | solution.py:326
  17.3 3.8 %collective-permute-done.1.high = f32[176,256]{1,0:T(8,128)S(1)} collective-permute-done((f32[176,256]{1,0:T(8,128)S(1)}, f32[176,256]{1,0:T(8,128)S(1)}, u32[]{:S(2)}, u32[]{:S(2)}) %collective-permute-start.1) | collective-permute-done | bytes 180256 | tf_op jit(solution)/shard_map/ppermute | solution.py:327
  21.2 0.0 copy-done.3
  21.2 0.0 copy-done.1
  21.2 8.5 %window.1 = (f32[2,8,32,256]{3,2,1,0:T(8,128)}, f32[32,8,128]{2,1,0:T(8,128)}, f32[8,128]{1,0:T(8,128)S(1)}) custom-call(s32[1]{0:T(128)} %bitcast.slab, f32[2,8,32,256]{3,2,1,0:T(8,128)S(1)} %copy-done, f32[2,4,16,128]{3,2,1,0:T(8,128)S(1)} %copy-done.2, f32[8,32,256]{2,1,0:T(8,128)S(1)} %copy-done.1, f32[176,256]{1,0:T(8,128)S(1)} %collective-permute-done.low, ...), custom_call_target="tpu_custom_call" | custom-call | tf_op jit(solution)/shard_map/window/pallas_call | solution.py:184
  29.6 0.0 all-to-all-done.3
  29.7 14.9 %all-to-all-start = ((f32[32,8,128]{2,1,0:T(8,128)}), f32[32,8,128]{2,1,0:T(8,128)S(1)}, u32[]{:S(2)}, u32[]{:S(2)}) async-start(f32[32,8,128]{2,1,0:T(8,128)} %get-tuple-element.12), calls=%async_computation | async-start | bytes 262144 | tf_op jit(solution)/shard_map/all_to_all | solution.py:335
  44.6 4.3 %collective-permute-start.2 = (f32[16,64,128]{2,1,0:T(8,128)S(1)}, f32[16,64,128]{2,1,0:T(8,128)S(1)}, u32[]{:S(2)}, u32[]{:S(2)}) collective-permute-start(f32[16,64,128]{2,1,0:T(8,128)S(1)} %bitcast.8), channel_id=1, source_target_pairs={{0,32},{32,0},{64,96},{96,64},{128,160},{160,128},{192,224},{224,1... | collective-permute-start | bytes 1572872 | tf_op jit(solution)/shard_map/ppermute | solution.py:333
  48.9 5.1 %all-to-all-done.arrived = f32[32,8,128]{2,1,0:T(8,128)S(1)} async-done(((f32[32,8,128]{2,1,0:T(8,128)}), f32[32,8,128]{2,1,0:T(8,128)S(1)}, u32[]{:S(2)}, u32[]{:S(2)}) %all-to-all-start) | async-done | bytes 131104 | tf_op jit(solution)/shard_map/all_to_all | solution.py:335
  54.0 18.1 %all_to_all.20 = f32[16,8,128]{2,1,0:T(8,128)S(1)} all-to-all(f32[16,8,128]{2,1,0:T(8,128)S(1)} %get-tuple-element.14), channel_id=1, replica_groups=mesh['group'=16,'slab'=32] {'group'}, dimensions={0} | all-to-all | bytes 131072 | tf_op jit(solution)/shard_map/all_to_all | solution.py:337
  72.0 0.7 copy-done.4
  72.7 0.0 copy-done.5
  72.7 1.0 %moments.1 = f32[32,8,128]{2,1,0:T(8,128)} custom-call(f32[128,128]{1,0:T(8,128)S(1)} %bitcast.11, f32[8,128]{1,0:T(8,128)S(1)} %get-tuple-element.15.own, f32[1,512]{1,0:T(1,128)S(1)} %bitcast.12, f32[1,512]{1,0:T(1,128)S(1)} %bitcast.13, f32[2,512]{1,0:T(2,128)S(1)} %copy-done.4), custom_call_target="tpu_custom_call" | custom-call | tf_op jit(solution)/shard_map/moments/pallas_call | solution.py:259
  73.8 3.8 %all-to-all-start.2 = ((f32[32,8,128]{2,1,0:T(8,128)}), f32[32,8,128]{2,1,0:T(8,128)S(1)}, u32[]{:S(2)}, u32[]{:S(2)}) async-start(f32[32,8,128]{2,1,0:T(8,128)} %moments.1), calls=%async_computation.2 | async-start | bytes 262144 | tf_op jit(solution)/shard_map/all_to_all | solution.py:339
  77.6 9.8 %all-to-all-done.2.arrived = f32[32,8,128]{2,1,0:T(8,128)S(1)} async-done(((f32[32,8,128]{2,1,0:T(8,128)}), f32[32,8,128]{2,1,0:T(8,128)S(1)}, u32[]{:S(2)}, u32[]{:S(2)}) %all-to-all-start.2) | async-done | bytes 131104 | tf_op jit(solution)/shard_map/all_to_all | solution.py:339
  87.5 0.0 collective-permute-done.2.others
  87.5 3.8 %update.1 = f32[2,64,128]{2,1,0:T(8,128)} custom-call(s32[1]{0:T(128)} %bitcast.1.group, f32[32,8,128]{2,1,0:T(8,128)S(1)} %all-to-all-done.2.arrived, f32[16,64,128]{2,1,0:T(8,128)S(1)} %bitcast.9, f32[16,64,128]{2,1,0:T(8,128)S(1)} %collective-permute-done.2.others), custom_call_target="tpu_custom_call" | custom-call | tf_op jit(solution)/shard_map/update/pallas_call | solution.py:312
  (9 shorter events, 0.1 us)
Async XLA Ops:
  2.3 18.8 %copy-start.3 = (s32[6,16384]{1,0:T(8,128)S(1)}, s32[6,16384]{1,0:T(8,128)}, u32[]{:S(2)}) copy-start(s32[6,16384]{1,0:T(8,128)} %boxes.1) | copy-start | bytes 1179652
  2.3 27.3 %all-to-all-start.3 = ((f32[8,2,64,128]{3,2,1,0:T(8,128)}), f32[8,2,64,128]{3,2,1,0:T(8,128)S(1)}, u32[]{:S(2)}, u32[]{:S(2)}) async-start(f32[8,2,64,128]{3,2,1,0:T(8,128)} %broadcast_in_dim.8), calls=%async_computation.3 | async-start | bytes 1048576 | tf_op jit(solution)/shard_map/all_to_all | solution.py:331
  10.1 11.1 %copy-start = (f32[2,8,32,256]{3,2,1,0:T(8,128)S(1)}, f32[2,8,32,256]{3,2,1,0:T(8,128)}, u32[]{:S(2)}) copy-start(f32[2,8,32,256]{3,2,1,0:T(8,128)} %state.3) | copy-start | bytes 1572868
  10.1 11.1 %copy-start.1 = (f32[8,32,256]{2,1,0:T(8,128)S(1)}, f32[8,32,256]{2,1,0:T(8,128)}, u32[]{:S(2)}) copy-start(f32[8,32,256]{2,1,0:T(8,128)} %forcing.3) | copy-start | bytes 786436
  10.1 11.1 %copy-start.2 = (f32[2,4,16,128]{3,2,1,0:T(8,128)S(1)}, f32[2,4,16,128]{3,2,1,0:T(8,128)}, u32[]{:S(2)}) copy-start(f32[2,4,16,128]{3,2,1,0:T(8,128)} %theta.3) | copy-start | bytes 196612
  11.3 6.1 %collective-permute-start = (f32[176,256]{1,0:T(8,128)S(1)}, f32[176,256]{1,0:T(8,128)S(1)}, u32[]{:S(2)}, u32[]{:S(2)}) collective-permute-start(f32[176,256]{1,0:T(8,128)S(1)} %get-tuple-element.9), channel_id=1, source_target_pairs={{0,1},{1,2},{2,3},{3,4},{4,5},{5,6},{6,7},{7,8},{8,9},{9,10},{10,1... | collective-permute-start | bytes 540680 | tf_op jit(solution)/shard_map/ppermute | solution.py:326
  14.4 6.8 %collective-permute-start.1 = (f32[176,256]{1,0:T(8,128)S(1)}, f32[176,256]{1,0:T(8,128)S(1)}, u32[]{:S(2)}, u32[]{:S(2)}) collective-permute-start(f32[176,256]{1,0:T(8,128)S(1)} %get-tuple-element.10), channel_id=1, source_target_pairs={{1,0},{2,1},{3,2},{4,3},{5,4},{6,5},{7,6},{8,7},{9,8},{10,9},{11,1... | collective-permute-start | bytes 540680 | tf_op jit(solution)/shard_map/ppermute | solution.py:327
  29.7 24.3 %all-to-all-start = ((f32[32,8,128]{2,1,0:T(8,128)}), f32[32,8,128]{2,1,0:T(8,128)S(1)}, u32[]{:S(2)}, u32[]{:S(2)}) async-start(f32[32,8,128]{2,1,0:T(8,128)} %get-tuple-element.12), calls=%async_computation | async-start | bytes 262144 | tf_op jit(solution)/shard_map/all_to_all | solution.py:335
  44.6 42.9 %collective-permute-start.2 = (f32[16,64,128]{2,1,0:T(8,128)S(1)}, f32[16,64,128]{2,1,0:T(8,128)S(1)}, u32[]{:S(2)}, u32[]{:S(2)}) collective-permute-start(f32[16,64,128]{2,1,0:T(8,128)S(1)} %bitcast.8), channel_id=1, source_target_pairs={{0,32},{32,0},{64,96},{96,64},{128,160},{160,128},{192,224},{224,1... | collective-permute-start | bytes 1572872 | tf_op jit(solution)/shard_map/ppermute | solution.py:333
  54.0 18.1 %copy-start.6 = (f32[512]{0:T(512)S(1)}, f32[512]{0:T(512)}, u32[]{:S(2)}) copy-start(f32[512]{0:T(512)} %param.12) | copy-start | bytes 6148
  72.0 0.7 copy-start.4
  72.0 0.7 copy-start.5
  73.8 13.7 %all-to-all-start.2 = ((f32[32,8,128]{2,1,0:T(8,128)}), f32[32,8,128]{2,1,0:T(8,128)S(1)}, u32[]{:S(2)}, u32[]{:S(2)}) async-start(f32[32,8,128]{2,1,0:T(8,128)} %moments.1), calls=%async_computation.2 | async-start | bytes 262144 | tf_op jit(solution)/shard_map/all_to_all | solution.py:339

commit v3 on v2

--- a/solution.py
+++ b/solution.py
@@ -20,6 +20,8 @@
 MEMBERS = 32
 BLOCK = 512
 MIB = 1 << 20
+EVEN = (0, -2, 2, 4)
+ODD = (-1, -3, 1, 3)
 HALO_ROWS = 176
 
 
@@ -64,7 +66,12 @@
     )(*(pltpu.with_memory_space_constraint(a, pltpu.HBM) for a in (state, theta, forcing)))
 
 
-def window_kernel(slab, state, theta, forcing, low, high, boxes, final, part, count, diff, mid, fresh, done, sem):
+def window_kernel(
+    slab, state, theta, forcing, low, high, observed, noise, perturb, footprints,
+    final, part, count, given, diff, mid, fresh, done, boxes, sems,
+):
+    enter = pltpu.make_async_copy(footprints, boxes, sems.at[0])
+    enter.start()
     s = slab[0]
     keep_low = jnp.where(s > 0, 0.5, 0.0).astype(F32)
     keep_high = jnp.where(s < SLABS - 1, 0.5, 0.0).astype(F32)
@@ -130,7 +137,7 @@
             for h in range(2):
                 done[h, to : to + ROWS, :] = new[:, h * 128 : (h + 1) * 128]
 
-    leave = pltpu.make_async_copy(fresh, final, sem)
+    leave = pltpu.make_async_copy(fresh, final, sems.at[1])
     leave.start()
 
     tall = LOCAL * PLANES * 8
@@ -146,6 +153,7 @@
     lane = lax.broadcasted_iota(jnp.int32, (tall, 128), 1)
     left = jnp.where(lane < 64, top, tiles - top).astype(BF16)
 
+    enter.wait()
     iota_x = lax.broadcasted_iota(jnp.int32, (64, BLOCK), 0)
     iota_y = lax.broadcasted_iota(jnp.int32, (8, BLOCK), 0)
 
@@ -169,17 +177,21 @@
                 part[d, m * 4 + q : m * 4 + q + 1, :] = total[:, q * 128 : (q + 1) * 128]
         return carry
 
-    lax.fori_loop(0, SLABS, observe, 0)
+    lax.fori_loop(0, SLABS, observe, 0, unroll=4)
 
     b = boxes[:, pl.ds(pl.multiple_of(s * BLOCK, BLOCK), BLOCK)]
     cells = ((b[1:2] - b[0:1]) * (b[3:4] - b[2:3]) * (b[5:6] - b[4:5]) * 16).astype(F32)
     for m in range(LOCAL):
         for q in range(4):
             count[m * 4 + q : m * 4 + q + 1, :] = cells[:, q * 128 : (q + 1) * 128]
+    var = noise[...]
+    given[0:LOCAL, :] = observed[...] + jnp.sqrt(var) * perturb[...]
+    given[LOCAL : LOCAL + 1, :] = var
+    given[LOCAL + 1 : 8, :] = jnp.zeros((5, BLOCK), F32)
     leave.wait()
 
 
-def window(slab, state, theta, forcing, low, high, boxes):
+def window(slab, state, theta, forcing, low, high, boxes, observed, noise, perturb):
     vmem = pl.BlockSpec(memory_space=pltpu.VMEM)
     return pl.pallas_call(
         window_kernel,
@@ -187,19 +199,26 @@
             jax.ShapeDtypeStruct(state.shape, F32),
             jax.ShapeDtypeStruct((SLABS, 8, 128), F32),
             jax.ShapeDtypeStruct((8, 128), F32),
+            jax.ShapeDtypeStruct((8, BLOCK), F32),
         ),
-        in_specs=[pl.BlockSpec(memory_space=pltpu.SMEM)] + [vmem] * 6,
-        out_specs=(pl.BlockSpec(memory_space=pltpu.HBM), vmem, vmem),
+        in_specs=[pl.BlockSpec(memory_space=pltpu.SMEM)]
+        + [vmem] * 8
+        + [pl.BlockSpec(memory_space=pltpu.HBM)],
+        out_specs=(pl.BlockSpec(memory_space=pltpu.HBM), vmem, vmem, vmem),
         compiler_params=pltpu.CompilerParams(vmem_limit_bytes=12 * MIB),
         scratch_shapes=[
             pltpu.VMEM((2, LOCAL * (COARSE + 2) * ROWS, 128), F32),
             pltpu.VMEM((LOCAL * (PLANES + 2), ROWS, COLS), F32),
             pltpu.VMEM((LOCAL, PLANES, ROWS, COLS), F32),
             pltpu.VMEM((2, LOCAL * PLANES * ROWS, 128), F32),
-            pltpu.SemaphoreType.DMA,
+            pltpu.VMEM(boxes.shape, jnp.int32),
+            pltpu.SemaphoreType.DMA((2,)),
         ],
         name="window",
-    )(slab, state, theta, forcing, low, high, boxes)
+    )(
+        slab, state, theta, forcing, low, high, observed, noise, perturb,
+        pltpu.with_memory_space_constraint(boxes, pltpu.HBM),
+    )
 
 
 def gather_kernel(arrived, count, copies, own):
@@ -221,102 +240,112 @@
     )(arrived, count)
 
 
-def moments_kernel(preds, own, observed, noise, perturb, out):
+def moments_kernel(preds, own, given, out):
     scale = 1.0 / (float(MEMBERS - 1) ** 0.5)
     everyone = jnp.concatenate(
         [preds[pl.ds(q, MEMBERS, stride=4), :] for q in range(4)], axis=1
     )
     mine = jnp.concatenate([own[pl.ds(q, LOCAL, stride=4), :] for q in range(4)], axis=1)
     anomaly = (everyone - jnp.mean(everyone, axis=0, keepdims=True)) * scale
-    var = noise[...]
-    misfit = observed[...] + jnp.sqrt(var) * perturb[...] - mine
+    misfit = given[0:LOCAL, :] - mine
+    var = given[LOCAL : LOCAL + 1, :]
     weighted = anomaly / var
-    left = jnp.concatenate([anomaly, misfit, jnp.zeros((6, BLOCK), F32)], axis=0)
+    pad = jnp.zeros((6, BLOCK), F32)
     right = jnp.concatenate(
-        [
-            weighted,
-            weighted[8:],
-            weighted[16:],
-            weighted[24:],
-            weighted,
-            jnp.zeros((16, BLOCK), F32),
-        ],
+        [anomaly, anomaly[8:], anomaly[16:], anomaly[24:]]
+        + [misfit, pad] * 4
+        + [jnp.zeros((16, BLOCK), F32)],
         axis=0,
     )
     product = lax.dot_general(
-        left, right, (((1,), (1,)), ((), ())), precision=lax.Precision.HIGHEST,
+        weighted, right, (((1,), (1,)), ((), ())), precision=lax.Precision.HIGHEST,
         preferred_element_type=F32,
     )
     lane = lax.broadcasted_iota(jnp.int32, (8, 128), 1)
     packed = product[0:8]
-    for start, at in ((32, 8), (56, 16), (72, 24), (80, 32)):
-        packed = jnp.where(lane >= start, product[at : at + 8], packed)
+    for c, start, stop in ((1, 32, 56), (2, 56, 72), (3, 72, 80)):
+        mine = ((lane >= start) & (lane < stop)) | (lane // 8 == 10 + c)
+        packed = jnp.where(mine, product[8 * c : 8 * c + 8], packed)
     for d in range(SLABS):
         out[d] = packed
 
 
-def moments(preds, own, observed, noise, perturb):
+def moments(preds, own, given):
     return pl.pallas_call(
         moments_kernel,
         out_shape=jax.ShapeDtypeStruct((SLABS, 8, 128), F32),
         compiler_params=pltpu.CompilerParams(vmem_limit_bytes=4 * MIB),
         name="moments",
-    )(preds, own, observed, noise, perturb)
-
-
-def update_kernel(group, arrived, theta, others, out):
-    packed = jnp.sum(arrived[...], axis=0)
+    )(preds, own, given)
+
+
+def update_kernel(group, arrived, even, odd, even_other, odd_other, out):
+    parts = [arrived[d] for d in range(SLABS)]
+    while len(parts) > 1:
+        parts = [x + y for x, y in zip(parts[::2], parts[1::2])]
+    packed = parts[0]
     lane8 = lax.broadcasted_iota(jnp.int32, (8, 128), 1)
-    blocks = []
+    uppers, cross = [], []
     for c, start in enumerate((0, 32, 56, 72)):
         moved = pltpu.roll(packed, (8 * c - start) % 128, 1)
-        blocks.append(jnp.where((lane8 >= 8 * c) & (lane8 < 32), moved, 0.0))
-    upper = jnp.concatenate(blocks + [jnp.zeros((96, 128), F32)], axis=0)
-    mirrored = upper.T[0:MEMBERS]
-    upper = upper[0:MEMBERS]
+        uppers.append(jnp.where((lane8 >= 8 * c) & (lane8 < MEMBERS), moved, 0.0))
+        cross.append(pltpu.roll(packed, (MEMBERS - 80 - 8 * c) % 128, 1))
+    upper = jnp.concatenate(uppers, axis=0)
+    cross = jnp.concatenate(cross, axis=0)
+    tall = jnp.concatenate([upper, jnp.zeros((96, 128), F32)], axis=0)
+    mirrored = tall.T[0:MEMBERS]
     row = lax.broadcasted_iota(jnp.int32, (MEMBERS, 128), 0)
     lane = lax.broadcasted_iota(jnp.int32, (MEMBERS, 128), 1)
-    matrix = jnp.where(lane // 8 >= row // 8, upper, mirrored)
-    matrix = jnp.where(row == lane, matrix + 1.0, matrix)
-    cross_rows = jnp.where(lane8 < MEMBERS, pltpu.roll(packed, 128 - 80, 1), 0.0)
-    cross = jnp.concatenate([cross_rows, jnp.zeros((120, 128), F32)], axis=0).T[0:MEMBERS]
-    cross = pltpu.roll(cross, MEMBERS, 1)
-    work = jnp.where((lane >= MEMBERS) & (lane < MEMBERS + LOCAL), cross, matrix)
-    for k in range(MEMBERS):
-        column = jnp.broadcast_to(work[:, k : k + 1], (MEMBERS, 128))
-        pivot = column[k : k + 1, :]
-        line = work[k : k + 1, :] / pivot
-        work = jnp.where(row == k, line, work - column * line)
-    gain = work
-    mixing = (gain - jnp.mean(gain, axis=0, keepdims=True)) * (1.0 / float(MEMBERS - 1) ** 0.5)
-    first = group[0] * LOCAL
-    mixing = jnp.where(row - first == lane - MEMBERS, mixing + 1.0, mixing)
+    work = jnp.where(lane // 8 >= row // 8, upper, mirrored)
+    work = jnp.where(row == lane, work + 1.0, work)
+    work = jnp.where(lane < MEMBERS, work, jnp.where(lane < MEMBERS + LOCAL, cross, 0.0))
+    for first in range(0, MEMBERS, 8):
+        columns = [
+            jnp.broadcast_to(work[:, k : k + 1], (MEMBERS, 128)) for k in range(first, first + 8)
+        ]
+        for i in range(8):
+            k = first + i
+            column = columns[i]
+            inverse = 1.0 / column[k : k + 1, :]
+            line = work[k : k + 1, :] * inverse
+            work = jnp.where(row == k, line, work - column * line)
+            for later in range(i + 1, 8):
+                line = columns[later][k : k + 1, :] * inverse
+                columns[later] = jnp.where(row == k, line, columns[later] - column * line)
+    mixing = work - jnp.mean(work, axis=0, keepdims=True)
+    mixing = mixing * (1.0 / float(MEMBERS - 1) ** 0.5)
+    mixing = jnp.where(row - group[0] * LOCAL == lane - MEMBERS, mixing + 1.0, mixing)
     south = group[0] % 2 == 0
+    turn = MEMBERS - LOCAL * group[0]
     totals = [jnp.zeros((64, 128), F32) for _ in range(LOCAL)]
     for j in range(LOCAL):
         column = jnp.broadcast_to(mixing[:, MEMBERS + j : MEMBERS + j + 1], (MEMBERS, 128))
-        later = pltpu.roll(column, MEMBERS - 2, 0)
-        here = jnp.where(south, column, later)
-        there = jnp.where(south, later, column)
-        for y in range(GROUPS // 2):
-            for m in range(LOCAL):
-                at = 4 * y + m
-                totals[j] = totals[j] + here[at : at + 1, :] * theta[2 * y + m]
-                totals[j] = totals[j] + there[at : at + 1, :] * others[2 * y + m]
+        here = pltpu.roll(column, turn, 0)
+        there = jnp.where(south, pltpu.roll(here, MEMBERS - 2, 0), pltpu.roll(here, 2, 0))
+        for rows, fields, offsets in (
+            (here, even, EVEN),
+            (here, odd, ODD),
+            (there, even_other, EVEN),
+            (there, odd_other, ODD),
+        ):
+            for i, offset in enumerate(offsets):
+                for m in range(LOCAL):
+                    at = (4 * offset + m) % MEMBERS
+                    totals[j] = totals[j] + rows[at : at + 1, :] * fields[2 * i + m]
     for j in range(LOCAL):
         out[j] = totals[j]
 
 
-def update(group, arrived, theta, others):
+def update(group, arrived, *fields):
     vmem = pl.BlockSpec(memory_space=pltpu.VMEM)
     return pl.pallas_call(
         update_kernel,
         out_shape=jax.ShapeDtypeStruct((LOCAL, 64, 128), F32),
-        in_specs=[pl.BlockSpec(memory_space=pltpu.SMEM)] + [vmem] * 3,
+        in_specs=[pl.BlockSpec(memory_space=pltpu.SMEM)] + [vmem] * 5,
         out_specs=vmem,
         compiler_params=pltpu.CompilerParams(vmem_limit_bytes=4 * MIB),
         name="update",
-    )(group, arrived, theta, others)
+    )(group, arrived, *fields)
 
 
 def local(state, theta, forcing, boxes, observed, noise_var, perturb):
@@ -325,19 +354,32 @@
     first, last = pack(state, theta, forcing)
     low = lax.ppermute(last, "slab", [(i, i + 1) for i in range(SLABS - 1)])
     high = lax.ppermute(first, "slab", [(i + 1, i) for i in range(SLABS - 1)])
-    field = theta.reshape(1, LOCAL, 64, 128)
-    copies = jnp.broadcast_to(field, (GROUPS // 2, LOCAL, 64, 128))
-    sides = [list(range(core, GROUPS, 2)) for core in range(2)]
-    fields = lax.all_to_all(copies, "group", 0, 0, axis_index_groups=sides, tiled=True)
-    fields = fields.reshape(GROUPS, 64, 128)
-    others = lax.ppermute(fields, "group", [(i, i ^ 1) for i in range(GROUPS)])
-    final, part, count = window(slab, state, theta, forcing, low, high, boxes)
+    field = theta.reshape(LOCAL, 64, 128)
+
+    def along_y(value, chips):
+        moves = [(i, (i + 2 * chips) % GROUPS) for i in range(GROUPS)]
+        return lax.ppermute(value, "group", moves)
+
+    def other_core(value):
+        return lax.ppermute(value, "group", [(i, i ^ 1) for i in range(GROUPS)])
+
+    before = along_y(field, 2)
+    after = along_y(field, -2)
+    across = along_y(field, 4)
+    final, part, count, given = window(
+        slab, state, theta, forcing, low, high, boxes,
+        observed.reshape(1, BLOCK), noise_var.reshape(1, BLOCK), perturb,
+    )
     arrived = lax.all_to_all(part, "slab", 0, 0, tiled=True)
+    even = jnp.concatenate([field, before, after, across], axis=0)
+    odd = along_y(even, 1)
+    even_other = other_core(even)
     copies, own = own_predictions(arrived, count)
     preds = lax.all_to_all(copies, "group", 0, 0, tiled=True).reshape(GROUPS * 8, 128)
-    sums = moments(preds, own, observed.reshape(1, BLOCK), noise_var.reshape(1, BLOCK), perturb)
+    odd_other = other_core(odd)
+    sums = moments(preds, own, given)
     sums = lax.all_to_all(sums, "slab", 0, 0, tiled=True)
-    updated = update(group, sums, fields, others)
+    updated = update(group, sums, even, odd, even_other, odd_other)
     return final, updated.reshape(theta.shape)
 
 

time: 91.8 us -> 83.9 us (0.914)
  blocking collectives: 18.1 us -> 0 us
  starting transfers between devices: 35.2 us -> 50.9 us
  Pallas kernels: 14.4 us -> 10.6 us
  local copies, waits for them, and re-layouts: 2.42 us -> 0.67 us
    all_to_all x1 -> x0, blocking collectives: 18.1 us -> none  [local(): lax.all_to_all(copies, 'group', 0, 0, tiled=True).reshape(GROUPS * 8, 128)]
    ppermute x1 -> x6, starting transfers between devices: 4.28 us -> 20.3 us  [the longest x4 16 us: along_y(): return lax.ppermute(value, 'group', moves)]
    ppermute x1, waiting for transfers between devices: 3.84 us -> 0.01 us  [local(): high = lax.ppermute(first, 'slab', [(i + 1, i) for i in range(SLABS - 1)])]
    all_to_all x1, waiting for transfers between devices: 0.01 us -> 3.43 us  [local(): lax.all_to_all(copies, 'group', 0, 0, tiled=True).reshape(GROUPS * 8, 128)]
    pallas_call x1, Pallas kernels: 8.46 us -> 5.96 us  [window(): pl.pallas_call(window_kernel, out_shape=(jax.ShapeDtypeStruct(state.shape...]
    pallas_call x1, Pallas kernels: 3.76 us -> 1.81 us  [update(): pl.pallas_call(update_kernel, out_shape=jax.ShapeDtypeStruct((LOCAL, 64,...]
    all_to_all x1, waiting for transfers between devices: 5.05 us -> 6.96 us  [local(): arrived = lax.all_to_all(part, 'slab', 0, 0, tiled=True)]
    broadcast_in_dim x1 -> x0, local copies, waits for them, and re-layouts: 1.7 us -> none  [local(): copies = jnp.broadcast_to(field, (GROUPS // 2, LOCAL, 64, 128))]
  transfers between devices with their start and end apart: 6 -> 11, of which waited for: 4 -> 3; matrix products, arithmetic and copies ran while one was open for 0% -> 0% of each run, Pallas kernels for 12% -> 9%
where the time goes in v3:
time: 83.9 us; the launch traced here: 83.3 us
  starting transfers between devices  50.9 us (61%)
  waiting for transfers between devices  20.2 us (24%)
  Pallas kernels  10.6 us (13%)
  between operations  0.89 us (1%)
    ppermute x4, starting transfers between devices, along_y(): return lax.ppermute(value, 'group', moves)  16 us
    all_to_all x1, starting transfers between devices, local(): arrived = lax.all_to_all(part, 'slab', 0, 0, tiled=True)  14.6 us
    all_to_all x1, waiting for transfers between devices, local(): sums = lax.all_to_all(sums, 'slab', 0, 0, tiled=True)  9.82 us
    all_to_all x1, starting transfers between devices, local(): lax.all_to_all(copies, 'group', 0, 0, tiled=True).reshape(GROUPS * 8, 128)  6.96 us
    all_to_all x1, waiting for transfers between devices, local(): arrived = lax.all_to_all(part, 'slab', 0, 0, tiled=True)  6.96 us
    pallas_call x1, Pallas kernels, window(): pl.pallas_call(window_kernel, out_shape=(jax.ShapeDtypeStruct(state.shape...  5.96 us
    ppermute x2, starting transfers between devices, other_core(): return lax.ppermute(value, 'group', [(i, i ^ 1) for i in range(GROUPS)])  4.31 us
    ppermute x1, starting transfers between devices, local(): low = lax.ppermute(last, 'slab', [(i, i + 1) for i in range(SLABS - 1)])  3.94 us
  transfers between devices with their start and end apart: 11, of which 3 were waited for; matrix products, arithmetic and copies ran while one was open for 0% of the time, Pallas kernels for 9%

profile of v3, /device:TPU:1, one launch (start us, length us, event | category | flops | bytes accessed | tf_op | source)
XLA Modules:
  0.0 83.3 jit_solution(834151940756533614)
XLA Ops:
  0.7 1.1 %pack.1 = (f32[176,256]{1,0:T(8,128)S(1)}, f32[176,256]{1,0:T(8,128)S(1)}) custom-call(f32[2,8,32,256]{3,2,1,0:T(8,128)} %state.3, f32[2,4,16,128]{3,2,1,0:T(8,128)} %theta.3, f32[8,32,256]{2,1,0:T(8,128)} %forcing.3), custom_call_target="tpu_custom_call" | custom-call | tf_op jit(solution)/shard_map/pack/pallas_call | solution.py:58
  1.8 3.9 %collective-permute-start = (f32[176,256]{1,0:T(8,128)S(1)}, f32[176,256]{1,0:T(8,128)S(1)}, u32[]{:S(2)}, u32[]{:S(2)}) collective-permute-start(f32[176,256]{1,0:T(8,128)S(1)} %get-tuple-element.10), channel_id=1, source_target_pairs={{0,1},{1,2},{2,3},{3,4},{4,5},{5,6},{6,7},{7,8},{8,9},{9,10},{10,1... | collective-permute-start | bytes 540680 | tf_op jit(solution)/shard_map/ppermute | solution.py:355
  5.7 0.0 copy-start.5
  5.8 1.3 %collective-permute-start.1 = (f32[176,256]{1,0:T(8,128)S(1)}, f32[176,256]{1,0:T(8,128)S(1)}, u32[]{:S(2)}, u32[]{:S(2)}) collective-permute-start(f32[176,256]{1,0:T(8,128)S(1)} %get-tuple-element.11), channel_id=1, source_target_pairs={{1,0},{2,1},{3,2},{4,3},{5,4},{6,5},{7,6},{8,7},{9,8},{10,9},{11,1... | collective-permute-start | bytes 540680 | tf_op jit(solution)/shard_map/ppermute | solution.py:356
  7.1 7.5 %collective-permute-start.4 = (f32[2,64,128]{2,1,0:T(8,128)S(1)}, f32[2,64,128]{2,1,0:T(8,128)S(1)}, u32[]{:S(2)}, u32[]{:S(2)}) collective-permute-start(f32[2,64,128]{2,1,0:T(8,128)S(1)} %bitcast.7), channel_id=1, source_target_pairs={{0,256},{32,288},{64,320},{96,352},{128,384},{160,416},{192,448},{... | collective-permute-start | bytes 196616 | tf_op jit(solution)/shard_map/ppermute | solution.py:361
  14.5 2.0 %collective-permute-start.3 = (f32[2,64,128]{2,1,0:T(8,128)S(1)}, f32[2,64,128]{2,1,0:T(8,128)S(1)}, u32[]{:S(2)}, u32[]{:S(2)}) collective-permute-start(f32[2,64,128]{2,1,0:T(8,128)S(1)} %bitcast.8), channel_id=1, source_target_pairs={{0,384},{32,416},{64,448},{96,480},{128,0},{160,32},{192,64},{224,... | collective-permute-start | bytes 196616 | tf_op jit(solution)/shard_map/ppermute | solution.py:361
  16.5 4.2 %collective-permute-start.2 = (f32[2,64,128]{2,1,0:T(8,128)S(1)}, f32[2,64,128]{2,1,0:T(8,128)S(1)}, u32[]{:S(2)}, u32[]{:S(2)}) collective-permute-start(f32[2,64,128]{2,1,0:T(8,128)S(1)} %bitcast.9), channel_id=1, source_target_pairs={{0,128},{32,160},{64,192},{96,224},{128,256},{160,288},{192,320},{... | collective-permute-start | bytes 196616 | tf_op jit(solution)/shard_map/ppermute | solution.py:361
  20.7 0.0 copy-start.3
  20.8 0.0 copy-start.4
  20.8 0.6 copy-done.3
  21.4 0.0 copy-done.4
  21.4 6.0 %window.1 = (f32[2,8,32,256]{3,2,1,0:T(8,128)}, f32[32,8,128]{2,1,0:T(8,128)}, f32[8,128]{1,0:T(8,128)S(1)}, f32[8,512]{1,0:T(8,128)S(1)}) custom-call(s32[1]{0:T(128)} %bitcast.slab, f32[2,8,32,256]{3,2,1,0:T(8,128)S(1)} %copy-done, f32[2,4,16,128]{3,2,1,0:T(8,128)S(1)} %copy-done.2, f32[8,32,256]{2,1,0:T(8,128)S(1)} %copy-done.1, ...), custom_call_target="tpu_custom_call" | custom-call | tf_op jit(solution)/shard_map/window/pallas_call | solution.py:196
  27.4 14.6 %all-to-all-start = ((f32[32,8,128]{2,1,0:T(8,128)}), f32[32,8,128]{2,1,0:T(8,128)S(1)}, u32[]{:S(2)}, u32[]{:S(2)}) async-start(f32[32,8,128]{2,1,0:T(8,128)} %get-tuple-element.13), calls=%async_computation | async-start | bytes 262144 | tf_op jit(solution)/shard_map/all_to_all | solution.py:373
  42.1 2.3 %collective-permute-start.5 = (f32[8,64,128]{2,1,0:T(8,128)S(1)}, f32[8,64,128]{2,1,0:T(8,128)S(1)}, u32[]{:S(2)}, u32[]{:S(2)}) collective-permute-start(f32[8,64,128]{2,1,0:T(8,128)S(1)} %pad_maximum_fusion.even), channel_id=1, source_target_pairs={{0,64},{32,96},{64,128},{96,160},{128,192},{160,224},{192,256},{22... | collective-permute-start | bytes 786440 | tf_op jit(solution)/shard_map/ppermute | solution.py:361
  44.4 7.0 %all-to-all-done.arrived = f32[32,8,128]{2,1,0:T(8,128)S(1)} async-done(((f32[32,8,128]{2,1,0:T(8,128)}), f32[32,8,128]{2,1,0:T(8,128)S(1)}, u32[]{:S(2)}, u32[]{:S(2)}) %all-to-all-start) | async-done | bytes 131104 | tf_op jit(solution)/shard_map/all_to_all | solution.py:373
  51.3 0.7 own_predictions.1
  52.0 7.0 %all-to-all-start.1 = ((f32[16,8,128]{2,1,0:T(8,128)}), f32[16,8,128]{2,1,0:T(8,128)S(1)}, u32[]{:S(2)}, u32[]{:S(2)}) async-start(f32[16,8,128]{2,1,0:T(8,128)} %get-tuple-element.15), calls=%async_computation.1 | async-start | bytes 131072 | tf_op jit(solution)/shard_map/all_to_all | solution.py:378
  59.0 2.0 %collective-permute-start.6 = (f32[8,64,128]{2,1,0:T(8,128)S(1)}, f32[8,64,128]{2,1,0:T(8,128)S(1)}, u32[]{:S(2)}, u32[]{:S(2)}) collective-permute-start(f32[8,64,128]{2,1,0:T(8,128)S(1)} %pad_maximum_fusion.even), channel_id=1, source_target_pairs={{0,32},{32,0},{64,96},{96,64},{128,160},{160,128},{192,224},{224,1... | collective-permute-start | bytes 786440 | tf_op jit(solution)/shard_map/ppermute | solution.py:364
  61.0 2.3 %collective-permute-start.7 = (f32[8,64,128]{2,1,0:T(8,128)S(1)}, f32[8,64,128]{2,1,0:T(8,128)S(1)}, u32[]{:S(2)}, u32[]{:S(2)}) collective-permute-start(f32[8,64,128]{2,1,0:T(8,128)S(1)} %collective-permute-done.5.odd), channel_id=1, source_target_pairs={{0,32},{32,0},{64,96},{96,64},{128,160},{160,128},{192,224},{224,1... | collective-permute-start | bytes 786440 | tf_op jit(solution)/shard_map/ppermute | solution.py:364
  63.3 3.4 %all-to-all-done.1 = f32[16,8,128]{2,1,0:T(8,128)S(1)} async-done(((f32[16,8,128]{2,1,0:T(8,128)}), f32[16,8,128]{2,1,0:T(8,128)S(1)}, u32[]{:S(2)}, u32[]{:S(2)}) %all-to-all-start.1) | async-done | bytes 65568 | tf_op jit(solution)/shard_map/all_to_all | solution.py:378
  66.7 1.0 %moments.1 = f32[32,8,128]{2,1,0:T(8,128)} custom-call(f32[128,128]{1,0:T(8,128)S(1)} %bitcast.11, f32[8,128]{1,0:T(8,128)S(1)} %get-tuple-element.16.own, f32[8,512]{1,0:T(8,128)S(1)} %get-tuple-element.17.given), custom_call_target="tpu_custom_call" | custom-call | tf_op jit(solution)/shard_map/moments/pallas_call | solution.py:274
  67.8 3.9 %all-to-all-start.2 = ((f32[32,8,128]{2,1,0:T(8,128)}), f32[32,8,128]{2,1,0:T(8,128)S(1)}, u32[]{:S(2)}, u32[]{:S(2)}) async-start(f32[32,8,128]{2,1,0:T(8,128)} %moments.1), calls=%async_computation.2 | async-start | bytes 262144 | tf_op jit(solution)/shard_map/all_to_all | solution.py:381
  71.6 9.8 %all-to-all-done.2.arrived = f32[32,8,128]{2,1,0:T(8,128)S(1)} async-done(((f32[32,8,128]{2,1,0:T(8,128)}), f32[32,8,128]{2,1,0:T(8,128)S(1)}, u32[]{:S(2)}, u32[]{:S(2)}) %all-to-all-start.2) | async-done | bytes 131104 | tf_op jit(solution)/shard_map/all_to_all | solution.py:381
  81.5 1.8 %update.1 = f32[2,64,128]{2,1,0:T(8,128)} custom-call(s32[1]{0:T(128)} %bitcast.3.group, f32[32,8,128]{2,1,0:T(8,128)S(1)} %all-to-all-done.2.arrived, f32[8,64,128]{2,1,0:T(8,128)S(1)} %pad_maximum_fusion.even, f32[8,64,128]{2,1,0:T(8,128)S(1)} %collective-permute-done.5.odd, f32[8,64,128]{2,1,0:T(8,128)S(1)} %collective-permute-done.6.even_other, ...), custom_call_target="tpu_custom_call" | custom-call | tf_op jit(solution)/shard_map/update/pallas_call | solution.py:341
  (16 shorter events, 0.1 us)
Async XLA Ops:
  0.6 20.1 %copy-start = (f32[2,8,32,256]{3,2,1,0:T(8,128)S(1)}, f32[2,8,32,256]{3,2,1,0:T(8,128)}, u32[]{:S(2)}) copy-start(f32[2,8,32,256]{3,2,1,0:T(8,128)} %state.3) | copy-start | bytes 1572868
  0.6 6.4 %copy-start.2 = (f32[2,4,16,128]{3,2,1,0:T(8,128)S(1)}, f32[2,4,16,128]{3,2,1,0:T(8,128)}, u32[]{:S(2)}) copy-start(f32[2,4,16,128]{3,2,1,0:T(8,128)} %theta.3) | copy-start | bytes 196612
  0.6 20.1 %copy-start.1 = (f32[8,32,256]{2,1,0:T(8,128)S(1)}, f32[8,32,256]{2,1,0:T(8,128)}, u32[]{:S(2)}) copy-start(f32[8,32,256]{2,1,0:T(8,128)} %forcing.3) | copy-start | bytes 786436
  1.8 19.0 %collective-permute-start = (f32[176,256]{1,0:T(8,128)S(1)}, f32[176,256]{1,0:T(8,128)S(1)}, u32[]{:S(2)}, u32[]{:S(2)}) collective-permute-start(f32[176,256]{1,0:T(8,128)S(1)} %get-tuple-element.10), channel_id=1, source_target_pairs={{0,1},{1,2},{2,3},{3,4},{4,5},{5,6},{6,7},{7,8},{8,9},{9,10},{10,1... | collective-permute-start | bytes 540680 | tf_op jit(solution)/shard_map/ppermute | solution.py:355
  5.7 15.1 %copy-start.5 = (f32[512]{0:T(512)S(1)}, f32[512]{0:T(512)}, u32[]{:S(2)}) copy-start(f32[512]{0:T(512)} %param.12) | copy-start | bytes 6148
  5.8 15.0 %collective-permute-start.1 = (f32[176,256]{1,0:T(8,128)S(1)}, f32[176,256]{1,0:T(8,128)S(1)}, u32[]{:S(2)}, u32[]{:S(2)}) collective-permute-start(f32[176,256]{1,0:T(8,128)S(1)} %get-tuple-element.11), channel_id=1, source_target_pairs={{1,0},{2,1},{3,2},{4,3},{5,4},{6,5},{7,6},{8,7},{9,8},{10,9},{11,1... | collective-permute-start | bytes 540680 | tf_op jit(solution)/shard_map/ppermute | solution.py:356
  7.1 34.9 %collective-permute-start.4 = (f32[2,64,128]{2,1,0:T(8,128)S(1)}, f32[2,64,128]{2,1,0:T(8,128)S(1)}, u32[]{:S(2)}, u32[]{:S(2)}) collective-permute-start(f32[2,64,128]{2,1,0:T(8,128)S(1)} %bitcast.7), channel_id=1, source_target_pairs={{0,256},{32,288},{64,320},{96,352},{128,384},{160,416},{192,448},{... | collective-permute-start | bytes 196616 | tf_op jit(solution)/shard_map/ppermute | solution.py:361
  14.5 27.5 %collective-permute-start.3 = (f32[2,64,128]{2,1,0:T(8,128)S(1)}, f32[2,64,128]{2,1,0:T(8,128)S(1)}, u32[]{:S(2)}, u32[]{:S(2)}) collective-permute-start(f32[2,64,128]{2,1,0:T(8,128)S(1)} %bitcast.8), channel_id=1, source_target_pairs={{0,384},{32,416},{64,448},{96,480},{128,0},{160,32},{192,64},{224,... | collective-permute-start | bytes 196616 | tf_op jit(solution)/shard_map/ppermute | solution.py:361
  16.5 25.5 %collective-permute-start.2 = (f32[2,64,128]{2,1,0:T(8,128)S(1)}, f32[2,64,128]{2,1,0:T(8,128)S(1)}, u32[]{:S(2)}, u32[]{:S(2)}) collective-permute-start(f32[2,64,128]{2,1,0:T(8,128)S(1)} %bitcast.9), channel_id=1, source_target_pairs={{0,128},{32,160},{64,192},{96,224},{128,256},{160,288},{192,320},{... | collective-permute-start | bytes 196616 | tf_op jit(solution)/shard_map/ppermute | solution.py:361
  20.7 0.7 copy-start.3
  20.8 0.7 copy-start.4
  27.4 23.9 %all-to-all-start = ((f32[32,8,128]{2,1,0:T(8,128)}), f32[32,8,128]{2,1,0:T(8,128)S(1)}, u32[]{:S(2)}, u32[]{:S(2)}) async-start(f32[32,8,128]{2,1,0:T(8,128)} %get-tuple-element.13), calls=%async_computation | async-start | bytes 262144 | tf_op jit(solution)/shard_map/all_to_all | solution.py:373
  42.1 18.9 %collective-permute-start.5 = (f32[8,64,128]{2,1,0:T(8,128)S(1)}, f32[8,64,128]{2,1,0:T(8,128)S(1)}, u32[]{:S(2)}, u32[]{:S(2)}) collective-permute-start(f32[8,64,128]{2,1,0:T(8,128)S(1)} %pad_maximum_fusion.even), channel_id=1, source_target_pairs={{0,64},{32,96},{64,128},{96,160},{128,192},{160,224},{192,256},{22... | collective-permute-start | bytes 786440 | tf_op jit(solution)/shard_map/ppermute | solution.py:361
  52.0 14.7 %all-to-all-start.1 = ((f32[16,8,128]{2,1,0:T(8,128)}), f32[16,8,128]{2,1,0:T(8,128)S(1)}, u32[]{:S(2)}, u32[]{:S(2)}) async-start(f32[16,8,128]{2,1,0:T(8,128)} %get-tuple-element.15), calls=%async_computation.1 | async-start | bytes 131072 | tf_op jit(solution)/shard_map/all_to_all | solution.py:378
  59.0 12.6 %collective-permute-start.6 = (f32[8,64,128]{2,1,0:T(8,128)S(1)}, f32[8,64,128]{2,1,0:T(8,128)S(1)}, u32[]{:S(2)}, u32[]{:S(2)}) collective-permute-start(f32[8,64,128]{2,1,0:T(8,128)S(1)} %pad_maximum_fusion.even), channel_id=1, source_target_pairs={{0,32},{32,0},{64,96},{96,64},{128,160},{160,128},{192,224},{224,1... | collective-permute-start | bytes 786440 | tf_op jit(solution)/shard_map/ppermute | solution.py:364
  61.0 10.6 %collective-permute-start.7 = (f32[8,64,128]{2,1,0:T(8,128)S(1)}, f32[8,64,128]{2,1,0:T(8,128)S(1)}, u32[]{:S(2)}, u32[]{:S(2)}) collective-permute-start(f32[8,64,128]{2,1,0:T(8,128)S(1)} %collective-permute-done.5.odd), channel_id=1, source_target_pairs={{0,32},{32,0},{64,96},{96,64},{128,160},{160,128},{192,224},{224,1... | collective-permute-start | bytes 786440 | tf_op jit(solution)/shard_map/ppermute | solution.py:364
  67.8 13.7 %all-to-all-start.2 = ((f32[32,8,128]{2,1,0:T(8,128)}), f32[32,8,128]{2,1,0:T(8,128)S(1)}, u32[]{:S(2)}, u32[]{:S(2)}) async-start(f32[32,8,128]{2,1,0:T(8,128)} %moments.1), calls=%async_computation.2 | async-start | bytes 262144 | tf_op jit(solution)/shard_map/all_to_all | solution.py:381

commit v4 on v3

--- a/solution.py
+++ b/solution.py
@@ -20,8 +20,7 @@
 MEMBERS = 32
 BLOCK = 512
 MIB = 1 << 20
-EVEN = (0, -2, 2, 4)
-ODD = (-1, -3, 1, 3)
+PARTS = (0, 1, 2, 3, -3, -2, -1, 4)
 HALO_ROWS = 176
 
 
@@ -68,10 +67,16 @@
 
 def window_kernel(
     slab, state, theta, forcing, low, high, observed, noise, perturb, footprints,
-    final, part, count, given, diff, mid, fresh, done, boxes, sems,
+    final, part, count, given, diff, mid, fresh, done, boxes, target, spread, draws, sems,
 ):
-    enter = pltpu.make_async_copy(footprints, boxes, sems.at[0])
-    enter.start()
+    enter = [
+        pltpu.make_async_copy(src, dst, sems.at[i])
+        for i, (src, dst) in enumerate(
+            ((footprints, boxes), (observed, target), (noise, spread), (perturb, draws))
+        )
+    ]
+    for e in enter:
+        e.start()
     s = slab[0]
     keep_low = jnp.where(s > 0, 0.5, 0.0).astype(F32)
     keep_high = jnp.where(s < SLABS - 1, 0.5, 0.0).astype(F32)
@@ -137,7 +142,7 @@
             for h in range(2):
                 done[h, to : to + ROWS, :] = new[:, h * 128 : (h + 1) * 128]
 
-    leave = pltpu.make_async_copy(fresh, final, sems.at[1])
+    leave = pltpu.make_async_copy(fresh, final, sems.at[4])
     leave.start()
 
     tall = LOCAL * PLANES * 8
@@ -153,7 +158,8 @@
     lane = lax.broadcasted_iota(jnp.int32, (tall, 128), 1)
     left = jnp.where(lane < 64, top, tiles - top).astype(BF16)
 
-    enter.wait()
+    for e in enter:
+        e.wait()
     iota_x = lax.broadcasted_iota(jnp.int32, (64, BLOCK), 0)
     iota_y = lax.broadcasted_iota(jnp.int32, (8, BLOCK), 0)
 
@@ -184,14 +190,14 @@
     for m in range(LOCAL):
         for q in range(4):
             count[m * 4 + q : m * 4 + q + 1, :] = cells[:, q * 128 : (q + 1) * 128]
-    var = noise[...]
-    given[0:LOCAL, :] = observed[...] + jnp.sqrt(var) * perturb[...]
+    var = spread[...]
+    given[0:LOCAL, :] = target[...] + jnp.sqrt(var) * draws[...]
     given[LOCAL : LOCAL + 1, :] = var
     given[LOCAL + 1 : 8, :] = jnp.zeros((5, BLOCK), F32)
     leave.wait()
 
 
-def window(slab, state, theta, forcing, low, high, boxes, observed, noise, perturb):
+def window(slab, state, theta, forcing, low, high, *kept):
     vmem = pl.BlockSpec(memory_space=pltpu.VMEM)
     return pl.pallas_call(
         window_kernel,
@@ -202,8 +208,8 @@
             jax.ShapeDtypeStruct((8, BLOCK), F32),
         ),
         in_specs=[pl.BlockSpec(memory_space=pltpu.SMEM)]
-        + [vmem] * 8
-        + [pl.BlockSpec(memory_space=pltpu.HBM)],
+        + [vmem] * 5
+        + [pl.BlockSpec(memory_space=pltpu.HBM)] * 4,
         out_specs=(pl.BlockSpec(memory_space=pltpu.HBM), vmem, vmem, vmem),
         compiler_params=pltpu.CompilerParams(vmem_limit_bytes=12 * MIB),
         scratch_shapes=[
@@ -211,13 +217,16 @@
             pltpu.VMEM((LOCAL * (PLANES + 2), ROWS, COLS), F32),
             pltpu.VMEM((LOCAL, PLANES, ROWS, COLS), F32),
             pltpu.VMEM((2, LOCAL * PLANES * ROWS, 128), F32),
-            pltpu.VMEM(boxes.shape, jnp.int32),
-            pltpu.SemaphoreType.DMA((2,)),
+            pltpu.VMEM(kept[-1].shape, jnp.int32),
+            pltpu.VMEM((1, BLOCK), F32),
+            pltpu.VMEM((1, BLOCK), F32),
+            pltpu.VMEM((LOCAL, BLOCK), F32),
+            pltpu.SemaphoreType.DMA((5,)),
         ],
         name="window",
     )(
-        slab, state, theta, forcing, low, high, observed, noise, perturb,
-        pltpu.with_memory_space_constraint(boxes, pltpu.HBM),
+        slab, state, theta, forcing, low, high,
+        *(pltpu.with_memory_space_constraint(a, pltpu.HBM) for a in kept),
     )
 
 
@@ -279,7 +288,7 @@
     )(preds, own, given)
 
 
-def update_kernel(group, arrived, even, odd, even_other, odd_other, out):
+def update_kernel(group, arrived, here, there, out):
     parts = [arrived[d] for d in range(SLABS)]
     while len(parts) > 1:
         parts = [x + y for x, y in zip(parts[::2], parts[1::2])]
@@ -320,18 +329,18 @@
     totals = [jnp.zeros((64, 128), F32) for _ in range(LOCAL)]
     for j in range(LOCAL):
         column = jnp.broadcast_to(mixing[:, MEMBERS + j : MEMBERS + j + 1], (MEMBERS, 128))
-        here = pltpu.roll(column, turn, 0)
-        there = jnp.where(south, pltpu.roll(here, MEMBERS - 2, 0), pltpu.roll(here, 2, 0))
-        for rows, fields, offsets in (
-            (here, even, EVEN),
-            (here, odd, ODD),
-            (there, even_other, EVEN),
-            (there, odd_other, ODD),
-        ):
-            for i, offset in enumerate(offsets):
-                for m in range(LOCAL):
-                    at = (4 * offset + m) % MEMBERS
-                    totals[j] = totals[j] + rows[at : at + 1, :] * fields[2 * i + m]
+        rows = pltpu.roll(column, turn, 0)
+
+        def weight(at_south, at_north):
+            at_south, at_north = at_south % MEMBERS, at_north % MEMBERS
+            return jnp.where(
+                south, rows[at_south : at_south + 1, :], rows[at_north : at_north + 1, :]
+            )
+
+        for i, d in enumerate(PARTS):
+            for m in range(LOCAL):
+                totals[j] = totals[j] + weight(4 * d + m, m - 4 * d) * here[2 * i + m]
+                totals[j] = totals[j] + weight(2 + m - 4 * d, 4 * d + m - 2) * there[2 * i + m]
     for j in range(LOCAL):
         out[j] = totals[j]
 
@@ -341,7 +350,7 @@
     return pl.pallas_call(
         update_kernel,
         out_shape=jax.ShapeDtypeStruct((LOCAL, 64, 128), F32),
-        in_specs=[pl.BlockSpec(memory_space=pltpu.SMEM)] + [vmem] * 5,
+        in_specs=[pl.BlockSpec(memory_space=pltpu.SMEM)] + [vmem] * 3,
         out_specs=vmem,
         compiler_params=pltpu.CompilerParams(vmem_limit_bytes=4 * MIB),
         name="update",
@@ -356,30 +365,31 @@
     high = lax.ppermute(first, "slab", [(i + 1, i) for i in range(SLABS - 1)])
     field = theta.reshape(LOCAL, 64, 128)
 
-    def along_y(value, chips):
-        moves = [(i, (i + 2 * chips) % GROUPS) for i in range(GROUPS)]
+    def from_chip(value, chips):
+        half = GROUPS // 2
+        moves = [
+            (((y + (1 - 2 * core) * chips) % half) * 2 + core, y * 2 + core)
+            for y in range(half)
+            for core in range(2)
+        ]
         return lax.ppermute(value, "group", moves)
 
-    def other_core(value):
-        return lax.ppermute(value, "group", [(i, i ^ 1) for i in range(GROUPS)])
-
-    before = along_y(field, 2)
-    after = along_y(field, -2)
-    across = along_y(field, 4)
+    one = from_chip(field, 1)
     final, part, count, given = window(
-        slab, state, theta, forcing, low, high, boxes,
-        observed.reshape(1, BLOCK), noise_var.reshape(1, BLOCK), perturb,
+        slab, state, theta, forcing, low, high,
+        observed.reshape(1, BLOCK), noise_var.reshape(1, BLOCK), perturb, boxes,
     )
     arrived = lax.all_to_all(part, "slab", 0, 0, tiled=True)
-    even = jnp.concatenate([field, before, after, across], axis=0)
-    odd = along_y(even, 1)
-    even_other = other_core(even)
+    two = from_chip(jnp.concatenate([field, one], axis=0), 2)
     copies, own = own_predictions(arrived, count)
     preds = lax.all_to_all(copies, "group", 0, 0, tiled=True).reshape(GROUPS * 8, 128)
-    odd_other = other_core(odd)
+    back = from_chip(jnp.concatenate([field, one, two[:LOCAL]], axis=0), -3)
+    far = from_chip(two[LOCAL:], 1)
     sums = moments(preds, own, given)
     sums = lax.all_to_all(sums, "slab", 0, 0, tiled=True)
-    updated = update(group, sums, even, odd, even_other, odd_other)
+    here = jnp.concatenate([field, one, two, back, far], axis=0)
+    there = lax.ppermute(here, "group", [(i, i ^ 1) for i in range(GROUPS)])
+    updated = update(group, sums, here, there)
     return final, updated.reshape(theta.shape)
 
 

time: 83.9 us -> 92 us (1.097)
  blocking collectives: 0 us -> 14.5 us
  waiting for transfers between devices: 20.2 us -> 16.8 us
  starting transfers between devices: 50.9 us -> 48.4 us
    all_to_all x0 -> x1, blocking collectives: none -> 14.5 us  [local(): lax.all_to_all(copies, 'group', 0, 0, tiled=True).reshape(GROUPS * 8, 128)]
    all_to_all x1 -> x0, starting transfers between devices: 6.96 us -> none  [local(): lax.all_to_all(copies, 'group', 0, 0, tiled=True).reshape(GROUPS * 8, 128)]
    all_to_all x1, waiting for transfers between devices: 6.96 us -> 0.01 us  [local(): arrived = lax.all_to_all(part, 'slab', 0, 0, tiled=True)]
    ppermute x6 -> x5, waiting for transfers between devices: 0.02 us -> 6.88 us  [the longest x4 6.88 us: from_chip(): return lax.ppermute(value, 'group', moves)]
    all_to_all x1 -> x0, waiting for transfers between devices: 3.43 us -> none  [local(): lax.all_to_all(copies, 'group', 0, 0, tiled=True).reshape(GROUPS * 8, 128)]
    all_to_all x1, starting transfers between devices: 3.85 us -> 7.2 us  [local(): sums = lax.all_to_all(sums, 'slab', 0, 0, tiled=True)]
    ppermute x6 -> x5, starting transfers between devices: 20.3 us -> 22.1 us  [the longest x4 14.8 us: from_chip(): return lax.ppermute(value, 'group', moves)]
  transfers between devices with their start and end apart: 11 -> 9, of which waited for: 3 -> 5; matrix products, arithmetic and copies ran while one was open for 0% -> 0% of each run, Pallas kernels for 9% -> 9%
where the time goes in v4:
time: 92 us; the launch traced here: 91.4 us
  starting transfers between devices  48.4 us (53%)
  waiting for transfers between devices  16.8 us (18%)
  blocking collectives  14.5 us (16%)
  Pallas kernels  9.93 us (11%)
    ppermute x4, starting transfers between devices, from_chip(): return lax.ppermute(value, 'group', moves)  14.8 us
    all_to_all x1, starting transfers between devices, local(): arrived = lax.all_to_all(part, 'slab', 0, 0, tiled=True)  14.6 us
    all_to_all x1, blocking collectives, local(): lax.all_to_all(copies, 'group', 0, 0, tiled=True).reshape(GROUPS * 8, 128)  14.5 us
    all_to_all x1, waiting for transfers between devices, local(): sums = lax.all_to_all(sums, 'slab', 0, 0, tiled=True)  9.83 us
    ppermute x1, starting transfers between devices, local(): there = lax.ppermute(here, 'group', [(i, i ^ 1) for i in range(GROUPS)])  7.32 us
    all_to_all x1, starting transfers between devices, local(): sums = lax.all_to_all(sums, 'slab', 0, 0, tiled=True)  7.2 us
    ppermute x4, waiting for transfers between devices, from_chip(): return lax.ppermute(value, 'group', moves)  6.88 us
    pallas_call x1, Pallas kernels, window(): pl.pallas_call(window_kernel, out_shape=(jax.ShapeDtypeStruct(state.shape...  6 us
  transfers between devices with their start and end apart: 9, of which 5 were waited for; matrix products, arithmetic and copies ran while one was open for 0% of the time, Pallas kernels for 9%

profile of v4, /device:TPU:1, one launch (start us, length us, event | category | flops | bytes accessed | tf_op | source)
XLA Modules:
  0.0 91.4 jit_solution(11421509100670423666)
XLA Ops:
  0.6 4.0 %collective-permute-start.2 = (f32[2,64,128]{2,1,0:T(8,128)}, f32[2,64,128]{2,1,0:T(8,128)S(1)}, u32[]{:S(2)}, u32[]{:S(2)}) collective-permute-start(f32[2,64,128]{2,1,0:T(8,128)} %bitcast.7), channel_id=1, source_target_pairs={{64,0},{480,32},{128,64},{32,96},{192,128},{96,160},{256,192},{160... | collective-permute-start | bytes 196616 | tf_op jit(solution)/shard_map/ppermute | solution.py:375
  4.7 3.7 %collective-permute-done.2 = f32[2,64,128]{2,1,0:T(8,128)S(1)} collective-permute-done((f32[2,64,128]{2,1,0:T(8,128)}, f32[2,64,128]{2,1,0:T(8,128)S(1)}, u32[]{:S(2)}, u32[]{:S(2)}) %collective-permute-start.2) | collective-permute-done | bytes 65568 | tf_op jit(solution)/shard_map/ppermute | solution.py:375
  8.4 0.8 pad_maximum_fusion.1
  9.3 0.0 copy-start.1
  9.3 2.7 %collective-permute-start.3 = (f32[4,64,128]{2,1,0:T(8,128)S(1)}, f32[4,64,128]{2,1,0:T(8,128)S(1)}, u32[]{:S(2)}, u32[]{:S(2)}) collective-permute-start(f32[4,64,128]{2,1,0:T(8,128)S(1)} %pad_maximum_fusion.1), channel_id=1, source_target_pairs={{128,0},{416,32},{192,64},{480,96},{256,128},{32,160},{320,192},{9... | collective-permute-start | bytes 393224 | tf_op jit(solution)/shard_map/ppermute | solution.py:375
  12.0 1.1 %pack.1 = (f32[176,256]{1,0:T(8,128)S(1)}, f32[176,256]{1,0:T(8,128)S(1)}) custom-call(f32[2,8,32,256]{3,2,1,0:T(8,128)} %state.3, f32[2,4,16,128]{3,2,1,0:T(8,128)} %theta.3, f32[8,32,256]{2,1,0:T(8,128)} %forcing.3), custom_call_target="tpu_custom_call" | custom-call | tf_op jit(solution)/shard_map/pack/pallas_call | solution.py:57
  13.1 0.0 copy-start
  13.1 3.1 %collective-permute-start = (f32[176,256]{1,0:T(8,128)S(1)}, f32[176,256]{1,0:T(8,128)S(1)}, u32[]{:S(2)}, u32[]{:S(2)}) collective-permute-start(f32[176,256]{1,0:T(8,128)S(1)} %get-tuple-element.10), channel_id=1, source_target_pairs={{0,1},{1,2},{2,3},{3,4},{4,5},{5,6},{6,7},{7,8},{8,9},{9,10},{10,1... | collective-permute-start | bytes 540680 | tf_op jit(solution)/shard_map/ppermute | solution.py:364
  16.2 1.3 %collective-permute-start.1 = (f32[176,256]{1,0:T(8,128)S(1)}, f32[176,256]{1,0:T(8,128)S(1)}, u32[]{:S(2)}, u32[]{:S(2)}) collective-permute-start(f32[176,256]{1,0:T(8,128)S(1)} %get-tuple-element.11), channel_id=1, source_target_pairs={{1,0},{2,1},{3,2},{4,3},{5,4},{6,5},{7,6},{8,7},{9,8},{10,9},{11,1... | collective-permute-start | bytes 540680 | tf_op jit(solution)/shard_map/ppermute | solution.py:365
  17.6 1.0 %collective-permute-done.3 = f32[4,64,128]{2,1,0:T(8,128)S(1)} collective-permute-done((f32[4,64,128]{2,1,0:T(8,128)S(1)}, f32[4,64,128]{2,1,0:T(8,128)S(1)}, u32[]{:S(2)}, u32[]{:S(2)}) %collective-permute-start.3) | collective-permute-done | bytes 131104 | tf_op jit(solution)/shard_map/ppermute | solution.py:375
  18.6 0.0 copy-start.2
  18.6 4.0 %collective-permute-start.4 = (f32[6,64,128]{2,1,0:T(8,128)S(1)}, f32[6,64,128]{2,1,0:T(8,128)S(1)}, u32[]{:S(2)}, u32[]{:S(2)}) collective-permute-start(f32[6,64,128]{2,1,0:T(8,128)S(1)} %pad_maximum_fusion), channel_id=1, source_target_pairs={{320,0},{224,32},{384,64},{288,96},{448,128},{352,160},{0,192},{41... | collective-permute-start | bytes 589832 | tf_op jit(solution)/shard_map/ppermute | solution.py:375
  22.7 0.0 collective-permute-done.low
  22.7 0.1 collective-permute-done.1.high
  22.8 6.0 %window.1 = (f32[2,8,32,256]{3,2,1,0:T(8,128)}, f32[32,8,128]{2,1,0:T(8,128)}, f32[8,128]{1,0:T(8,128)S(1)}, f32[8,512]{1,0:T(8,128)S(1)}) custom-call(s32[1]{0:T(128)} %bitcast.slab, f32[2,8,32,256]{3,2,1,0:T(8,128)S(1)} %copy-done, f32[2,4,16,128]{3,2,1,0:T(8,128)S(1)} %copy-done.1, f32[8,32,256]{2,1,0:T(8,128)S(1)} %copy-done.2, ...), custom_call_target="tpu_custom_call" | custom-call | tf_op jit(solution)/shard_map/window/pallas_call | solution.py:202
  28.8 14.6 %all-to-all-start = ((f32[32,8,128]{2,1,0:T(8,128)}), f32[32,8,128]{2,1,0:T(8,128)S(1)}, u32[]{:S(2)}, u32[]{:S(2)}) async-start(f32[32,8,128]{2,1,0:T(8,128)} %get-tuple-element.13), calls=%async_computation | async-start | bytes 262144 | tf_op jit(solution)/shard_map/all_to_all | solution.py:382
  43.4 4.0 %collective-permute-start.5 = (f32[2,64,128]{2,1,0:T(8,128)S(1)}, f32[2,64,128]{2,1,0:T(8,128)S(1)}, u32[]{:S(2)}, u32[]{:S(2)}) collective-permute-start(f32[2,64,128]{2,1,0:T(8,128)S(1)} %get-tuple-element.18), channel_id=1, source_target_pairs={{64,0},{480,32},{128,64},{32,96},{192,128},{96,160},{256,192},{160... | collective-permute-start | bytes 196616 | tf_op jit(solution)/shard_map/ppermute | solution.py:375
  47.5 2.1 %collective-permute-done.5 = f32[2,64,128]{2,1,0:T(8,128)S(1)} collective-permute-done((f32[2,64,128]{2,1,0:T(8,128)S(1)}, f32[2,64,128]{2,1,0:T(8,128)S(1)}, u32[]{:S(2)}, u32[]{:S(2)}) %collective-permute-start.5) | collective-permute-done | bytes 65568 | tf_op jit(solution)/shard_map/ppermute | solution.py:375
  49.6 7.3 %collective-permute-start.6 = (f32[16,64,128]{2,1,0:T(8,128)S(1)}, f32[16,64,128]{2,1,0:T(8,128)S(1)}, u32[]{:S(2)}, u32[]{:S(2)}) collective-permute-start(f32[16,64,128]{2,1,0:T(8,128)S(1)} %constant_dynamic-update-slice_fusion.here), channel_id=1, source_target_pairs={{0,32},{32,0},{64,96},{96,64},{128,160},{160,128},{192,224},{224,1... | collective-permute-start | bytes 1572872 | tf_op jit(solution)/shard_map/ppermute | solution.py:391
  57.0 14.5 %all_to_all.15 = f32[16,8,128]{2,1,0:T(8,128)S(1)} all-to-all(f32[16,8,128]{2,1,0:T(8,128)S(1)} %get-tuple-element.15), channel_id=1, replica_groups=mesh['group'=16,'slab'=32] {'group'}, dimensions={0} | all-to-all | bytes 131072 | tf_op jit(solution)/shard_map/all_to_all | solution.py:385
  71.5 1.0 %moments.1 = f32[32,8,128]{2,1,0:T(8,128)} custom-call(f32[128,128]{1,0:T(8,128)S(1)} %bitcast.11, f32[8,128]{1,0:T(8,128)S(1)} %get-tuple-element.16.own, f32[8,512]{1,0:T(8,128)S(1)} %get-tuple-element.17.given), custom_call_target="tpu_custom_call" | custom-call | tf_op jit(solution)/shard_map/moments/pallas_call | solution.py:283
  72.5 7.2 %all-to-all-start.2 = ((f32[32,8,128]{2,1,0:T(8,128)}), f32[32,8,128]{2,1,0:T(8,128)S(1)}, u32[]{:S(2)}, u32[]{:S(2)}) async-start(f32[32,8,128]{2,1,0:T(8,128)} %moments.1), calls=%async_computation.2 | async-start | bytes 262144 | tf_op jit(solution)/shard_map/all_to_all | solution.py:389
  79.7 9.8 %all-to-all-done.2.arrived = f32[32,8,128]{2,1,0:T(8,128)S(1)} async-done(((f32[32,8,128]{2,1,0:T(8,128)}), f32[32,8,128]{2,1,0:T(8,128)S(1)}, u32[]{:S(2)}, u32[]{:S(2)}) %all-to-all-start.2) | async-done | bytes 131104 | tf_op jit(solution)/shard_map/all_to_all | solution.py:389
  89.6 1.8 %update.1 = f32[2,64,128]{2,1,0:T(8,128)} custom-call(s32[1]{0:T(128)} %bitcast.3.group, f32[32,8,128]{2,1,0:T(8,128)S(1)} %all-to-all-done.2.arrived, f32[16,64,128]{2,1,0:T(8,128)S(1)} %constant_dynamic-update-slice_fusion.here, f32[16,64,128]{2,1,0:T(8,128)S(1)} %collective-permute-done.6.there), custom_call_target="tpu_custom_call" | custom-call | tf_op jit(solution)/shard_map/update/pallas_call | solution.py:350
  (14 shorter events, 0.1 us)
Async XLA Ops:
  0.6 7.8 %collective-permute-start.2 = (f32[2,64,128]{2,1,0:T(8,128)}, f32[2,64,128]{2,1,0:T(8,128)S(1)}, u32[]{:S(2)}, u32[]{:S(2)}) collective-permute-start(f32[2,64,128]{2,1,0:T(8,128)} %bitcast.7), channel_id=1, source_target_pairs={{64,0},{480,32},{128,64},{32,96},{192,128},{96,160},{256,192},{160... | collective-permute-start | bytes 196616 | tf_op jit(solution)/shard_map/ppermute | solution.py:375
  9.3 8.3 %copy-start.1 = (f32[2,4,16,128]{3,2,1,0:T(8,128)S(1)}, f32[2,4,16,128]{3,2,1,0:T(8,128)}, u32[]{:S(2)}) copy-start(f32[2,4,16,128]{3,2,1,0:T(8,128)} %theta.3) | copy-start | bytes 196612
  9.3 9.3 %collective-permute-start.3 = (f32[4,64,128]{2,1,0:T(8,128)S(1)}, f32[4,64,128]{2,1,0:T(8,128)S(1)}, u32[]{:S(2)}, u32[]{:S(2)}) collective-permute-start(f32[4,64,128]{2,1,0:T(8,128)S(1)} %pad_maximum_fusion.1), channel_id=1, source_target_pairs={{128,0},{416,32},{192,64},{480,96},{256,128},{32,160},{320,192},{9... | collective-permute-start | bytes 393224 | tf_op jit(solution)/shard_map/ppermute | solution.py:375
  13.1 9.7 %copy-start = (f32[2,8,32,256]{3,2,1,0:T(8,128)S(1)}, f32[2,8,32,256]{3,2,1,0:T(8,128)}, u32[]{:S(2)}) copy-start(f32[2,8,32,256]{3,2,1,0:T(8,128)} %state.3) | copy-start | bytes 1572868
  13.1 9.6 %collective-permute-start = (f32[176,256]{1,0:T(8,128)S(1)}, f32[176,256]{1,0:T(8,128)S(1)}, u32[]{:S(2)}, u32[]{:S(2)}) collective-permute-start(f32[176,256]{1,0:T(8,128)S(1)} %get-tuple-element.10), channel_id=1, source_target_pairs={{0,1},{1,2},{2,3},{3,4},{4,5},{5,6},{6,7},{7,8},{8,9},{9,10},{10,1... | collective-permute-start | bytes 540680 | tf_op jit(solution)/shard_map/ppermute | solution.py:364
  16.2 6.5 %collective-permute-start.1 = (f32[176,256]{1,0:T(8,128)S(1)}, f32[176,256]{1,0:T(8,128)S(1)}, u32[]{:S(2)}, u32[]{:S(2)}) collective-permute-start(f32[176,256]{1,0:T(8,128)S(1)} %get-tuple-element.11), channel_id=1, source_target_pairs={{1,0},{2,1},{3,2},{4,3},{5,4},{6,5},{7,6},{8,7},{9,8},{10,9},{11,1... | collective-permute-start | bytes 540680 | tf_op jit(solution)/shard_map/ppermute | solution.py:365
  18.6 4.2 %copy-start.2 = (f32[8,32,256]{2,1,0:T(8,128)S(1)}, f32[8,32,256]{2,1,0:T(8,128)}, u32[]{:S(2)}) copy-start(f32[8,32,256]{2,1,0:T(8,128)} %forcing.3) | copy-start | bytes 786436
  18.6 28.8 %collective-permute-start.4 = (f32[6,64,128]{2,1,0:T(8,128)S(1)}, f32[6,64,128]{2,1,0:T(8,128)S(1)}, u32[]{:S(2)}, u32[]{:S(2)}) collective-permute-start(f32[6,64,128]{2,1,0:T(8,128)S(1)} %pad_maximum_fusion), channel_id=1, source_target_pairs={{320,0},{224,32},{384,64},{288,96},{448,128},{352,160},{0,192},{41... | collective-permute-start | bytes 589832 | tf_op jit(solution)/shard_map/ppermute | solution.py:375
  28.8 28.2 %all-to-all-start = ((f32[32,8,128]{2,1,0:T(8,128)}), f32[32,8,128]{2,1,0:T(8,128)S(1)}, u32[]{:S(2)}, u32[]{:S(2)}) async-start(f32[32,8,128]{2,1,0:T(8,128)} %get-tuple-element.13), calls=%async_computation | async-start | bytes 262144 | tf_op jit(solution)/shard_map/all_to_all | solution.py:382
  43.4 6.2 %collective-permute-start.5 = (f32[2,64,128]{2,1,0:T(8,128)S(1)}, f32[2,64,128]{2,1,0:T(8,128)S(1)}, u32[]{:S(2)}, u32[]{:S(2)}) collective-permute-start(f32[2,64,128]{2,1,0:T(8,128)S(1)} %get-tuple-element.18), channel_id=1, source_target_pairs={{64,0},{480,32},{128,64},{32,96},{192,128},{96,160},{256,192},{160... | collective-permute-start | bytes 196616 | tf_op jit(solution)/shard_map/ppermute | solution.py:375
  49.6 39.9 %collective-permute-start.6 = (f32[16,64,128]{2,1,0:T(8,128)S(1)}, f32[16,64,128]{2,1,0:T(8,128)S(1)}, u32[]{:S(2)}, u32[]{:S(2)}) collective-permute-start(f32[16,64,128]{2,1,0:T(8,128)S(1)} %constant_dynamic-update-slice_fusion.here), channel_id=1, source_target_pairs={{0,32},{32,0},{64,96},{96,64},{128,160},{160,128},{192,224},{224,1... | collective-permute-start | bytes 1572872 | tf_op jit(solution)/shard_map/ppermute | solution.py:391
  72.5 17.0 %all-to-all-start.2 = ((f32[32,8,128]{2,1,0:T(8,128)}), f32[32,8,128]{2,1,0:T(8,128)S(1)}, u32[]{:S(2)}, u32[]{:S(2)}) async-start(f32[32,8,128]{2,1,0:T(8,128)} %moments.1), calls=%async_computation.2 | async-start | bytes 262144 | tf_op jit(solution)/shard_map/all_to_all | solution.py:389

commit v5 on v4

--- a/solution.py
+++ b/solution.py
@@ -20,7 +20,7 @@
 MEMBERS = 32
 BLOCK = 512
 MIB = 1 << 20
-PARTS = (0, 1, 2, 3, -3, -2, -1, 4)
+PARTS = (0, 2, 4, 6, 1, 3, 5, 7)
 HALO_ROWS = 176
 
 
@@ -374,20 +374,21 @@
         ]
         return lax.ppermute(value, "group", moves)
 
-    one = from_chip(field, 1)
+    pair = from_chip(field, 2)
     final, part, count, given = window(
         slab, state, theta, forcing, low, high,
         observed.reshape(1, BLOCK), noise_var.reshape(1, BLOCK), perturb, boxes,
     )
     arrived = lax.all_to_all(part, "slab", 0, 0, tiled=True)
-    two = from_chip(jnp.concatenate([field, one], axis=0), 2)
+    pair = jnp.concatenate([field, pair], axis=0)
+    across = from_chip(pair, 4)
     copies, own = own_predictions(arrived, count)
     preds = lax.all_to_all(copies, "group", 0, 0, tiled=True).reshape(GROUPS * 8, 128)
-    back = from_chip(jnp.concatenate([field, one, two[:LOCAL]], axis=0), -3)
-    far = from_chip(two[LOCAL:], 1)
+    even = jnp.concatenate([pair, across], axis=0)
+    odd = from_chip(even, 1)
     sums = moments(preds, own, given)
     sums = lax.all_to_all(sums, "slab", 0, 0, tiled=True)
-    here = jnp.concatenate([field, one, two, back, far], axis=0)
+    here = jnp.concatenate([even, odd], axis=0)
     there = lax.ppermute(here, "group", [(i, i ^ 1) for i in range(GROUPS)])
     updated = update(group, sums, here, there)
     return final, updated.reshape(theta.shape)

time: 92 us -> 103 us (1.12)
  waiting for transfers between devices: 16.8 us -> 23.3 us
  blocking collectives: 14.5 us -> 18.7 us
    all_to_all x1, blocking collectives: 14.5 us -> 18.7 us  [local(): lax.all_to_all(copies, 'group', 0, 0, tiled=True).reshape(GROUPS * 8, 128)]
    ppermute x1, waiting for transfers between devices: 0.11 us -> 3.83 us  [local(): high = lax.ppermute(first, 'slab', [(i + 1, i) for i in range(SLABS - 1)])]
    all_to_all x1, starting transfers between devices: 7.2 us -> 3.85 us  [local(): sums = lax.all_to_all(sums, 'slab', 0, 0, tiled=True)]
    ppermute x4 -> x3, starting transfers between devices: 14.8 us -> 18.1 us  [from_chip(): return lax.ppermute(value, 'group', moves)]
    all_to_all x1, waiting for transfers between devices: 0.01 us -> 2.12 us  [local(): arrived = lax.all_to_all(part, 'slab', 0, 0, tiled=True)]
    ppermute x1, waiting for transfers between devices: 0.01 us -> 1.11 us  [local(): low = lax.ppermute(last, 'slab', [(i, i + 1) for i in range(SLABS - 1)])]
    ppermute x4 -> x3, waiting for transfers between devices: 6.88 us -> 6.4 us  [from_chip(): return lax.ppermute(value, 'group', moves)]
  transfers between devices with their start and end apart: 9 -> 8, of which waited for: 5 -> 6; matrix products, arithmetic and copies ran while one was open for 0% -> 0% of each run, Pallas kernels for 9% -> 8%
where the time goes in v5:
time: 103 us; the launch traced here: 102 us
  starting transfers between devices  48.4 us (47%)
  waiting for transfers between devices  23.3 us (23%)
  blocking collectives  18.7 us (18%)
  Pallas kernels  9.94 us (10%)
    all_to_all x1, blocking collectives, local(): lax.all_to_all(copies, 'group', 0, 0, tiled=True).reshape(GROUPS * 8, 128)  18.7 us
    ppermute x3, starting transfers between devices, from_chip(): return lax.ppermute(value, 'group', moves)  18.1 us
    all_to_all x1, starting transfers between devices, local(): arrived = lax.all_to_all(part, 'slab', 0, 0, tiled=True)  14.9 us
    all_to_all x1, waiting for transfers between devices, local(): sums = lax.all_to_all(sums, 'slab', 0, 0, tiled=True)  9.84 us
    ppermute x1, starting transfers between devices, local(): there = lax.ppermute(here, 'group', [(i, i ^ 1) for i in range(GROUPS)])  7.15 us
    ppermute x3, waiting for transfers between devices, from_chip(): return lax.ppermute(value, 'group', moves)  6.4 us
    pallas_call x1, Pallas kernels, window(): pl.pallas_call(window_kernel, out_shape=(jax.ShapeDtypeStruct(state.shape...  6 us
    all_to_all x1, starting transfers between devices, local(): sums = lax.all_to_all(sums, 'slab', 0, 0, tiled=True)  3.85 us
  transfers between devices with their start and end apart: 8, of which 6 were waited for; matrix products, arithmetic and copies ran while one was open for 0% of the time, Pallas kernels for 8%

profile of v5, /device:TPU:1, one launch (start us, length us, event | category | flops | bytes accessed | tf_op | source)
XLA Modules:
  0.0 102.1 jit_solution(13854398624190019836)
XLA Ops:
  0.6 0.0 copy-start.1
  0.6 5.2 %collective-permute-start.2 = (f32[2,64,128]{2,1,0:T(8,128)}, f32[2,64,128]{2,1,0:T(8,128)S(1)}, u32[]{:S(2)}, u32[]{:S(2)}) collective-permute-start(f32[2,64,128]{2,1,0:T(8,128)} %bitcast.7), channel_id=1, source_target_pairs={{128,0},{416,32},{192,64},{480,96},{256,128},{32,160},{320,192},{9... | collective-permute-start | bytes 196616 | tf_op jit(solution)/shard_map/ppermute | solution.py:375
  5.8 3.6 %collective-permute-done.2 = f32[2,64,128]{2,1,0:T(8,128)S(1)} collective-permute-done((f32[2,64,128]{2,1,0:T(8,128)}, f32[2,64,128]{2,1,0:T(8,128)S(1)}, u32[]{:S(2)}, u32[]{:S(2)}) %collective-permute-start.2) | collective-permute-done | bytes 65568 | tf_op jit(solution)/shard_map/ppermute | solution.py:375
  9.4 0.8 pad_maximum_fusion.2
  10.3 6.9 %collective-permute-start.3 = (f32[4,64,128]{2,1,0:T(8,128)S(1)}, f32[4,64,128]{2,1,0:T(8,128)S(1)}, u32[]{:S(2)}, u32[]{:S(2)}) collective-permute-start(f32[4,64,128]{2,1,0:T(8,128)S(1)} %pad_maximum_fusion.2), channel_id=1, source_target_pairs={{256,0},{288,32},{320,64},{352,96},{384,128},{416,160},{448,192},{... | collective-permute-start | bytes 393224 | tf_op jit(solution)/shard_map/ppermute | solution.py:375
  17.2 2.8 %collective-permute-done.3 = f32[4,64,128]{2,1,0:T(8,128)S(1)} collective-permute-done((f32[4,64,128]{2,1,0:T(8,128)S(1)}, f32[4,64,128]{2,1,0:T(8,128)S(1)}, u32[]{:S(2)}, u32[]{:S(2)}) %collective-permute-start.3) | collective-permute-done | bytes 131104 | tf_op jit(solution)/shard_map/ppermute | solution.py:375
  20.0 0.0 copy-start
  20.0 0.0 copy-start.2
  20.1 0.0 copy-start.3
  20.1 6.0 %collective-permute-start.4 = (f32[8,64,128]{2,1,0:T(8,128)S(1)}, f32[8,64,128]{2,1,0:T(8,128)S(1)}, u32[]{:S(2)}, u32[]{:S(2)}) collective-permute-start(f32[8,64,128]{2,1,0:T(8,128)S(1)} %pad_maximum_fusion.1), channel_id=1, source_target_pairs={{64,0},{480,32},{128,64},{32,96},{192,128},{96,160},{256,192},{160... | collective-permute-start | bytes 786440 | tf_op jit(solution)/shard_map/ppermute | solution.py:375
  26.0 1.1 %pack.1 = (f32[176,256]{1,0:T(8,128)S(1)}, f32[176,256]{1,0:T(8,128)S(1)}) custom-call(f32[2,8,32,256]{3,2,1,0:T(8,128)} %state.3, f32[2,4,16,128]{3,2,1,0:T(8,128)} %theta.3, f32[8,32,256]{2,1,0:T(8,128)} %forcing.3), custom_call_target="tpu_custom_call" | custom-call | tf_op jit(solution)/shard_map/pack/pallas_call | solution.py:57
  27.1 3.1 %collective-permute-start = (f32[176,256]{1,0:T(8,128)S(1)}, f32[176,256]{1,0:T(8,128)S(1)}, u32[]{:S(2)}, u32[]{:S(2)}) collective-permute-start(f32[176,256]{1,0:T(8,128)S(1)} %get-tuple-element.10), channel_id=1, source_target_pairs={{0,1},{1,2},{2,3},{3,4},{4,5},{5,6},{6,7},{7,8},{8,9},{9,10},{10,1... | collective-permute-start | bytes 540680 | tf_op jit(solution)/shard_map/ppermute | solution.py:364
  30.3 1.3 %collective-permute-start.1 = (f32[176,256]{1,0:T(8,128)S(1)}, f32[176,256]{1,0:T(8,128)S(1)}, u32[]{:S(2)}, u32[]{:S(2)}) collective-permute-start(f32[176,256]{1,0:T(8,128)S(1)} %get-tuple-element.11), channel_id=1, source_target_pairs={{1,0},{2,1},{3,2},{4,3},{5,4},{6,5},{7,6},{8,7},{9,8},{10,9},{11,1... | collective-permute-start | bytes 540680 | tf_op jit(solution)/shard_map/ppermute | solution.py:365
  31.6 1.1 %collective-permute-done.low = f32[176,256]{1,0:T(8,128)S(1)} collective-permute-done((f32[176,256]{1,0:T(8,128)S(1)}, f32[176,256]{1,0:T(8,128)S(1)}, u32[]{:S(2)}, u32[]{:S(2)}) %collective-permute-start) | collective-permute-done | bytes 180256 | tf_op jit(solution)/shard_map/ppermute | solution.py:364
  32.7 3.8 %collective-permute-done.1.high = f32[176,256]{1,0:T(8,128)S(1)} collective-permute-done((f32[176,256]{1,0:T(8,128)S(1)}, f32[176,256]{1,0:T(8,128)S(1)}, u32[]{:S(2)}, u32[]{:S(2)}) %collective-permute-start.1) | collective-permute-done | bytes 180256 | tf_op jit(solution)/shard_map/ppermute | solution.py:365
  36.5 6.0 %window.1 = (f32[2,8,32,256]{3,2,1,0:T(8,128)}, f32[32,8,128]{2,1,0:T(8,128)}, f32[8,128]{1,0:T(8,128)S(1)}, f32[8,512]{1,0:T(8,128)S(1)}) custom-call(s32[1]{0:T(128)} %bitcast.slab, f32[2,8,32,256]{3,2,1,0:T(8,128)S(1)} %copy-done, f32[2,4,16,128]{3,2,1,0:T(8,128)S(1)} %copy-done.2, f32[8,32,256]{2,1,0:T(8,128)S(1)} %copy-done.3, ...), custom_call_target="tpu_custom_call" | custom-call | tf_op jit(solution)/shard_map/window/pallas_call | solution.py:202
  42.5 14.9 %all-to-all-start = ((f32[32,8,128]{2,1,0:T(8,128)}), f32[32,8,128]{2,1,0:T(8,128)S(1)}, u32[]{:S(2)}, u32[]{:S(2)}) async-start(f32[32,8,128]{2,1,0:T(8,128)} %get-tuple-element.13), calls=%async_computation | async-start | bytes 262144 | tf_op jit(solution)/shard_map/all_to_all | solution.py:382
  57.5 7.2 %collective-permute-start.5 = (f32[16,64,128]{2,1,0:T(8,128)S(1)}, f32[16,64,128]{2,1,0:T(8,128)S(1)}, u32[]{:S(2)}, u32[]{:S(2)}) collective-permute-start(f32[16,64,128]{2,1,0:T(8,128)S(1)} %pad_maximum_fusion.here), channel_id=1, source_target_pairs={{0,32},{32,0},{64,96},{96,64},{128,160},{160,128},{192,224},{224,1... | collective-permute-start | bytes 1572872 | tf_op jit(solution)/shard_map/ppermute | solution.py:392
  64.6 2.1 %all-to-all-done.arrived = f32[32,8,128]{2,1,0:T(8,128)S(1)} async-done(((f32[32,8,128]{2,1,0:T(8,128)}), f32[32,8,128]{2,1,0:T(8,128)S(1)}, u32[]{:S(2)}, u32[]{:S(2)}) %all-to-all-start) | async-done | bytes 131104 | tf_op jit(solution)/shard_map/all_to_all | solution.py:382
  66.8 18.7 %all_to_all.15 = f32[16,8,128]{2,1,0:T(8,128)S(1)} all-to-all(f32[16,8,128]{2,1,0:T(8,128)S(1)} %get-tuple-element.15), channel_id=1, replica_groups=mesh['group'=16,'slab'=32] {'group'}, dimensions={0} | all-to-all | bytes 131072 | tf_op jit(solution)/shard_map/all_to_all | solution.py:386
  85.5 1.0 moments.1
  86.6 3.9 %all-to-all-start.2 = ((f32[32,8,128]{2,1,0:T(8,128)}), f32[32,8,128]{2,1,0:T(8,128)S(1)}, u32[]{:S(2)}, u32[]{:S(2)}) async-start(f32[32,8,128]{2,1,0:T(8,128)} %moments.1), calls=%async_computation.2 | async-start | bytes 262144 | tf_op jit(solution)/shard_map/all_to_all | solution.py:390
  90.4 9.8 %all-to-all-done.2.arrived = f32[32,8,128]{2,1,0:T(8,128)S(1)} async-done(((f32[32,8,128]{2,1,0:T(8,128)}), f32[32,8,128]{2,1,0:T(8,128)S(1)}, u32[]{:S(2)}, u32[]{:S(2)}) %all-to-all-start.2) | async-done | bytes 131104 | tf_op jit(solution)/shard_map/all_to_all | solution.py:390
  100.3 1.8 %update.1 = f32[2,64,128]{2,1,0:T(8,128)} custom-call(s32[1]{0:T(128)} %bitcast.3.group, f32[32,8,128]{2,1,0:T(8,128)S(1)} %all-to-all-done.2.arrived, f32[16,64,128]{2,1,0:T(8,128)S(1)} %pad_maximum_fusion.here, f32[16,64,128]{2,1,0:T(8,128)S(1)} %collective-permute-done.5.there), custom_call_target="tpu_custom_call" | custom-call | tf_op jit(solution)/shard_map/update/pallas_call | solution.py:350
  (9 shorter events, 0.1 us)
Async XLA Ops:
  0.6 19.4 %copy-start.1 = (f32[2,4,16,128]{3,2,1,0:T(8,128)S(1)}, f32[2,4,16,128]{3,2,1,0:T(8,128)}, u32[]{:S(2)}) copy-start(f32[2,4,16,128]{3,2,1,0:T(8,128)} %theta.3) | copy-start | bytes 196612
  0.6 8.8 %collective-permute-start.2 = (f32[2,64,128]{2,1,0:T(8,128)}, f32[2,64,128]{2,1,0:T(8,128)S(1)}, u32[]{:S(2)}, u32[]{:S(2)}) collective-permute-start(f32[2,64,128]{2,1,0:T(8,128)} %bitcast.7), channel_id=1, source_target_pairs={{128,0},{416,32},{192,64},{480,96},{256,128},{32,160},{320,192},{9... | collective-permute-start | bytes 196616 | tf_op jit(solution)/shard_map/ppermute | solution.py:375
  10.3 9.7 %collective-permute-start.3 = (f32[4,64,128]{2,1,0:T(8,128)S(1)}, f32[4,64,128]{2,1,0:T(8,128)S(1)}, u32[]{:S(2)}, u32[]{:S(2)}) collective-permute-start(f32[4,64,128]{2,1,0:T(8,128)S(1)} %pad_maximum_fusion.2), channel_id=1, source_target_pairs={{256,0},{288,32},{320,64},{352,96},{384,128},{416,160},{448,192},{... | collective-permute-start | bytes 393224 | tf_op jit(solution)/shard_map/ppermute | solution.py:375
  20.0 16.5 %copy-start = (f32[2,8,32,256]{3,2,1,0:T(8,128)S(1)}, f32[2,8,32,256]{3,2,1,0:T(8,128)}, u32[]{:S(2)}) copy-start(f32[2,8,32,256]{3,2,1,0:T(8,128)} %state.3) | copy-start | bytes 1572868
  20.0 16.4 %copy-start.2 = (f32[2,4,16,128]{3,2,1,0:T(8,128)S(1)}, f32[2,4,16,128]{3,2,1,0:T(8,128)}, u32[]{:S(2)}) copy-start(f32[2,4,16,128]{3,2,1,0:T(8,128)} %theta.3) | copy-start | bytes 196612
  20.1 16.4 %copy-start.3 = (f32[8,32,256]{2,1,0:T(8,128)S(1)}, f32[8,32,256]{2,1,0:T(8,128)}, u32[]{:S(2)}) copy-start(f32[8,32,256]{2,1,0:T(8,128)} %forcing.3) | copy-start | bytes 786436
  20.1 37.3 %collective-permute-start.4 = (f32[8,64,128]{2,1,0:T(8,128)S(1)}, f32[8,64,128]{2,1,0:T(8,128)S(1)}, u32[]{:S(2)}, u32[]{:S(2)}) collective-permute-start(f32[8,64,128]{2,1,0:T(8,128)S(1)} %pad_maximum_fusion.1), channel_id=1, source_target_pairs={{64,0},{480,32},{128,64},{32,96},{192,128},{96,160},{256,192},{160... | collective-permute-start | bytes 786440 | tf_op jit(solution)/shard_map/ppermute | solution.py:375
  27.1 5.5 %collective-permute-start = (f32[176,256]{1,0:T(8,128)S(1)}, f32[176,256]{1,0:T(8,128)S(1)}, u32[]{:S(2)}, u32[]{:S(2)}) collective-permute-start(f32[176,256]{1,0:T(8,128)S(1)} %get-tuple-element.10), channel_id=1, source_target_pairs={{0,1},{1,2},{2,3},{3,4},{4,5},{5,6},{6,7},{7,8},{8,9},{9,10},{10,1... | collective-permute-start | bytes 540680 | tf_op jit(solution)/shard_map/ppermute | solution.py:364
  30.3 6.2 %collective-permute-start.1 = (f32[176,256]{1,0:T(8,128)S(1)}, f32[176,256]{1,0:T(8,128)S(1)}, u32[]{:S(2)}, u32[]{:S(2)}) collective-permute-start(f32[176,256]{1,0:T(8,128)S(1)} %get-tuple-element.11), channel_id=1, source_target_pairs={{1,0},{2,1},{3,2},{4,3},{5,4},{6,5},{7,6},{8,7},{9,8},{10,9},{11,1... | collective-permute-start | bytes 540680 | tf_op jit(solution)/shard_map/ppermute | solution.py:365
  42.5 24.2 %all-to-all-start = ((f32[32,8,128]{2,1,0:T(8,128)}), f32[32,8,128]{2,1,0:T(8,128)S(1)}, u32[]{:S(2)}, u32[]{:S(2)}) async-start(f32[32,8,128]{2,1,0:T(8,128)} %get-tuple-element.13), calls=%async_computation | async-start | bytes 262144 | tf_op jit(solution)/shard_map/all_to_all | solution.py:382
  57.5 42.8 %collective-permute-start.5 = (f32[16,64,128]{2,1,0:T(8,128)S(1)}, f32[16,64,128]{2,1,0:T(8,128)S(1)}, u32[]{:S(2)}, u32[]{:S(2)}) collective-permute-start(f32[16,64,128]{2,1,0:T(8,128)S(1)} %pad_maximum_fusion.here), channel_id=1, source_target_pairs={{0,32},{32,0},{64,96},{96,64},{128,160},{160,128},{192,224},{224,1... | collective-permute-start | bytes 1572872 | tf_op jit(solution)/shard_map/ppermute | solution.py:392
  86.6 13.7 %all-to-all-start.2 = ((f32[32,8,128]{2,1,0:T(8,128)}), f32[32,8,128]{2,1,0:T(8,128)S(1)}, u32[]{:S(2)}, u32[]{:S(2)}) async-start(f32[32,8,128]{2,1,0:T(8,128)} %moments.1), calls=%async_computation.2 | async-start | bytes 262144 | tf_op jit(solution)/shard_map/all_to_all | solution.py:390

commit v6 on v5

--- a/solution.py
+++ b/solution.py
@@ -19,6 +19,7 @@
 GROUPS = 16
 MEMBERS = 32
 BLOCK = 512
+OBS = SLABS * BLOCK
 MIB = 1 << 20
 PARTS = (0, 2, 4, 6, 1, 3, 5, 7)
 HALO_ROWS = 176
@@ -65,18 +66,91 @@
     )(*(pltpu.with_memory_space_constraint(a, pltpu.HBM) for a in (state, theta, forcing)))
 
 
-def window_kernel(
-    slab, state, theta, forcing, low, high, observed, noise, perturb, footprints,
-    final, part, count, given, diff, mid, fresh, done, boxes, target, spread, draws, sems,
+def masks_kernel(
+    slab, observed, noise, perturb, footprints, state, theta, forcing,
+    in_x, in_z, in_y, count, given, state_here, theta_here, forcing_here,
+    boxes, target, spread, draws, sems,
 ):
+    quarter = OBS // 4
+    chunks = [pl.ds(i * quarter, quarter) for i in range(4)]
     enter = [
-        pltpu.make_async_copy(src, dst, sems.at[i])
+        pltpu.make_async_copy(footprints.at[:, c], boxes.at[:, c], sems.at[i])
+        for i, c in enumerate(chunks)
+    ]
+    small = [
+        pltpu.make_async_copy(src, dst, sems.at[4 + i])
         for i, (src, dst) in enumerate(
-            ((footprints, boxes), (observed, target), (noise, spread), (perturb, draws))
+            (
+                (observed, target),
+                (noise, spread),
+                (perturb, draws),
+                (state, state_here),
+                (theta, theta_here),
+                (forcing, forcing_here),
+            )
         )
     ]
-    for e in enter:
+    for e in enter + small:
         e.start()
+    first = slab[0] * PLANES
+    iota_x = lax.broadcasted_iota(jnp.int32, (64, BLOCK), 0)
+    iota = lax.broadcasted_iota(jnp.int32, (8, BLOCK), 0)
+    for i, e in enumerate(enter):
+        e.wait()
+
+        def build(d, carry):
+            at = pl.ds(pl.multiple_of(i * quarter + d * BLOCK, BLOCK), BLOCK)
+            b = boxes[:, at]
+            in_x[:, at] = ((iota_x >= b[4:5]) & (iota_x < b[5:6])).astype(F32).astype(BF16)
+            in_z[:, at] = ((iota + first >= b[0:1]) & (iota + first < b[1:2])).astype(F32)
+            in_y[:, at] = ((iota >= b[2:3]) & (iota < b[3:4])).astype(F32)
+            return carry
+
+        lax.fori_loop(0, quarter // BLOCK, build, 0, unroll=8)
+    b = boxes[:, pl.ds(pl.multiple_of(slab[0] * BLOCK, BLOCK), BLOCK)]
+    cells = ((b[1:2] - b[0:1]) * (b[3:4] - b[2:3]) * (b[5:6] - b[4:5]) * 16).astype(F32)
+    for m in range(LOCAL):
+        for q in range(4):
+            count[m * 4 + q : m * 4 + q + 1, :] = cells[:, q * 128 : (q + 1) * 128]
+    for e in small:
+        e.wait()
+    var = spread[...]
+    given[0:LOCAL, :] = target[...] + jnp.sqrt(var) * draws[...]
+    given[LOCAL : LOCAL + 1, :] = var
+    given[LOCAL + 1 : 8, :] = jnp.zeros((5, BLOCK), F32)
+
+
+def masks(slab, *kept):
+    vmem = pl.BlockSpec(memory_space=pltpu.VMEM)
+    return pl.pallas_call(
+        masks_kernel,
+        out_shape=(
+            jax.ShapeDtypeStruct((64, OBS), BF16),
+            jax.ShapeDtypeStruct((8, OBS), F32),
+            jax.ShapeDtypeStruct((8, OBS), F32),
+            jax.ShapeDtypeStruct((8, 128), F32),
+            jax.ShapeDtypeStruct((8, BLOCK), F32),
+            *(jax.ShapeDtypeStruct(a.shape, F32) for a in kept[-3:]),
+        ),
+        in_specs=[pl.BlockSpec(memory_space=pltpu.SMEM)]
+        + [pl.BlockSpec(memory_space=pltpu.HBM)] * 7,
+        out_specs=(vmem,) * 8,
+        compiler_params=pltpu.CompilerParams(vmem_limit_bytes=8 * MIB),
+        scratch_shapes=[
+            pltpu.VMEM((6, OBS), jnp.int32),
+            pltpu.VMEM((1, BLOCK), F32),
+            pltpu.VMEM((1, BLOCK), F32),
+            pltpu.VMEM((LOCAL, BLOCK), F32),
+            pltpu.SemaphoreType.DMA((10,)),
+        ],
+        name="masks",
+    )(slab, *(pltpu.with_memory_space_constraint(a, pltpu.HBM) for a in kept))
+
+
+def window_kernel(
+    slab, state, theta, forcing, low, high, in_x, in_z, in_y,
+    final, part, diff, mid, fresh, done, sem,
+):
     s = slab[0]
     keep_low = jnp.where(s > 0, 0.5, 0.0).astype(F32)
     keep_high = jnp.where(s < SLABS - 1, 0.5, 0.0).astype(F32)
@@ -142,7 +216,7 @@
             for h in range(2):
                 done[h, to : to + ROWS, :] = new[:, h * 128 : (h + 1) * 128]
 
-    leave = pltpu.make_async_copy(fresh, final, sems.at[4])
+    leave = pltpu.make_async_copy(fresh, final, sem)
     leave.start()
 
     tall = LOCAL * PLANES * 8
@@ -158,76 +232,47 @@
     lane = lax.broadcasted_iota(jnp.int32, (tall, 128), 1)
     left = jnp.where(lane < 64, top, tiles - top).astype(BF16)
 
-    for e in enter:
-        e.wait()
-    iota_x = lax.broadcasted_iota(jnp.int32, (64, BLOCK), 0)
-    iota_y = lax.broadcasted_iota(jnp.int32, (8, BLOCK), 0)
-
     def observe(d, carry):
-        here = pl.ds(pl.multiple_of(d * BLOCK, BLOCK), BLOCK)
-        b = boxes[:, here]
-        in_x = ((iota_x >= b[4:5]) & (iota_x < b[5:6])).astype(F32).astype(BF16)
-        along = jnp.dot(left, jnp.concatenate([in_x, in_x], axis=0), preferred_element_type=F32)
-        z0 = jnp.broadcast_to(b[0:1], (8, BLOCK)) - s * PLANES
-        z1 = jnp.broadcast_to(b[1:2], (8, BLOCK)) - s * PLANES
-        in_y = (iota_y >= b[2:3]) & (iota_y < b[3:4])
+        at = pl.ds(pl.multiple_of(d * BLOCK, BLOCK), BLOCK)
+        wide_x = in_x[:, at]
+        along = jnp.dot(left, jnp.concatenate([wide_x, wide_x], axis=0), preferred_element_type=F32)
         sums = [jnp.zeros((8, BLOCK), F32) for _ in range(LOCAL)]
         for z in range(PLANES):
-            in_z = (z0 <= z) & (z1 > z)
+            plane_z = jnp.broadcast_to(in_z[z : z + 1, at], (8, BLOCK))
             for m in range(LOCAL):
-                at = (m * PLANES + z) * 8
-                sums[m] = sums[m] + jnp.where(in_z, along[at : at + 8], 0.0)
+                row0 = (m * PLANES + z) * 8
+                sums[m] = sums[m] + plane_z * along[row0 : row0 + 8]
+        rows_y = in_y[:, at]
         for m in range(LOCAL):
-            total = jnp.sum(jnp.where(in_y, sums[m], 0.0), axis=0, keepdims=True)
+            total = jnp.sum(rows_y * sums[m], axis=0, keepdims=True)
             for q in range(4):
                 part[d, m * 4 + q : m * 4 + q + 1, :] = total[:, q * 128 : (q + 1) * 128]
         return carry
 
-    lax.fori_loop(0, SLABS, observe, 0, unroll=4)
-
-    b = boxes[:, pl.ds(pl.multiple_of(s * BLOCK, BLOCK), BLOCK)]
-    cells = ((b[1:2] - b[0:1]) * (b[3:4] - b[2:3]) * (b[5:6] - b[4:5]) * 16).astype(F32)
-    for m in range(LOCAL):
-        for q in range(4):
-            count[m * 4 + q : m * 4 + q + 1, :] = cells[:, q * 128 : (q + 1) * 128]
-    var = spread[...]
-    given[0:LOCAL, :] = target[...] + jnp.sqrt(var) * draws[...]
-    given[LOCAL : LOCAL + 1, :] = var
-    given[LOCAL + 1 : 8, :] = jnp.zeros((5, BLOCK), F32)
+    lax.fori_loop(0, SLABS, observe, 0, unroll=8)
     leave.wait()
 
 
-def window(slab, state, theta, forcing, low, high, *kept):
+def window(slab, *given):
     vmem = pl.BlockSpec(memory_space=pltpu.VMEM)
     return pl.pallas_call(
         window_kernel,
         out_shape=(
-            jax.ShapeDtypeStruct(state.shape, F32),
+            jax.ShapeDtypeStruct(given[0].shape, F32),
             jax.ShapeDtypeStruct((SLABS, 8, 128), F32),
-            jax.ShapeDtypeStruct((8, 128), F32),
-            jax.ShapeDtypeStruct((8, BLOCK), F32),
         ),
-        in_specs=[pl.BlockSpec(memory_space=pltpu.SMEM)]
-        + [vmem] * 5
-        + [pl.BlockSpec(memory_space=pltpu.HBM)] * 4,
-        out_specs=(pl.BlockSpec(memory_space=pltpu.HBM), vmem, vmem, vmem),
+        in_specs=[pl.BlockSpec(memory_space=pltpu.SMEM)] + [vmem] * 8,
+        out_specs=(pl.BlockSpec(memory_space=pltpu.HBM), vmem),
         compiler_params=pltpu.CompilerParams(vmem_limit_bytes=12 * MIB),
         scratch_shapes=[
             pltpu.VMEM((2, LOCAL * (COARSE + 2) * ROWS, 128), F32),
             pltpu.VMEM((LOCAL * (PLANES + 2), ROWS, COLS), F32),
             pltpu.VMEM((LOCAL, PLANES, ROWS, COLS), F32),
             pltpu.VMEM((2, LOCAL * PLANES * ROWS, 128), F32),
-            pltpu.VMEM(kept[-1].shape, jnp.int32),
-            pltpu.VMEM((1, BLOCK), F32),
-            pltpu.VMEM((1, BLOCK), F32),
-            pltpu.VMEM((LOCAL, BLOCK), F32),
-            pltpu.SemaphoreType.DMA((5,)),
+            pltpu.SemaphoreType.DMA,
         ],
         name="window",
-    )(
-        slab, state, theta, forcing, low, high,
-        *(pltpu.with_memory_space_constraint(a, pltpu.HBM) for a in kept),
-    )
+    )(slab, *given)
 
 
 def gather_kernel(arrived, count, copies, own):
@@ -375,12 +420,13 @@
         return lax.ppermute(value, "group", moves)
 
     pair = from_chip(field, 2)
-    final, part, count, given = window(
-        slab, state, theta, forcing, low, high,
-        observed.reshape(1, BLOCK), noise_var.reshape(1, BLOCK), perturb, boxes,
-    )
+    in_x, in_z, in_y, count, given, *fields = masks(
+        slab, observed.reshape(1, BLOCK), noise_var.reshape(1, BLOCK), perturb, boxes,
+        state, theta, forcing,
+    )
+    final, part = window(slab, *fields, low, high, in_x, in_z, in_y)
     arrived = lax.all_to_all(part, "slab", 0, 0, tiled=True)
-    pair = jnp.concatenate([field, pair], axis=0)
+    pair = jnp.concatenate([fields[1].reshape(field.shape), pair], axis=0)
     across = from_chip(pair, 4)
     copies, own = own_predictions(arrived, count)
     preds = lax.all_to_all(copies, "group", 0, 0, tiled=True).reshape(GROUPS * 8, 128)

time: 103 us -> 99.2 us (0.963)
  waiting for transfers between devices: 23.3 us -> 21.5 us
    ppermute x3, waiting for transfers between devices: 6.4 us -> 4.61 us  [from_chip(): return lax.ppermute(value, 'group', moves)]
    pallas_call x1 -> x2, Pallas kernels: 6 us -> 5.53 us  [the longest x1 3.76 us: window(): pl.pallas_call(window_kernel, out_shape=(jax.ShapeDtypeStruct(given[0].sh...]
where the time goes in v6:
time: 99.2 us; the launch traced here: 98.6 us
  starting transfers between devices  48.1 us (48%)
  waiting for transfers between devices  21.5 us (22%)
  blocking collectives  18.7 us (19%)
  Pallas kernels  9.46 us (10%)
    all_to_all x1, blocking collectives, local(): lax.all_to_all(copies, 'group', 0, 0, tiled=True).reshape(GROUPS * 8, 128)  18.7 us
    ppermute x3, starting transfers between devices, from_chip(): return lax.ppermute(value, 'group', moves)  17.8 us
    all_to_all x1, starting transfers between devices, local(): arrived = lax.all_to_all(part, 'slab', 0, 0, tiled=True)  14.9 us
    all_to_all x1, waiting for transfers between devices, local(): sums = lax.all_to_all(sums, 'slab', 0, 0, tiled=True)  9.84 us
    ppermute x1, starting transfers between devices, local(): there = lax.ppermute(here, 'group', [(i, i ^ 1) for i in range(GROUPS)])  7.15 us
    ppermute x3, waiting for transfers between devices, from_chip(): return lax.ppermute(value, 'group', moves)  4.61 us
    all_to_all x1, starting transfers between devices, local(): sums = lax.all_to_all(sums, 'slab', 0, 0, tiled=True)  3.84 us
    ppermute x1, waiting for transfers between devices, local(): high = lax.ppermute(first, 'slab', [(i + 1, i) for i in range(SLABS - 1)])  3.83 us
  transfers between devices with their start and end apart: 8, of which 6 were waited for; matrix products, arithmetic and copies ran while one was open for 0% of the time, Pallas kernels for 8%

profile of v6, /device:TPU:1, one launch (start us, length us, event | category | flops | bytes accessed | tf_op | source)
XLA Modules:
  0.0 98.6 jit_solution(10763302188925339283)
XLA Ops:
  0.6 5.0 %collective-permute-start.2 = (f32[2,64,128]{2,1,0:T(8,128)}, f32[2,64,128]{2,1,0:T(8,128)S(1)}, u32[]{:S(2)}, u32[]{:S(2)}) collective-permute-start(f32[2,64,128]{2,1,0:T(8,128)} %bitcast.12), channel_id=1, source_target_pairs={{128,0},{416,32},{192,64},{480,96},{256,128},{32,160},{320,192},{9... | collective-permute-start | bytes 196616 | tf_op jit(solution)/shard_map/ppermute | solution.py:420
  5.7 1.8 %masks.1 = (bf16[64,16384]{1,0:T(8,128)(2,1)S(1)}, f32[8,16384]{1,0:T(8,128)S(1)}, f32[8,16384]{1,0:T(8,128)S(1)}, f32[8,128]{1,0:T(8,128)S(1)}, f32[8,512]{1,0:...) custom-call(s32[1]{0:T(128)} %bitcast.slab, ...), custom_call_target="tpu_custom_call" | custom-call | tf_op jit(solution)/shard_map/masks/pallas_call | solution.py:125
  7.5 1.8 %collective-permute-done.2 = f32[2,64,128]{2,1,0:T(8,128)S(1)} collective-permute-done((f32[2,64,128]{2,1,0:T(8,128)}, f32[2,64,128]{2,1,0:T(8,128)S(1)}, u32[]{:S(2)}, u32[]{:S(2)}) %collective-permute-start.2) | collective-permute-done | bytes 65568 | tf_op jit(solution)/shard_map/ppermute | solution.py:420
  9.3 6.9 %collective-permute-start.3 = (f32[4,64,128]{2,1,0:T(8,128)S(1)}, f32[4,64,128]{2,1,0:T(8,128)S(1)}, u32[]{:S(2)}, u32[]{:S(2)}) collective-permute-start(f32[4,64,128]{2,1,0:T(8,128)S(1)} %pad_maximum_fusion.2), channel_id=1, source_target_pairs={{256,0},{288,32},{320,64},{352,96},{384,128},{416,160},{448,192},{... | collective-permute-start | bytes 393224 | tf_op jit(solution)/shard_map/ppermute | solution.py:420
  16.3 2.8 %collective-permute-done.3 = f32[4,64,128]{2,1,0:T(8,128)S(1)} collective-permute-done((f32[4,64,128]{2,1,0:T(8,128)S(1)}, f32[4,64,128]{2,1,0:T(8,128)S(1)}, u32[]{:S(2)}, u32[]{:S(2)}) %collective-permute-start.3) | collective-permute-done | bytes 131104 | tf_op jit(solution)/shard_map/ppermute | solution.py:420
  19.1 5.8 %collective-permute-start.4 = (f32[8,64,128]{2,1,0:T(8,128)S(1)}, f32[8,64,128]{2,1,0:T(8,128)S(1)}, u32[]{:S(2)}, u32[]{:S(2)}) collective-permute-start(f32[8,64,128]{2,1,0:T(8,128)S(1)} %pad_maximum_fusion.1), channel_id=1, source_target_pairs={{64,0},{480,32},{128,64},{32,96},{192,128},{96,160},{256,192},{160... | collective-permute-start | bytes 786440 | tf_op jit(solution)/shard_map/ppermute | solution.py:420
  24.9 1.1 %pack.1 = (f32[176,256]{1,0:T(8,128)S(1)}, f32[176,256]{1,0:T(8,128)S(1)}) custom-call(f32[2,8,32,256]{3,2,1,0:T(8,128)} %state.3, f32[2,4,16,128]{3,2,1,0:T(8,128)} %theta.3, f32[8,32,256]{2,1,0:T(8,128)} %forcing.3), custom_call_target="tpu_custom_call" | custom-call | tf_op jit(solution)/shard_map/pack/pallas_call | solution.py:58
  26.0 3.1 %collective-permute-start = (f32[176,256]{1,0:T(8,128)S(1)}, f32[176,256]{1,0:T(8,128)S(1)}, u32[]{:S(2)}, u32[]{:S(2)}) collective-permute-start(f32[176,256]{1,0:T(8,128)S(1)} %get-tuple-element.19), channel_id=1, source_target_pairs={{0,1},{1,2},{2,3},{3,4},{4,5},{5,6},{6,7},{7,8},{8,9},{9,10},{10,1... | collective-permute-start | bytes 540680 | tf_op jit(solution)/shard_map/ppermute | solution.py:409
  29.1 1.3 %collective-permute-start.1 = (f32[176,256]{1,0:T(8,128)S(1)}, f32[176,256]{1,0:T(8,128)S(1)}, u32[]{:S(2)}, u32[]{:S(2)}) collective-permute-start(f32[176,256]{1,0:T(8,128)S(1)} %get-tuple-element.20), channel_id=1, source_target_pairs={{1,0},{2,1},{3,2},{4,3},{5,4},{6,5},{7,6},{8,7},{9,8},{10,9},{11,1... | collective-permute-start | bytes 540680 | tf_op jit(solution)/shard_map/ppermute | solution.py:410
  30.4 1.1 %collective-permute-done.low = f32[176,256]{1,0:T(8,128)S(1)} collective-permute-done((f32[176,256]{1,0:T(8,128)S(1)}, f32[176,256]{1,0:T(8,128)S(1)}, u32[]{:S(2)}, u32[]{:S(2)}) %collective-permute-start) | collective-permute-done | bytes 180256 | tf_op jit(solution)/shard_map/ppermute | solution.py:409
  31.5 3.8 %collective-permute-done.1.high = f32[176,256]{1,0:T(8,128)S(1)} collective-permute-done((f32[176,256]{1,0:T(8,128)S(1)}, f32[176,256]{1,0:T(8,128)S(1)}, u32[]{:S(2)}, u32[]{:S(2)}) %collective-permute-start.1) | collective-permute-done | bytes 180256 | tf_op jit(solution)/shard_map/ppermute | solution.py:410
  35.3 3.8 %window.1 = (f32[2,8,32,256]{3,2,1,0:T(8,128)}, f32[32,8,128]{2,1,0:T(8,128)}) custom-call(s32[1]{0:T(128)} %bitcast.slab, f32[2,8,32,256]{3,2,1,0:T(8,128)S(1)} %get-tuple-element.16.state, f32[2,4,16,128]{3,2,1,0:T(8,128)S(1)} %get-tuple-element.17.theta, f32[8,32,256]{2,1,0:T(8,128)S(1)} %get-tuple-element.18.forcing, ...), custom_call_target="tpu_custom_call" | custom-call | tf_op jit(solution)/shard_map/window/pallas_call | solution.py:258
  39.1 14.9 %all-to-all-start = ((f32[32,8,128]{2,1,0:T(8,128)}), f32[32,8,128]{2,1,0:T(8,128)S(1)}, u32[]{:S(2)}, u32[]{:S(2)}) async-start(f32[32,8,128]{2,1,0:T(8,128)} %get-tuple-element.25), calls=%async_computation | async-start | bytes 262144 | tf_op jit(solution)/shard_map/all_to_all | solution.py:428
  54.0 0.0 collective-permute-done.4
  54.1 7.1 %collective-permute-start.5 = (f32[16,64,128]{2,1,0:T(8,128)S(1)}, f32[16,64,128]{2,1,0:T(8,128)S(1)}, u32[]{:S(2)}, u32[]{:S(2)}) collective-permute-start(f32[16,64,128]{2,1,0:T(8,128)S(1)} %pad_maximum_fusion.here), channel_id=1, source_target_pairs={{0,32},{32,0},{64,96},{96,64},{128,160},{160,128},{192,224},{224,1... | collective-permute-start | bytes 1572872 | tf_op jit(solution)/shard_map/ppermute | solution.py:438
  61.2 2.1 %all-to-all-done.arrived = f32[32,8,128]{2,1,0:T(8,128)S(1)} async-done(((f32[32,8,128]{2,1,0:T(8,128)}), f32[32,8,128]{2,1,0:T(8,128)S(1)}, u32[]{:S(2)}, u32[]{:S(2)}) %all-to-all-start) | async-done | bytes 131104 | tf_op jit(solution)/shard_map/all_to_all | solution.py:428
  63.4 18.7 %all_to_all.15 = f32[16,8,128]{2,1,0:T(8,128)S(1)} all-to-all(f32[16,8,128]{2,1,0:T(8,128)S(1)} %get-tuple-element.27), channel_id=1, replica_groups=mesh['group'=16,'slab'=32] {'group'}, dimensions={0} | all-to-all | bytes 131072 | tf_op jit(solution)/shard_map/all_to_all | solution.py:432
  82.1 1.0 %moments.1 = f32[32,8,128]{2,1,0:T(8,128)} custom-call(f32[128,128]{1,0:T(8,128)S(1)} %bitcast.11, f32[8,128]{1,0:T(8,128)S(1)} %get-tuple-element.28.own, f32[8,512]{1,0:T(8,128)S(1)} %get-tuple-element.29.given), custom_call_target="tpu_custom_call" | custom-call | tf_op jit(solution)/shard_map/moments/pallas_call | solution.py:328
  83.1 3.8 %all-to-all-start.2 = ((f32[32,8,128]{2,1,0:T(8,128)}), f32[32,8,128]{2,1,0:T(8,128)S(1)}, u32[]{:S(2)}, u32[]{:S(2)}) async-start(f32[32,8,128]{2,1,0:T(8,128)} %moments.1), calls=%async_computation.2 | async-start | bytes 262144 | tf_op jit(solution)/shard_map/all_to_all | solution.py:436
  87.0 9.8 %all-to-all-done.2.arrived = f32[32,8,128]{2,1,0:T(8,128)S(1)} async-done(((f32[32,8,128]{2,1,0:T(8,128)}), f32[32,8,128]{2,1,0:T(8,128)S(1)}, u32[]{:S(2)}, u32[]{:S(2)}) %all-to-all-start.2) | async-done | bytes 131104 | tf_op jit(solution)/shard_map/all_to_all | solution.py:436
  96.8 0.0 collective-permute-done.5.there
  96.8 1.8 %update.1 = f32[2,64,128]{2,1,0:T(8,128)} custom-call(s32[1]{0:T(128)} %bitcast.3.group, f32[32,8,128]{2,1,0:T(8,128)S(1)} %all-to-all-done.2.arrived, f32[16,64,128]{2,1,0:T(8,128)S(1)} %pad_maximum_fusion.here, f32[16,64,128]{2,1,0:T(8,128)S(1)} %collective-permute-done.5.there), custom_call_target="tpu_custom_call" | custom-call | tf_op jit(solution)/shard_map/update/pallas_call | solution.py:395
  (4 shorter events, 0.1 us)
Async XLA Ops:
  0.6 8.7 %collective-permute-start.2 = (f32[2,64,128]{2,1,0:T(8,128)}, f32[2,64,128]{2,1,0:T(8,128)S(1)}, u32[]{:S(2)}, u32[]{:S(2)}) collective-permute-start(f32[2,64,128]{2,1,0:T(8,128)} %bitcast.12), channel_id=1, source_target_pairs={{128,0},{416,32},{192,64},{480,96},{256,128},{32,160},{320,192},{9... | collective-permute-start | bytes 196616 | tf_op jit(solution)/shard_map/ppermute | solution.py:420
  9.3 9.7 %collective-permute-start.3 = (f32[4,64,128]{2,1,0:T(8,128)S(1)}, f32[4,64,128]{2,1,0:T(8,128)S(1)}, u32[]{:S(2)}, u32[]{:S(2)}) collective-permute-start(f32[4,64,128]{2,1,0:T(8,128)S(1)} %pad_maximum_fusion.2), channel_id=1, source_target_pairs={{256,0},{288,32},{320,64},{352,96},{384,128},{416,160},{448,192},{... | collective-permute-start | bytes 393224 | tf_op jit(solution)/shard_map/ppermute | solution.py:420
  19.1 35.0 %collective-permute-start.4 = (f32[8,64,128]{2,1,0:T(8,128)S(1)}, f32[8,64,128]{2,1,0:T(8,128)S(1)}, u32[]{:S(2)}, u32[]{:S(2)}) collective-permute-start(f32[8,64,128]{2,1,0:T(8,128)S(1)} %pad_maximum_fusion.1), channel_id=1, source_target_pairs={{64,0},{480,32},{128,64},{32,96},{192,128},{96,160},{256,192},{160... | collective-permute-start | bytes 786440 | tf_op jit(solution)/shard_map/ppermute | solution.py:420
  26.0 5.5 %collective-permute-start = (f32[176,256]{1,0:T(8,128)S(1)}, f32[176,256]{1,0:T(8,128)S(1)}, u32[]{:S(2)}, u32[]{:S(2)}) collective-permute-start(f32[176,256]{1,0:T(8,128)S(1)} %get-tuple-element.19), channel_id=1, source_target_pairs={{0,1},{1,2},{2,3},{3,4},{4,5},{5,6},{6,7},{7,8},{8,9},{9,10},{10,1... | collective-permute-start | bytes 540680 | tf_op jit(solution)/shard_map/ppermute | solution.py:409
  29.1 6.2 %collective-permute-start.1 = (f32[176,256]{1,0:T(8,128)S(1)}, f32[176,256]{1,0:T(8,128)S(1)}, u32[]{:S(2)}, u32[]{:S(2)}) collective-permute-start(f32[176,256]{1,0:T(8,128)S(1)} %get-tuple-element.20), channel_id=1, source_target_pairs={{1,0},{2,1},{3,2},{4,3},{5,4},{6,5},{7,6},{8,7},{9,8},{10,9},{11,1... | collective-permute-start | bytes 540680 | tf_op jit(solution)/shard_map/ppermute | solution.py:410
  39.1 24.3 %all-to-all-start = ((f32[32,8,128]{2,1,0:T(8,128)}), f32[32,8,128]{2,1,0:T(8,128)S(1)}, u32[]{:S(2)}, u32[]{:S(2)}) async-start(f32[32,8,128]{2,1,0:T(8,128)} %get-tuple-element.25), calls=%async_computation | async-start | bytes 262144 | tf_op jit(solution)/shard_map/all_to_all | solution.py:428
  54.1 42.8 %collective-permute-start.5 = (f32[16,64,128]{2,1,0:T(8,128)S(1)}, f32[16,64,128]{2,1,0:T(8,128)S(1)}, u32[]{:S(2)}, u32[]{:S(2)}) collective-permute-start(f32[16,64,128]{2,1,0:T(8,128)S(1)} %pad_maximum_fusion.here), channel_id=1, source_target_pairs={{0,32},{32,0},{64,96},{96,64},{128,160},{160,128},{192,224},{224,1... | collective-permute-start | bytes 1572872 | tf_op jit(solution)/shard_map/ppermute | solution.py:438
  83.1 13.7 %all-to-all-start.2 = ((f32[32,8,128]{2,1,0:T(8,128)}), f32[32,8,128]{2,1,0:T(8,128)S(1)}, u32[]{:S(2)}, u32[]{:S(2)}) async-start(f32[32,8,128]{2,1,0:T(8,128)} %moments.1), calls=%async_computation.2 | async-start | bytes 262144 | tf_op jit(solution)/shard_map/all_to_all | solution.py:436

commit v7 on v6

--- a/solution.py
+++ b/solution.py
@@ -33,6 +33,50 @@
     return a, b, c
 
 
+def upsampled(coarse):
+    up = (
+        lax.broadcasted_iota(jnp.int32, (128, COLS), 1) // 2
+        == lax.broadcasted_iota(jnp.int32, (128, COLS), 0)
+    ).astype(F32).astype(BF16)
+    wide = sum(jnp.dot(part_, up, preferred_element_type=F32) for part_ in split3(coarse))
+    return [wide[:, h * 128 : (h + 1) * 128] for h in range(2)]
+
+
+def spread_rows(ref, coarse, rows):
+    for h, half in enumerate(upsampled(coarse)):
+        ref[h, pl.ds(0, rows, stride=2), :] = half
+        ref[h, pl.ds(1, rows, stride=2), :] = half
+
+
+def plane_of(ref, at):
+    return jnp.concatenate([ref[h, at : at + ROWS, :] for h in range(2)], axis=1)
+
+
+def step(below, center, above, d, f):
+    row = lax.broadcasted_iota(jnp.int32, (ROWS, COLS), 0)
+    col = lax.broadcasted_iota(jnp.int32, (ROWS, COLS), 1)
+    beside = jnp.where(row == ROWS - 1, 0.0, pltpu.roll(center, ROWS - 1, 0))
+    beside = beside + jnp.where(row == 0, 0.0, pltpu.roll(center, 1, 0))
+    beside = beside + jnp.where(col == COLS - 1, 0.0, pltpu.roll(center, COLS - 1, 1))
+    beside = beside + jnp.where(col == 0, 0.0, pltpu.roll(center, 1, 1))
+    for side in (below, above):
+        if side is not None:
+            beside = beside + side
+    change = d * (beside - 6.0 * center) + 0.5 * center * (1.0 - center * center) + f
+    return center + STEP_SIZE * change
+
+
+def store_halves(ref, at, plane):
+    for h in range(2):
+        ref[h, at : at + ROWS, :] = plane[:, h * 128 : (h + 1) * 128]
+
+
+def sums_of_four(ref, rows):
+    return jnp.concatenate(
+        [sum(ref[h, pl.ds(q, rows, stride=4), :] for q in range(4)) for h in range(2)], axis=1
+    )
+
+
 def pack_kernel(state, theta, forcing, first, last, sems):
     copies = []
 
@@ -69,7 +113,7 @@
 def masks_kernel(
     slab, observed, noise, perturb, footprints, state, theta, forcing,
     in_x, in_z, in_y, count, given, state_here, theta_here, forcing_here,
-    boxes, target, spread, draws, sems,
+    diff, mid, inner, inner_sums, boxes, target, spread, draws, done, sems,
 ):
     quarter = OBS // 4
     chunks = [pl.ds(i * quarter, quarter) for i in range(4)]
@@ -114,6 +158,27 @@
             count[m * 4 + q : m * 4 + q + 1, :] = cells[:, q * 128 : (q + 1) * 128]
     for e in small:
         e.wait()
+    spread_rows(diff, 0.5 * jnp.exp(theta_here[...].reshape(-1, 128)), LOCAL * COARSE * 16)
+    for m in range(LOCAL):
+        for p in range(PLANES):
+            mid[m, p] = step(
+                state_here[m, p - 1] if p > 0 else None,
+                state_here[m, p],
+                state_here[m, p + 1] if p < PLANES - 1 else None,
+                plane_of(diff, (m * COARSE + p // 2) * ROWS),
+                forcing_here[p],
+            )
+        for p in range(2, PLANES - 2):
+            new = step(
+                mid[m, p - 1],
+                mid[m, p],
+                mid[m, p + 1],
+                plane_of(diff, (m * COARSE + p // 2) * ROWS),
+                forcing_here[p],
+            )
+            inner[m, p - 2] = new
+            store_halves(done, (m * 4 + p - 2) * ROWS, new)
+    inner_sums[...] = sums_of_four(done, LOCAL * 4 * 8)
     var = spread[...]
     given[0:LOCAL, :] = target[...] + jnp.sqrt(var) * draws[...]
     given[LOCAL : LOCAL + 1, :] = var
@@ -131,16 +196,21 @@
             jax.ShapeDtypeStruct((8, 128), F32),
             jax.ShapeDtypeStruct((8, BLOCK), F32),
             *(jax.ShapeDtypeStruct(a.shape, F32) for a in kept[-3:]),
+            jax.ShapeDtypeStruct((2, LOCAL * COARSE * ROWS, 128), F32),
+            jax.ShapeDtypeStruct((LOCAL, PLANES, ROWS, COLS), F32),
+            jax.ShapeDtypeStruct((LOCAL, 4, ROWS, COLS), F32),
+            jax.ShapeDtypeStruct((LOCAL * 4 * 8, COLS), F32),
         ),
         in_specs=[pl.BlockSpec(memory_space=pltpu.SMEM)]
         + [pl.BlockSpec(memory_space=pltpu.HBM)] * 7,
-        out_specs=(vmem,) * 8,
+        out_specs=(vmem,) * 12,
         compiler_params=pltpu.CompilerParams(vmem_limit_bytes=8 * MIB),
         scratch_shapes=[
             pltpu.VMEM((6, OBS), jnp.int32),
             pltpu.VMEM((1, BLOCK), F32),
             pltpu.VMEM((1, BLOCK), F32),
             pltpu.VMEM((LOCAL, BLOCK), F32),
+            pltpu.VMEM((2, LOCAL * 4 * ROWS, 128), F32),
             pltpu.SemaphoreType.DMA((10,)),
         ],
         name="masks",
@@ -148,80 +218,66 @@
 
 
 def window_kernel(
-    slab, state, theta, forcing, low, high, in_x, in_z, in_y,
-    final, part, diff, mid, fresh, done, sem,
+    slab, low, high, in_x, in_z, in_y, state, forcing, diff, mid, inner, inner_sums,
+    final, part, outer, edge, done, sems,
 ):
+    middle = pltpu.make_async_copy(inner, final.at[:, pl.ds(2, 4)], sems.at[0])
+    middle.start()
     s = slab[0]
-    keep_low = jnp.where(s > 0, 0.5, 0.0).astype(F32)
-    keep_high = jnp.where(s < SLABS - 1, 0.5, 0.0).astype(F32)
     pieces = []
     for m in range(LOCAL):
-        pieces.append(keep_low * jnp.exp(low[160:176, m * 128 : (m + 1) * 128]))
-        for c in range(COARSE):
-            pieces.append(0.5 * jnp.exp(theta[m, c]))
-        pieces.append(keep_high * jnp.exp(high[160:176, m * 128 : (m + 1) * 128]))
-    coarse = jnp.concatenate(pieces, axis=0)
-    up = (
-        lax.broadcasted_iota(jnp.int32, (128, COLS), 1) // 2
-        == lax.broadcasted_iota(jnp.int32, (128, COLS), 0)
-    ).astype(F32).astype(BF16)
-    wide = sum(jnp.dot(part_, up, preferred_element_type=F32) for part_ in split3(coarse))
-    rows = LOCAL * (COARSE + 2) * 16
-    for h in range(2):
-        diff[h, pl.ds(0, rows, stride=2), :] = wide[:, h * 128 : (h + 1) * 128]
-        diff[h, pl.ds(1, rows, stride=2), :] = wide[:, h * 128 : (h + 1) * 128]
-
-    row = lax.broadcasted_iota(jnp.int32, (ROWS, COLS), 0)
-    col = lax.broadcasted_iota(jnp.int32, (ROWS, COLS), 1)
-
-    def step(below, center, above, d, f):
-        beside = above + below
-        beside = beside + jnp.where(row == ROWS - 1, 0.0, pltpu.roll(center, ROWS - 1, 0))
-        beside = beside + jnp.where(row == 0, 0.0, pltpu.roll(center, 1, 0))
-        beside = beside + jnp.where(col == COLS - 1, 0.0, pltpu.roll(center, COLS - 1, 1))
-        beside = beside + jnp.where(col == 0, 0.0, pltpu.roll(center, 1, 1))
-        change = d * (beside - 6.0 * center) + 0.5 * center * (1.0 - center * center) + f
-        return center + STEP_SIZE * change
-
-    def plane(m, p):
-        if p < 0:
-            at = (m * 2 + p + 2) * ROWS
-            return low[at : at + ROWS, :]
-        if p >= PLANES:
-            at = (m * 2 + p - PLANES) * ROWS
-            return high[at : at + ROWS, :]
-        return state[m, p]
-
-    def force(p):
-        if p < 0:
-            return low[128:160, :]
-        if p >= PLANES:
-            return high[128:160, :]
-        return forcing[p]
-
-    def diffusivity(m, p):
-        at = (m * (COARSE + 2) + (p + 2) // 2) * ROWS
-        return jnp.concatenate([diff[h, at : at + ROWS, :] for h in range(2)], axis=1)
-
+        for halo, inside in ((low, s > 0), (high, s < SLABS - 1)):
+            keep = jnp.where(inside, 0.5, 0.0).astype(F32)
+            pieces.append(keep * jnp.exp(halo[160:176, m * 128 : (m + 1) * 128]))
+    spread_rows(outer, jnp.concatenate(pieces, axis=0), LOCAL * 2 * 16)
+
+    def own(m, p):
+        return plane_of(diff, (m * COARSE + p // 2) * ROWS)
+
+    leaving = []
     for m in range(LOCAL):
-        for p in range(-1, PLANES + 1):
-            mid[m * (PLANES + 2) + p + 1] = step(
-                plane(m, p - 1), plane(m, p), plane(m, p + 1), diffusivity(m, p), force(p)
+        below = [low[(m * 2 + p) * ROWS : (m * 2 + p + 1) * ROWS, :] for p in range(2)]
+        above = [high[(m * 2 + p) * ROWS : (m * 2 + p + 1) * ROWS, :] for p in range(2)]
+        ahead = step(
+            below[0], below[1], state[m, 0], plane_of(outer, m * 2 * ROWS), low[128:160, :]
+        )
+        behind = step(
+            state[m, PLANES - 1], above[0], above[1], plane_of(outer, (m * 2 + 1) * ROWS),
+            high[128:160, :],
+        )
+        bottom = mid[m, 0] + STEP_SIZE * (own(m, 0) * below[1])
+        top = mid[m, PLANES - 1] + STEP_SIZE * (own(m, PLANES - 1) * above[0])
+        news = (
+            step(ahead, bottom, mid[m, 1], own(m, 0), forcing[0]),
+            step(bottom, mid[m, 1], mid[m, 2], own(m, 1), forcing[1]),
+            step(mid[m, 5], mid[m, 6], top, own(m, 6), forcing[6]),
+            step(mid[m, 6], top, behind, own(m, 7), forcing[7]),
+        )
+        for i, new in enumerate(news):
+            edge[m, i // 2, i % 2] = new
+            store_halves(done, (m * 4 + i) * ROWS, new)
+        for i in range(2):
+            leaving.append(
+                pltpu.make_async_copy(
+                    edge.at[m, i], final.at[m, pl.ds(6 * i, 2)], sems.at[1 + 2 * m + i]
+                )
             )
-        for p in range(PLANES):
-            at = m * (PLANES + 2) + p
-            new = step(mid[at], mid[at + 1], mid[at + 2], diffusivity(m, p), forcing[p])
-            fresh[m, p] = new
-            to = (m * PLANES + p) * ROWS
-            for h in range(2):
-                done[h, to : to + ROWS, :] = new[:, h * 128 : (h + 1) * 128]
-
-    leave = pltpu.make_async_copy(fresh, final, sem)
-    leave.start()
+            leaving[-1].start()
 
     tall = LOCAL * PLANES * 8
+    outer_sums = sums_of_four(done, LOCAL * 4 * 8)
+    inside = inner_sums[...]
     sums = jnp.concatenate(
-        [sum(done[h, pl.ds(q, tall, stride=4), :] for q in range(4)) for h in range(2)], axis=1
+        [
+            x
+            for m in range(LOCAL)
+            for x in (
+                outer_sums[m * 32 : m * 32 + 16],
+                inside[m * 32 : m * 32 + 32],
+                outer_sums[m * 32 + 16 : m * 32 + 32],
+            )
+        ],
+        axis=0,
     )
     fold = (
         lax.broadcasted_iota(jnp.int32, (COLS, 128), 0) // 4
@@ -250,7 +306,9 @@
         return carry
 
     lax.fori_loop(0, SLABS, observe, 0, unroll=8)
-    leave.wait()
+    middle.wait()
+    for copy in leaving:
+        copy.wait()
 
 
 def window(slab, *given):
@@ -258,18 +316,17 @@
     return pl.pallas_call(
         window_kernel,
         out_shape=(
-            jax.ShapeDtypeStruct(given[0].shape, F32),
+            jax.ShapeDtypeStruct((LOCAL, PLANES, ROWS, COLS), F32),
             jax.ShapeDtypeStruct((SLABS, 8, 128), F32),
         ),
-        in_specs=[pl.BlockSpec(memory_space=pltpu.SMEM)] + [vmem] * 8,
+        in_specs=[pl.BlockSpec(memory_space=pltpu.SMEM)] + [vmem] * 11,
         out_specs=(pl.BlockSpec(memory_space=pltpu.HBM), vmem),
-        compiler_params=pltpu.CompilerParams(vmem_limit_bytes=12 * MIB),
+        compiler_params=pltpu.CompilerParams(vmem_limit_bytes=8 * MIB),
         scratch_shapes=[
-            pltpu.VMEM((2, LOCAL * (COARSE + 2) * ROWS, 128), F32),
-            pltpu.VMEM((LOCAL * (PLANES + 2), ROWS, COLS), F32),
-            pltpu.VMEM((LOCAL, PLANES, ROWS, COLS), F32),
-            pltpu.VMEM((2, LOCAL * PLANES * ROWS, 128), F32),
-            pltpu.SemaphoreType.DMA,
+            pltpu.VMEM((2, LOCAL * 2 * ROWS, 128), F32),
+            pltpu.VMEM((LOCAL, 2, 2, ROWS, COLS), F32),
+            pltpu.VMEM((2, LOCAL * 4 * ROWS, 128), F32),
+            pltpu.SemaphoreType.DMA((5,)),
         ],
         name="window",
     )(slab, *given)
@@ -420,13 +477,13 @@
         return lax.ppermute(value, "group", moves)
 
     pair = from_chip(field, 2)
-    in_x, in_z, in_y, count, given, *fields = masks(
+    in_x, in_z, in_y, count, given, state, here, forcing, *inside = masks(
         slab, observed.reshape(1, BLOCK), noise_var.reshape(1, BLOCK), perturb, boxes,
         state, theta, forcing,
     )
-    final, part = window(slab, *fields, low, high, in_x, in_z, in_y)
+    final, part = window(slab, low, high, in_x, in_z, in_y, state, forcing, *inside)
     arrived = lax.all_to_all(part, "slab", 0, 0, tiled=True)
-    pair = jnp.concatenate([fields[1].reshape(field.shape), pair], axis=0)
+    pair = jnp.concatenate([here.reshape(field.shape), pair], axis=0)
     across = from_chip(pair, 4)
     copies, own = own_predictions(arrived, count)
     preds = lax.all_to_all(copies, "group", 0, 0, tiled=True).reshape(GROUPS * 8, 128)

time: 99.2 us -> 98.5 us (level)
  no operation moved by 1% of the time
where the time goes in v7:
time: 98.5 us; the launch traced here: 98 us
  starting transfers between devices  47.7 us (48%)
  waiting for transfers between devices  20.7 us (21%)
  blocking collectives  19.1 us (19%)
  Pallas kernels  9.56 us (10%)
    all_to_all x1, blocking collectives, local(): lax.all_to_all(copies, 'group', 0, 0, tiled=True).reshape(GROUPS * 8, 128)  19.1 us
    ppermute x3, starting transfers between devices, from_chip(): return lax.ppermute(value, 'group', moves)  17.4 us
    all_to_all x1, starting transfers between devices, local(): arrived = lax.all_to_all(part, 'slab', 0, 0, tiled=True)  14.9 us
    all_to_all x1, waiting for transfers between devices, local(): sums = lax.all_to_all(sums, 'slab', 0, 0, tiled=True)  9.84 us
    ppermute x1, starting transfers between devices, local(): there = lax.ppermute(here, 'group', [(i, i ^ 1) for i in range(GROUPS)])  7.15 us
    all_to_all x1, starting transfers between devices, local(): sums = lax.all_to_all(sums, 'slab', 0, 0, tiled=True)  3.84 us
    ppermute x3, waiting for transfers between devices, from_chip(): return lax.ppermute(value, 'group', moves)  3.83 us
    ppermute x1, waiting for transfers between devices, local(): high = lax.ppermute(first, 'slab', [(i + 1, i) for i in range(SLABS - 1)])  3.83 us
  transfers between devices with their start and end apart: 8, of which 6 were waited for; matrix products, arithmetic and copies ran while one was open for 0% of the time, Pallas kernels for 8%

profile of v7, /device:TPU:1, one launch (start us, length us, event | category | flops | bytes accessed | tf_op | source)
XLA Modules:
  0.0 98.0 jit_solution(7429343615773460859)
XLA Ops:
  0.6 5.0 %collective-permute-start.2 = (f32[2,64,128]{2,1,0:T(8,128)}, f32[2,64,128]{2,1,0:T(8,128)S(1)}, u32[]{:S(2)}, u32[]{:S(2)}) collective-permute-start(f32[2,64,128]{2,1,0:T(8,128)} %bitcast.12), channel_id=1, source_target_pairs={{128,0},{416,32},{192,64},{480,96},{256,128},{32,160},{320,192},{9... | collective-permute-start | bytes 196616 | tf_op jit(solution)/shard_map/ppermute | solution.py:477
  5.7 2.6 %masks.1 = (bf16[64,16384]{1,0:T(8,128)(2,1)S(1)}, f32[8,16384]{1,0:T(8,128)S(1)}, f32[8,16384]{1,0:T(8,128)S(1)}, f32[8,128]{1,0:T(8,128)S(1)}, f32[8,512]{1,0:...) custom-call(s32[1]{0:T(128)} %bitcast.slab, ...), custom_call_target="tpu_custom_call" | custom-call | tf_op jit(solution)/shard_map/masks/pallas_call | solution.py:190
  8.2 1.1 %collective-permute-done.2 = f32[2,64,128]{2,1,0:T(8,128)S(1)} collective-permute-done((f32[2,64,128]{2,1,0:T(8,128)}, f32[2,64,128]{2,1,0:T(8,128)S(1)}, u32[]{:S(2)}, u32[]{:S(2)}) %collective-permute-start.2) | collective-permute-done | bytes 65568 | tf_op jit(solution)/shard_map/ppermute | solution.py:477
  9.3 6.9 %collective-permute-start.3 = (f32[4,64,128]{2,1,0:T(8,128)S(1)}, f32[4,64,128]{2,1,0:T(8,128)S(1)}, u32[]{:S(2)}, u32[]{:S(2)}) collective-permute-start(f32[4,64,128]{2,1,0:T(8,128)S(1)} %pad_maximum_fusion.2), channel_id=1, source_target_pairs={{256,0},{288,32},{320,64},{352,96},{384,128},{416,160},{448,192},{... | collective-permute-start | bytes 393224 | tf_op jit(solution)/shard_map/ppermute | solution.py:477
  16.3 2.8 %collective-permute-done.3 = f32[4,64,128]{2,1,0:T(8,128)S(1)} collective-permute-done((f32[4,64,128]{2,1,0:T(8,128)S(1)}, f32[4,64,128]{2,1,0:T(8,128)S(1)}, u32[]{:S(2)}, u32[]{:S(2)}) %collective-permute-start.3) | collective-permute-done | bytes 131104 | tf_op jit(solution)/shard_map/ppermute | solution.py:477
  19.0 5.4 %collective-permute-start.4 = (f32[8,64,128]{2,1,0:T(8,128)S(1)}, f32[8,64,128]{2,1,0:T(8,128)S(1)}, u32[]{:S(2)}, u32[]{:S(2)}) collective-permute-start(f32[8,64,128]{2,1,0:T(8,128)S(1)} %pad_maximum_fusion.1), channel_id=1, source_target_pairs={{64,0},{480,32},{128,64},{32,96},{192,128},{96,160},{256,192},{160... | collective-permute-start | bytes 786440 | tf_op jit(solution)/shard_map/ppermute | solution.py:477
  24.5 1.1 %pack.1 = (f32[176,256]{1,0:T(8,128)S(1)}, f32[176,256]{1,0:T(8,128)S(1)}) custom-call(f32[2,8,32,256]{3,2,1,0:T(8,128)} %state.3, f32[2,4,16,128]{3,2,1,0:T(8,128)} %theta.3, f32[8,32,256]{2,1,0:T(8,128)} %forcing.3), custom_call_target="tpu_custom_call" | custom-call | tf_op jit(solution)/shard_map/pack/pallas_call | solution.py:102
  25.6 3.1 %collective-permute-start = (f32[176,256]{1,0:T(8,128)S(1)}, f32[176,256]{1,0:T(8,128)S(1)}, u32[]{:S(2)}, u32[]{:S(2)}) collective-permute-start(f32[176,256]{1,0:T(8,128)S(1)} %get-tuple-element.20), channel_id=1, source_target_pairs={{0,1},{1,2},{2,3},{3,4},{4,5},{5,6},{6,7},{7,8},{8,9},{9,10},{10,1... | collective-permute-start | bytes 540680 | tf_op jit(solution)/shard_map/ppermute | solution.py:466
  28.7 1.3 %collective-permute-start.1 = (f32[176,256]{1,0:T(8,128)S(1)}, f32[176,256]{1,0:T(8,128)S(1)}, u32[]{:S(2)}, u32[]{:S(2)}) collective-permute-start(f32[176,256]{1,0:T(8,128)S(1)} %get-tuple-element.21), channel_id=1, source_target_pairs={{1,0},{2,1},{3,2},{4,3},{5,4},{6,5},{7,6},{8,7},{9,8},{10,9},{11,1... | collective-permute-start | bytes 540680 | tf_op jit(solution)/shard_map/ppermute | solution.py:467
  30.0 1.1 %collective-permute-done.low = f32[176,256]{1,0:T(8,128)S(1)} collective-permute-done((f32[176,256]{1,0:T(8,128)S(1)}, f32[176,256]{1,0:T(8,128)S(1)}, u32[]{:S(2)}, u32[]{:S(2)}) %collective-permute-start) | collective-permute-done | bytes 180256 | tf_op jit(solution)/shard_map/ppermute | solution.py:466
  31.1 3.8 %collective-permute-done.1.high = f32[176,256]{1,0:T(8,128)S(1)} collective-permute-done((f32[176,256]{1,0:T(8,128)S(1)}, f32[176,256]{1,0:T(8,128)S(1)}, u32[]{:S(2)}, u32[]{:S(2)}) %collective-permute-start.1) | collective-permute-done | bytes 180256 | tf_op jit(solution)/shard_map/ppermute | solution.py:467
  34.9 3.1 %window.1 = (f32[2,8,32,256]{3,2,1,0:T(8,128)}, f32[32,8,128]{2,1,0:T(8,128)}) custom-call(s32[1]{0:T(128)} %bitcast.slab, f32[176,256]{1,0:T(8,128)S(1)} %collective-permute-done.low, f32[176,256]{1,0:T(8,128)S(1)} %collective-permute-done.1.high, bf16[64,16384]{1,0:T(8,128)(2,1)S(1)} %get-tuple-element.22.in_x, f32[8,16384]{1,0:T(8,128)S(1)} %get-tuple-element.23.in_z, ...), custom_call_target="tpu_custom_call" | custom-call | tf_op jit(solution)/shard_map/window/pallas_call | solution.py:316
  38.0 14.9 %all-to-all-start = ((f32[32,8,128]{2,1,0:T(8,128)}), f32[32,8,128]{2,1,0:T(8,128)S(1)}, u32[]{:S(2)}, u32[]{:S(2)}) async-start(f32[32,8,128]{2,1,0:T(8,128)} %get-tuple-element.32), calls=%async_computation | async-start | bytes 262144 | tf_op jit(solution)/shard_map/all_to_all | solution.py:485
  53.0 0.0 collective-permute-done.4
  53.0 7.2 %collective-permute-start.5 = (f32[16,64,128]{2,1,0:T(8,128)S(1)}, f32[16,64,128]{2,1,0:T(8,128)S(1)}, u32[]{:S(2)}, u32[]{:S(2)}) collective-permute-start(f32[16,64,128]{2,1,0:T(8,128)S(1)} %pad_maximum_fusion.here), channel_id=1, source_target_pairs={{0,32},{32,0},{64,96},{96,64},{128,160},{160,128},{192,224},{224,1... | collective-permute-start | bytes 1572872 | tf_op jit(solution)/shard_map/ppermute | solution.py:495
  60.2 2.1 %all-to-all-done.arrived = f32[32,8,128]{2,1,0:T(8,128)S(1)} async-done(((f32[32,8,128]{2,1,0:T(8,128)}), f32[32,8,128]{2,1,0:T(8,128)S(1)}, u32[]{:S(2)}, u32[]{:S(2)}) %all-to-all-start) | async-done | bytes 131104 | tf_op jit(solution)/shard_map/all_to_all | solution.py:485
  62.3 19.1 %all_to_all.15 = f32[16,8,128]{2,1,0:T(8,128)S(1)} all-to-all(f32[16,8,128]{2,1,0:T(8,128)S(1)} %get-tuple-element.34), channel_id=1, replica_groups=mesh['group'=16,'slab'=32] {'group'}, dimensions={0} | all-to-all | bytes 131072 | tf_op jit(solution)/shard_map/all_to_all | solution.py:489
  81.4 1.0 %moments.1 = f32[32,8,128]{2,1,0:T(8,128)} custom-call(f32[128,128]{1,0:T(8,128)S(1)} %bitcast.11, f32[8,128]{1,0:T(8,128)S(1)} %get-tuple-element.35.own, f32[8,512]{1,0:T(8,128)S(1)} %get-tuple-element.36.given), custom_call_target="tpu_custom_call" | custom-call | tf_op jit(solution)/shard_map/moments/pallas_call | solution.py:385
  82.5 3.8 %all-to-all-start.2 = ((f32[32,8,128]{2,1,0:T(8,128)}), f32[32,8,128]{2,1,0:T(8,128)S(1)}, u32[]{:S(2)}, u32[]{:S(2)}) async-start(f32[32,8,128]{2,1,0:T(8,128)} %moments.1), calls=%async_computation.2 | async-start | bytes 262144 | tf_op jit(solution)/shard_map/all_to_all | solution.py:493
  86.3 9.8 %all-to-all-done.2.arrived = f32[32,8,128]{2,1,0:T(8,128)S(1)} async-done(((f32[32,8,128]{2,1,0:T(8,128)}), f32[32,8,128]{2,1,0:T(8,128)S(1)}, u32[]{:S(2)}, u32[]{:S(2)}) %all-to-all-start.2) | async-done | bytes 131104 | tf_op jit(solution)/shard_map/all_to_all | solution.py:493
  96.2 0.0 collective-permute-done.5.there
  96.2 1.8 %update.1 = f32[2,64,128]{2,1,0:T(8,128)} custom-call(s32[1]{0:T(128)} %bitcast.3.group, f32[32,8,128]{2,1,0:T(8,128)S(1)} %all-to-all-done.2.arrived, f32[16,64,128]{2,1,0:T(8,128)S(1)} %pad_maximum_fusion.here, f32[16,64,128]{2,1,0:T(8,128)S(1)} %collective-permute-done.5.there), custom_call_target="tpu_custom_call" | custom-call | tf_op jit(solution)/shard_map/update/pallas_call | solution.py:452
  (4 shorter events, 0.1 us)
Async XLA Ops:
  0.6 8.7 %collective-permute-start.2 = (f32[2,64,128]{2,1,0:T(8,128)}, f32[2,64,128]{2,1,0:T(8,128)S(1)}, u32[]{:S(2)}, u32[]{:S(2)}) collective-permute-start(f32[2,64,128]{2,1,0:T(8,128)} %bitcast.12), channel_id=1, source_target_pairs={{128,0},{416,32},{192,64},{480,96},{256,128},{32,160},{320,192},{9... | collective-permute-start | bytes 196616 | tf_op jit(solution)/shard_map/ppermute | solution.py:477
  9.3 9.7 %collective-permute-start.3 = (f32[4,64,128]{2,1,0:T(8,128)S(1)}, f32[4,64,128]{2,1,0:T(8,128)S(1)}, u32[]{:S(2)}, u32[]{:S(2)}) collective-permute-start(f32[4,64,128]{2,1,0:T(8,128)S(1)} %pad_maximum_fusion.2), channel_id=1, source_target_pairs={{256,0},{288,32},{320,64},{352,96},{384,128},{416,160},{448,192},{... | collective-permute-start | bytes 393224 | tf_op jit(solution)/shard_map/ppermute | solution.py:477
  19.0 33.9 %collective-permute-start.4 = (f32[8,64,128]{2,1,0:T(8,128)S(1)}, f32[8,64,128]{2,1,0:T(8,128)S(1)}, u32[]{:S(2)}, u32[]{:S(2)}) collective-permute-start(f32[8,64,128]{2,1,0:T(8,128)S(1)} %pad_maximum_fusion.1), channel_id=1, source_target_pairs={{64,0},{480,32},{128,64},{32,96},{192,128},{96,160},{256,192},{160... | collective-permute-start | bytes 786440 | tf_op jit(solution)/shard_map/ppermute | solution.py:477
  25.6 5.5 %collective-permute-start = (f32[176,256]{1,0:T(8,128)S(1)}, f32[176,256]{1,0:T(8,128)S(1)}, u32[]{:S(2)}, u32[]{:S(2)}) collective-permute-start(f32[176,256]{1,0:T(8,128)S(1)} %get-tuple-element.20), channel_id=1, source_target_pairs={{0,1},{1,2},{2,3},{3,4},{4,5},{5,6},{6,7},{7,8},{8,9},{9,10},{10,1... | collective-permute-start | bytes 540680 | tf_op jit(solution)/shard_map/ppermute | solution.py:466
  28.7 6.2 %collective-permute-start.1 = (f32[176,256]{1,0:T(8,128)S(1)}, f32[176,256]{1,0:T(8,128)S(1)}, u32[]{:S(2)}, u32[]{:S(2)}) collective-permute-start(f32[176,256]{1,0:T(8,128)S(1)} %get-tuple-element.21), channel_id=1, source_target_pairs={{1,0},{2,1},{3,2},{4,3},{5,4},{6,5},{7,6},{8,7},{9,8},{10,9},{11,1... | collective-permute-start | bytes 540680 | tf_op jit(solution)/shard_map/ppermute | solution.py:467
  38.0 24.3 %all-to-all-start = ((f32[32,8,128]{2,1,0:T(8,128)}), f32[32,8,128]{2,1,0:T(8,128)S(1)}, u32[]{:S(2)}, u32[]{:S(2)}) async-start(f32[32,8,128]{2,1,0:T(8,128)} %get-tuple-element.32), calls=%async_computation | async-start | bytes 262144 | tf_op jit(solution)/shard_map/all_to_all | solution.py:485
  53.0 43.1 %collective-permute-start.5 = (f32[16,64,128]{2,1,0:T(8,128)S(1)}, f32[16,64,128]{2,1,0:T(8,128)S(1)}, u32[]{:S(2)}, u32[]{:S(2)}) collective-permute-start(f32[16,64,128]{2,1,0:T(8,128)S(1)} %pad_maximum_fusion.here), channel_id=1, source_target_pairs={{0,32},{32,0},{64,96},{96,64},{128,160},{160,128},{192,224},{224,1... | collective-permute-start | bytes 1572872 | tf_op jit(solution)/shard_map/ppermute | solution.py:495
  82.5 13.7 %all-to-all-start.2 = ((f32[32,8,128]{2,1,0:T(8,128)}), f32[32,8,128]{2,1,0:T(8,128)S(1)}, u32[]{:S(2)}, u32[]{:S(2)}) async-start(f32[32,8,128]{2,1,0:T(8,128)} %moments.1), calls=%async_computation.2 | async-start | bytes 262144 | tf_op jit(solution)/shard_map/all_to_all | solution.py:493

commit v8 on v7

--- a/solution.py
+++ b/solution.py
@@ -410,17 +410,17 @@
     work = jnp.where(lane // 8 >= row // 8, upper, mirrored)
     work = jnp.where(row == lane, work + 1.0, work)
     work = jnp.where(lane < MEMBERS, work, jnp.where(lane < MEMBERS + LOCAL, cross, 0.0))
-    for first in range(0, MEMBERS, 8):
+    for first in range(0, MEMBERS, 16):
         columns = [
-            jnp.broadcast_to(work[:, k : k + 1], (MEMBERS, 128)) for k in range(first, first + 8)
+            jnp.broadcast_to(work[:, k : k + 1], (MEMBERS, 128)) for k in range(first, first + 16)
         ]
-        for i in range(8):
+        for i in range(16):
             k = first + i
             column = columns[i]
             inverse = 1.0 / column[k : k + 1, :]
             line = work[k : k + 1, :] * inverse
             work = jnp.where(row == k, line, work - column * line)
-            for later in range(i + 1, 8):
+            for later in range(i + 1, 16):
                 line = columns[later][k : k + 1, :] * inverse
                 columns[later] = jnp.where(row == k, line, columns[later] - column * line)
     mixing = work - jnp.mean(work, axis=0, keepdims=True)

time: 98.5 us -> 98.3 us (level)
  no operation moved by 1% of the time
where the time goes in v8:
time: 98.3 us; the launch traced here: 97.8 us
  starting transfers between devices  47.7 us (49%)
  waiting for transfers between devices  20.7 us (21%)
  blocking collectives  19.1 us (19%)
  Pallas kernels  9.42 us (10%)
    all_to_all x1, blocking collectives, local(): lax.all_to_all(copies, 'group', 0, 0, tiled=True).reshape(GROUPS * 8, 128)  19.1 us
    ppermute x3, starting transfers between devices, from_chip(): return lax.ppermute(value, 'group', moves)  17.4 us
    all_to_all x1, starting transfers between devices, local(): arrived = lax.all_to_all(part, 'slab', 0, 0, tiled=True)  14.9 us
    all_to_all x1, waiting for transfers between devices, local(): sums = lax.all_to_all(sums, 'slab', 0, 0, tiled=True)  9.84 us
    ppermute x1, starting transfers between devices, local(): there = lax.ppermute(here, 'group', [(i, i ^ 1) for i in range(GROUPS)])  7.15 us
    all_to_all x1, starting transfers between devices, local(): sums = lax.all_to_all(sums, 'slab', 0, 0, tiled=True)  3.84 us
    ppermute x3, waiting for transfers between devices, from_chip(): return lax.ppermute(value, 'group', moves)  3.83 us
    ppermute x1, waiting for transfers between devices, local(): high = lax.ppermute(first, 'slab', [(i + 1, i) for i in range(SLABS - 1)])  3.83 us
  transfers between devices with their start and end apart: 8, of which 6 were waited for; matrix products, arithmetic and copies ran while one was open for 0% of the time, Pallas kernels for 8%

profile of v8, /device:TPU:1, one launch (start us, length us, event | category | flops | bytes accessed | tf_op | source)
XLA Modules:
  0.0 97.8 jit_solution(4411119316859896578)
XLA Ops:
  0.6 5.0 %collective-permute-start.2 = (f32[2,64,128]{2,1,0:T(8,128)}, f32[2,64,128]{2,1,0:T(8,128)S(1)}, u32[]{:S(2)}, u32[]{:S(2)}) collective-permute-start(f32[2,64,128]{2,1,0:T(8,128)} %bitcast.12), channel_id=1, source_target_pairs={{128,0},{416,32},{192,64},{480,96},{256,128},{32,160},{320,192},{9... | collective-permute-start | bytes 196616 | tf_op jit(solution)/shard_map/ppermute | solution.py:477
  5.7 2.6 %masks.1 = (bf16[64,16384]{1,0:T(8,128)(2,1)S(1)}, f32[8,16384]{1,0:T(8,128)S(1)}, f32[8,16384]{1,0:T(8,128)S(1)}, f32[8,128]{1,0:T(8,128)S(1)}, f32[8,512]{1,0:...) custom-call(s32[1]{0:T(128)} %bitcast.slab, ...), custom_call_target="tpu_custom_call" | custom-call | tf_op jit(solution)/shard_map/masks/pallas_call | solution.py:190
  8.2 1.1 %collective-permute-done.2 = f32[2,64,128]{2,1,0:T(8,128)S(1)} collective-permute-done((f32[2,64,128]{2,1,0:T(8,128)}, f32[2,64,128]{2,1,0:T(8,128)S(1)}, u32[]{:S(2)}, u32[]{:S(2)}) %collective-permute-start.2) | collective-permute-done | bytes 65568 | tf_op jit(solution)/shard_map/ppermute | solution.py:477
  9.3 6.9 %collective-permute-start.3 = (f32[4,64,128]{2,1,0:T(8,128)S(1)}, f32[4,64,128]{2,1,0:T(8,128)S(1)}, u32[]{:S(2)}, u32[]{:S(2)}) collective-permute-start(f32[4,64,128]{2,1,0:T(8,128)S(1)} %pad_maximum_fusion.2), channel_id=1, source_target_pairs={{256,0},{288,32},{320,64},{352,96},{384,128},{416,160},{448,192},{... | collective-permute-start | bytes 393224 | tf_op jit(solution)/shard_map/ppermute | solution.py:477
  16.3 2.8 %collective-permute-done.3 = f32[4,64,128]{2,1,0:T(8,128)S(1)} collective-permute-done((f32[4,64,128]{2,1,0:T(8,128)S(1)}, f32[4,64,128]{2,1,0:T(8,128)S(1)}, u32[]{:S(2)}, u32[]{:S(2)}) %collective-permute-start.3) | collective-permute-done | bytes 131104 | tf_op jit(solution)/shard_map/ppermute | solution.py:477
  19.0 5.4 %collective-permute-start.4 = (f32[8,64,128]{2,1,0:T(8,128)S(1)}, f32[8,64,128]{2,1,0:T(8,128)S(1)}, u32[]{:S(2)}, u32[]{:S(2)}) collective-permute-start(f32[8,64,128]{2,1,0:T(8,128)S(1)} %pad_maximum_fusion.1), channel_id=1, source_target_pairs={{64,0},{480,32},{128,64},{32,96},{192,128},{96,160},{256,192},{160... | collective-permute-start | bytes 786440 | tf_op jit(solution)/shard_map/ppermute | solution.py:477
  24.5 1.1 %pack.1 = (f32[176,256]{1,0:T(8,128)S(1)}, f32[176,256]{1,0:T(8,128)S(1)}) custom-call(f32[2,8,32,256]{3,2,1,0:T(8,128)} %state.3, f32[2,4,16,128]{3,2,1,0:T(8,128)} %theta.3, f32[8,32,256]{2,1,0:T(8,128)} %forcing.3), custom_call_target="tpu_custom_call" | custom-call | tf_op jit(solution)/shard_map/pack/pallas_call | solution.py:102
  25.6 3.1 %collective-permute-start = (f32[176,256]{1,0:T(8,128)S(1)}, f32[176,256]{1,0:T(8,128)S(1)}, u32[]{:S(2)}, u32[]{:S(2)}) collective-permute-start(f32[176,256]{1,0:T(8,128)S(1)} %get-tuple-element.20), channel_id=1, source_target_pairs={{0,1},{1,2},{2,3},{3,4},{4,5},{5,6},{6,7},{7,8},{8,9},{9,10},{10,1... | collective-permute-start | bytes 540680 | tf_op jit(solution)/shard_map/ppermute | solution.py:466
  28.7 1.3 %collective-permute-start.1 = (f32[176,256]{1,0:T(8,128)S(1)}, f32[176,256]{1,0:T(8,128)S(1)}, u32[]{:S(2)}, u32[]{:S(2)}) collective-permute-start(f32[176,256]{1,0:T(8,128)S(1)} %get-tuple-element.21), channel_id=1, source_target_pairs={{1,0},{2,1},{3,2},{4,3},{5,4},{6,5},{7,6},{8,7},{9,8},{10,9},{11,1... | collective-permute-start | bytes 540680 | tf_op jit(solution)/shard_map/ppermute | solution.py:467
  30.0 1.1 %collective-permute-done.low = f32[176,256]{1,0:T(8,128)S(1)} collective-permute-done((f32[176,256]{1,0:T(8,128)S(1)}, f32[176,256]{1,0:T(8,128)S(1)}, u32[]{:S(2)}, u32[]{:S(2)}) %collective-permute-start) | collective-permute-done | bytes 180256 | tf_op jit(solution)/shard_map/ppermute | solution.py:466
  31.1 3.8 %collective-permute-done.1.high = f32[176,256]{1,0:T(8,128)S(1)} collective-permute-done((f32[176,256]{1,0:T(8,128)S(1)}, f32[176,256]{1,0:T(8,128)S(1)}, u32[]{:S(2)}, u32[]{:S(2)}) %collective-permute-start.1) | collective-permute-done | bytes 180256 | tf_op jit(solution)/shard_map/ppermute | solution.py:467
  34.9 3.1 %window.1 = (f32[2,8,32,256]{3,2,1,0:T(8,128)}, f32[32,8,128]{2,1,0:T(8,128)}) custom-call(s32[1]{0:T(128)} %bitcast.slab, f32[176,256]{1,0:T(8,128)S(1)} %collective-permute-done.low, f32[176,256]{1,0:T(8,128)S(1)} %collective-permute-done.1.high, bf16[64,16384]{1,0:T(8,128)(2,1)S(1)} %get-tuple-element.22.in_x, f32[8,16384]{1,0:T(8,128)S(1)} %get-tuple-element.23.in_z, ...), custom_call_target="tpu_custom_call" | custom-call | tf_op jit(solution)/shard_map/window/pallas_call | solution.py:316
  38.0 14.9 %all-to-all-start = ((f32[32,8,128]{2,1,0:T(8,128)}), f32[32,8,128]{2,1,0:T(8,128)S(1)}, u32[]{:S(2)}, u32[]{:S(2)}) async-start(f32[32,8,128]{2,1,0:T(8,128)} %get-tuple-element.32), calls=%async_computation | async-start | bytes 262144 | tf_op jit(solution)/shard_map/all_to_all | solution.py:485
  53.0 0.0 collective-permute-done.4
  53.0 7.2 %collective-permute-start.5 = (f32[16,64,128]{2,1,0:T(8,128)S(1)}, f32[16,64,128]{2,1,0:T(8,128)S(1)}, u32[]{:S(2)}, u32[]{:S(2)}) collective-permute-start(f32[16,64,128]{2,1,0:T(8,128)S(1)} %pad_maximum_fusion.here), channel_id=1, source_target_pairs={{0,32},{32,0},{64,96},{96,64},{128,160},{160,128},{192,224},{224,1... | collective-permute-start | bytes 1572872 | tf_op jit(solution)/shard_map/ppermute | solution.py:495
  60.2 2.1 %all-to-all-done.arrived = f32[32,8,128]{2,1,0:T(8,128)S(1)} async-done(((f32[32,8,128]{2,1,0:T(8,128)}), f32[32,8,128]{2,1,0:T(8,128)S(1)}, u32[]{:S(2)}, u32[]{:S(2)}) %all-to-all-start) | async-done | bytes 131104 | tf_op jit(solution)/shard_map/all_to_all | solution.py:485
  62.3 19.1 %all_to_all.15 = f32[16,8,128]{2,1,0:T(8,128)S(1)} all-to-all(f32[16,8,128]{2,1,0:T(8,128)S(1)} %get-tuple-element.34), channel_id=1, replica_groups=mesh['group'=16,'slab'=32] {'group'}, dimensions={0} | all-to-all | bytes 131072 | tf_op jit(solution)/shard_map/all_to_all | solution.py:489
  81.4 1.0 %moments.1 = f32[32,8,128]{2,1,0:T(8,128)} custom-call(f32[128,128]{1,0:T(8,128)S(1)} %bitcast.11, f32[8,128]{1,0:T(8,128)S(1)} %get-tuple-element.35.own, f32[8,512]{1,0:T(8,128)S(1)} %get-tuple-element.36.given), custom_call_target="tpu_custom_call" | custom-call | tf_op jit(solution)/shard_map/moments/pallas_call | solution.py:385
  82.5 3.8 %all-to-all-start.2 = ((f32[32,8,128]{2,1,0:T(8,128)}), f32[32,8,128]{2,1,0:T(8,128)S(1)}, u32[]{:S(2)}, u32[]{:S(2)}) async-start(f32[32,8,128]{2,1,0:T(8,128)} %moments.1), calls=%async_computation.2 | async-start | bytes 262144 | tf_op jit(solution)/shard_map/all_to_all | solution.py:493
  86.3 9.8 %all-to-all-done.2.arrived = f32[32,8,128]{2,1,0:T(8,128)S(1)} async-done(((f32[32,8,128]{2,1,0:T(8,128)}), f32[32,8,128]{2,1,0:T(8,128)S(1)}, u32[]{:S(2)}, u32[]{:S(2)}) %all-to-all-start.2) | async-done | bytes 131104 | tf_op jit(solution)/shard_map/all_to_all | solution.py:493
  96.2 0.0 collective-permute-done.5.there
  96.2 1.7 %update.1 = f32[2,64,128]{2,1,0:T(8,128)} custom-call(s32[1]{0:T(128)} %bitcast.3.group, f32[32,8,128]{2,1,0:T(8,128)S(1)} %all-to-all-done.2.arrived, f32[16,64,128]{2,1,0:T(8,128)S(1)} %pad_maximum_fusion.here, f32[16,64,128]{2,1,0:T(8,128)S(1)} %collective-permute-done.5.there), custom_call_target="tpu_custom_call" | custom-call | tf_op jit(solution)/shard_map/update/pallas_call | solution.py:452
  (4 shorter events, 0.1 us)
Async XLA Ops:
  0.6 8.7 %collective-permute-start.2 = (f32[2,64,128]{2,1,0:T(8,128)}, f32[2,64,128]{2,1,0:T(8,128)S(1)}, u32[]{:S(2)}, u32[]{:S(2)}) collective-permute-start(f32[2,64,128]{2,1,0:T(8,128)} %bitcast.12), channel_id=1, source_target_pairs={{128,0},{416,32},{192,64},{480,96},{256,128},{32,160},{320,192},{9... | collective-permute-start | bytes 196616 | tf_op jit(solution)/shard_map/ppermute | solution.py:477
  9.3 9.7 %collective-permute-start.3 = (f32[4,64,128]{2,1,0:T(8,128)S(1)}, f32[4,64,128]{2,1,0:T(8,128)S(1)}, u32[]{:S(2)}, u32[]{:S(2)}) collective-permute-start(f32[4,64,128]{2,1,0:T(8,128)S(1)} %pad_maximum_fusion.2), channel_id=1, source_target_pairs={{256,0},{288,32},{320,64},{352,96},{384,128},{416,160},{448,192},{... | collective-permute-start | bytes 393224 | tf_op jit(solution)/shard_map/ppermute | solution.py:477
  19.0 33.9 %collective-permute-start.4 = (f32[8,64,128]{2,1,0:T(8,128)S(1)}, f32[8,64,128]{2,1,0:T(8,128)S(1)}, u32[]{:S(2)}, u32[]{:S(2)}) collective-permute-start(f32[8,64,128]{2,1,0:T(8,128)S(1)} %pad_maximum_fusion.1), channel_id=1, source_target_pairs={{64,0},{480,32},{128,64},{32,96},{192,128},{96,160},{256,192},{160... | collective-permute-start | bytes 786440 | tf_op jit(solution)/shard_map/ppermute | solution.py:477
  25.6 5.5 %collective-permute-start = (f32[176,256]{1,0:T(8,128)S(1)}, f32[176,256]{1,0:T(8,128)S(1)}, u32[]{:S(2)}, u32[]{:S(2)}) collective-permute-start(f32[176,256]{1,0:T(8,128)S(1)} %get-tuple-element.20), channel_id=1, source_target_pairs={{0,1},{1,2},{2,3},{3,4},{4,5},{5,6},{6,7},{7,8},{8,9},{9,10},{10,1... | collective-permute-start | bytes 540680 | tf_op jit(solution)/shard_map/ppermute | solution.py:466
  28.7 6.2 %collective-permute-start.1 = (f32[176,256]{1,0:T(8,128)S(1)}, f32[176,256]{1,0:T(8,128)S(1)}, u32[]{:S(2)}, u32[]{:S(2)}) collective-permute-start(f32[176,256]{1,0:T(8,128)S(1)} %get-tuple-element.21), channel_id=1, source_target_pairs={{1,0},{2,1},{3,2},{4,3},{5,4},{6,5},{7,6},{8,7},{9,8},{10,9},{11,1... | collective-permute-start | bytes 540680 | tf_op jit(solution)/shard_map/ppermute | solution.py:467
  38.0 24.3 %all-to-all-start = ((f32[32,8,128]{2,1,0:T(8,128)}), f32[32,8,128]{2,1,0:T(8,128)S(1)}, u32[]{:S(2)}, u32[]{:S(2)}) async-start(f32[32,8,128]{2,1,0:T(8,128)} %get-tuple-element.32), calls=%async_computation | async-start | bytes 262144 | tf_op jit(solution)/shard_map/all_to_all | solution.py:485
  53.0 43.1 %collective-permute-start.5 = (f32[16,64,128]{2,1,0:T(8,128)S(1)}, f32[16,64,128]{2,1,0:T(8,128)S(1)}, u32[]{:S(2)}, u32[]{:S(2)}) collective-permute-start(f32[16,64,128]{2,1,0:T(8,128)S(1)} %pad_maximum_fusion.here), channel_id=1, source_target_pairs={{0,32},{32,0},{64,96},{96,64},{128,160},{160,128},{192,224},{224,1... | collective-permute-start | bytes 1572872 | tf_op jit(solution)/shard_map/ppermute | solution.py:495
  82.5 13.7 %all-to-all-start.2 = ((f32[32,8,128]{2,1,0:T(8,128)}), f32[32,8,128]{2,1,0:T(8,128)S(1)}, u32[]{:S(2)}, u32[]{:S(2)}) async-start(f32[32,8,128]{2,1,0:T(8,128)} %moments.1), calls=%async_computation.2 | async-start | bytes 262144 | tf_op jit(solution)/shard_map/all_to_all | solution.py:493

commit v9 on v8

--- a/solution.py
+++ b/solution.py
@@ -426,23 +426,19 @@
     mixing = work - jnp.mean(work, axis=0, keepdims=True)
     mixing = mixing * (1.0 / float(MEMBERS - 1) ** 0.5)
     mixing = jnp.where(row - group[0] * LOCAL == lane - MEMBERS, mixing + 1.0, mixing)
-    south = group[0] % 2 == 0
-    turn = MEMBERS - LOCAL * group[0]
     totals = [jnp.zeros((64, 128), F32) for _ in range(LOCAL)]
     for j in range(LOCAL):
-        column = jnp.broadcast_to(mixing[:, MEMBERS + j : MEMBERS + j + 1], (MEMBERS, 128))
-        rows = pltpu.roll(column, turn, 0)
-
-        def weight(at_south, at_north):
-            at_south, at_north = at_south % MEMBERS, at_north % MEMBERS
-            return jnp.where(
-                south, rows[at_south : at_south + 1, :], rows[at_north : at_north + 1, :]
+        rows = jnp.broadcast_to(mixing[:, MEMBERS + j : MEMBERS + j + 1], (MEMBERS, 128))
+        for size in (2, 4, 8, 16):
+            swapped = jnp.where(
+                row & size == 0, pltpu.roll(rows, MEMBERS - size, 0), pltpu.roll(rows, size, 0)
             )
-
+            rows = jnp.where((LOCAL * group[0]) & size != 0, swapped, rows)
         for i, d in enumerate(PARTS):
             for m in range(LOCAL):
-                totals[j] = totals[j] + weight(4 * d + m, m - 4 * d) * here[2 * i + m]
-                totals[j] = totals[j] + weight(2 + m - 4 * d, 4 * d + m - 2) * there[2 * i + m]
+                at = 4 * d + m
+                totals[j] = totals[j] + rows[at : at + 1, :] * here[2 * i + m]
+                totals[j] = totals[j] + rows[at + 2 : at + 3, :] * there[2 * i + m]
     for j in range(LOCAL):
         out[j] = totals[j]
 
@@ -467,14 +463,8 @@
     high = lax.ppermute(first, "slab", [(i + 1, i) for i in range(SLABS - 1)])
     field = theta.reshape(LOCAL, 64, 128)
 
-    def from_chip(value, chips):
-        half = GROUPS // 2
-        moves = [
-            (((y + (1 - 2 * core) * chips) % half) * 2 + core, y * 2 + core)
-            for y in range(half)
-            for core in range(2)
-        ]
-        return lax.ppermute(value, "group", moves)
+    def from_chip(value, bit):
+        return lax.ppermute(value, "group", [(i, i ^ (2 * bit)) for i in range(GROUPS)])
 
     pair = from_chip(field, 2)
     in_x, in_z, in_y, count, given, state, here, forcing, *inside = masks(

time: 98.3 us -> 97.4 us (level)
  waiting for transfers between devices: 20.7 us -> 18.5 us
  blocking collectives: 19.1 us -> 21.1 us
    all_to_all x1, blocking collectives: 19.1 us -> 21.1 us  [local(): lax.all_to_all(copies, 'group', 0, 0, tiled=True).reshape(GROUPS * 8, 128)]
    ppermute x3, starting transfers between devices: 17.4 us -> 15.7 us  [from_chip(): lax.ppermute(value, 'group', [(i, i ^ 2 * bit) for i in range(GROUPS)])]
    ppermute x3, waiting for transfers between devices: 3.83 us -> 2.35 us  [from_chip(): lax.ppermute(value, 'group', [(i, i ^ 2 * bit) for i in range(GROUPS)])]
    all_to_all x1, waiting for transfers between devices: 2.13 us -> 1.07 us  [local(): arrived = lax.all_to_all(part, 'slab', 0, 0, tiled=True)]
    ppermute x1, starting transfers between devices: 7.15 us -> 8.2 us  [local(): there = lax.ppermute(here, 'group', [(i, i ^ 1) for i in range(GROUPS)])]
  transfers between devices with their start and end apart: 8 -> 8, of which waited for: 6 -> 5; matrix products, arithmetic and copies ran while one was open for 0% -> 0% of each run, Pallas kernels for 8% -> 8%
where the time goes in v9:
time: 97.4 us; the launch traced here: 96.9 us
  starting transfers between devices  47.1 us (48%)
  blocking collectives  21.1 us (22%)
  waiting for transfers between devices  18.5 us (19%)
  Pallas kernels  9.43 us (10%)
    all_to_all x1, blocking collectives, local(): lax.all_to_all(copies, 'group', 0, 0, tiled=True).reshape(GROUPS * 8, 128)  21.1 us
    ppermute x3, starting transfers between devices, from_chip(): lax.ppermute(value, 'group', [(i, i ^ 2 * bit) for i in range(GROUPS)])  15.7 us
    all_to_all x1, starting transfers between devices, local(): arrived = lax.all_to_all(part, 'slab', 0, 0, tiled=True)  14.6 us
    all_to_all x1, waiting for transfers between devices, local(): sums = lax.all_to_all(sums, 'slab', 0, 0, tiled=True)  9.84 us
    ppermute x1, starting transfers between devices, local(): there = lax.ppermute(here, 'group', [(i, i ^ 1) for i in range(GROUPS)])  8.2 us
    ppermute x1, waiting for transfers between devices, local(): high = lax.ppermute(first, 'slab', [(i + 1, i) for i in range(SLABS - 1)])  4.12 us
    all_to_all x1, starting transfers between devices, local(): sums = lax.all_to_all(sums, 'slab', 0, 0, tiled=True)  3.84 us
    ppermute x1, starting transfers between devices, local(): low = lax.ppermute(last, 'slab', [(i, i + 1) for i in range(SLABS - 1)])  3.43 us
  transfers between devices with their start and end apart: 8, of which 5 were waited for; matrix products, arithmetic and copies ran while one was open for 0% of the time, Pallas kernels for 8%

profile of v9, /device:TPU:1, one launch (start us, length us, event | category | flops | bytes accessed | tf_op | source)
XLA Modules:
  0.0 96.9 jit_solution(1135012556751234374)
XLA Ops:
  0.6 5.0 %collective-permute-start.2 = (f32[2,64,128]{2,1,0:T(8,128)}, f32[2,64,128]{2,1,0:T(8,128)S(1)}, u32[]{:S(2)}, u32[]{:S(2)}) collective-permute-start(f32[2,64,128]{2,1,0:T(8,128)} %bitcast.12), channel_id=1, source_target_pairs={{0,128},{32,160},{64,192},{96,224},{128,0},{160,32},{192,64},{224,... | collective-permute-start | bytes 196616 | tf_op jit(solution)/shard_map/ppermute | solution.py:467
  5.7 2.6 %masks.1 = (bf16[64,16384]{1,0:T(8,128)(2,1)S(1)}, f32[8,16384]{1,0:T(8,128)S(1)}, f32[8,16384]{1,0:T(8,128)S(1)}, f32[8,128]{1,0:T(8,128)S(1)}, f32[8,512]{1,0:...) custom-call(s32[1]{0:T(128)} %bitcast.slab, ...), custom_call_target="tpu_custom_call" | custom-call | tf_op jit(solution)/shard_map/masks/pallas_call | solution.py:190
  8.2 0.0 collective-permute-done.2
  8.3 8.7 %collective-permute-start.3 = (f32[4,64,128]{2,1,0:T(8,128)S(1)}, f32[4,64,128]{2,1,0:T(8,128)S(1)}, u32[]{:S(2)}, u32[]{:S(2)}) collective-permute-start(f32[4,64,128]{2,1,0:T(8,128)S(1)} %pad_maximum_fusion.2), channel_id=1, source_target_pairs={{0,256},{32,288},{64,320},{96,352},{128,384},{160,416},{192,448},{... | collective-permute-start | bytes 393224 | tf_op jit(solution)/shard_map/ppermute | solution.py:467
  17.0 2.3 %collective-permute-done.3 = f32[4,64,128]{2,1,0:T(8,128)S(1)} collective-permute-done((f32[4,64,128]{2,1,0:T(8,128)S(1)}, f32[4,64,128]{2,1,0:T(8,128)S(1)}, u32[]{:S(2)}, u32[]{:S(2)}) %collective-permute-start.3) | collective-permute-done | bytes 131104 | tf_op jit(solution)/shard_map/ppermute | solution.py:467
  19.4 1.9 %collective-permute-start.4 = (f32[8,64,128]{2,1,0:T(8,128)S(1)}, f32[8,64,128]{2,1,0:T(8,128)S(1)}, u32[]{:S(2)}, u32[]{:S(2)}) collective-permute-start(f32[8,64,128]{2,1,0:T(8,128)S(1)} %pad_maximum_fusion.1), channel_id=1, source_target_pairs={{0,64},{32,96},{64,0},{96,32},{128,192},{160,224},{192,128},{224,1... | collective-permute-start | bytes 786440 | tf_op jit(solution)/shard_map/ppermute | solution.py:467
  21.3 1.1 %pack.1 = (f32[176,256]{1,0:T(8,128)S(1)}, f32[176,256]{1,0:T(8,128)S(1)}) custom-call(f32[2,8,32,256]{3,2,1,0:T(8,128)} %state.3, f32[2,4,16,128]{3,2,1,0:T(8,128)} %theta.3, f32[8,32,256]{2,1,0:T(8,128)} %forcing.3), custom_call_target="tpu_custom_call" | custom-call | tf_op jit(solution)/shard_map/pack/pallas_call | solution.py:102
  22.4 3.4 %collective-permute-start = (f32[176,256]{1,0:T(8,128)S(1)}, f32[176,256]{1,0:T(8,128)S(1)}, u32[]{:S(2)}, u32[]{:S(2)}) collective-permute-start(f32[176,256]{1,0:T(8,128)S(1)} %get-tuple-element.20), channel_id=1, source_target_pairs={{0,1},{1,2},{2,3},{3,4},{4,5},{5,6},{6,7},{7,8},{8,9},{9,10},{10,1... | collective-permute-start | bytes 540680 | tf_op jit(solution)/shard_map/ppermute | solution.py:462
  25.8 1.3 %collective-permute-start.1 = (f32[176,256]{1,0:T(8,128)S(1)}, f32[176,256]{1,0:T(8,128)S(1)}, u32[]{:S(2)}, u32[]{:S(2)}) collective-permute-start(f32[176,256]{1,0:T(8,128)S(1)} %get-tuple-element.21), channel_id=1, source_target_pairs={{1,0},{2,1},{3,2},{4,3},{5,4},{6,5},{7,6},{8,7},{9,8},{10,9},{11,1... | collective-permute-start | bytes 540680 | tf_op jit(solution)/shard_map/ppermute | solution.py:463
  27.1 1.1 %collective-permute-done.low = f32[176,256]{1,0:T(8,128)S(1)} collective-permute-done((f32[176,256]{1,0:T(8,128)S(1)}, f32[176,256]{1,0:T(8,128)S(1)}, u32[]{:S(2)}, u32[]{:S(2)}) %collective-permute-start) | collective-permute-done | bytes 180256 | tf_op jit(solution)/shard_map/ppermute | solution.py:462
  28.2 4.1 %collective-permute-done.1.high = f32[176,256]{1,0:T(8,128)S(1)} collective-permute-done((f32[176,256]{1,0:T(8,128)S(1)}, f32[176,256]{1,0:T(8,128)S(1)}, u32[]{:S(2)}, u32[]{:S(2)}) %collective-permute-start.1) | collective-permute-done | bytes 180256 | tf_op jit(solution)/shard_map/ppermute | solution.py:463
  32.4 3.1 %window.1 = (f32[2,8,32,256]{3,2,1,0:T(8,128)}, f32[32,8,128]{2,1,0:T(8,128)}) custom-call(s32[1]{0:T(128)} %bitcast.slab, f32[176,256]{1,0:T(8,128)S(1)} %collective-permute-done.low, f32[176,256]{1,0:T(8,128)S(1)} %collective-permute-done.1.high, bf16[64,16384]{1,0:T(8,128)(2,1)S(1)} %get-tuple-element.22.in_x, f32[8,16384]{1,0:T(8,128)S(1)} %get-tuple-element.23.in_z, ...), custom_call_target="tpu_custom_call" | custom-call | tf_op jit(solution)/shard_map/window/pallas_call | solution.py:316
  35.5 14.6 %all-to-all-start = ((f32[32,8,128]{2,1,0:T(8,128)}), f32[32,8,128]{2,1,0:T(8,128)S(1)}, u32[]{:S(2)}, u32[]{:S(2)}) async-start(f32[32,8,128]{2,1,0:T(8,128)} %get-tuple-element.32), calls=%async_computation | async-start | bytes 262144 | tf_op jit(solution)/shard_map/all_to_all | solution.py:475
  50.1 0.0 collective-permute-done.4
  50.1 8.2 %collective-permute-start.5 = (f32[16,64,128]{2,1,0:T(8,128)S(1)}, f32[16,64,128]{2,1,0:T(8,128)S(1)}, u32[]{:S(2)}, u32[]{:S(2)}) collective-permute-start(f32[16,64,128]{2,1,0:T(8,128)S(1)} %pad_maximum_fusion.here), channel_id=1, source_target_pairs={{0,32},{32,0},{64,96},{96,64},{128,160},{160,128},{192,224},{224,1... | collective-permute-start | bytes 1572872 | tf_op jit(solution)/shard_map/ppermute | solution.py:485
  58.3 1.1 %all-to-all-done.arrived = f32[32,8,128]{2,1,0:T(8,128)S(1)} async-done(((f32[32,8,128]{2,1,0:T(8,128)}), f32[32,8,128]{2,1,0:T(8,128)S(1)}, u32[]{:S(2)}, u32[]{:S(2)}) %all-to-all-start) | async-done | bytes 131104 | tf_op jit(solution)/shard_map/all_to_all | solution.py:475
  59.5 21.1 %all_to_all.15 = f32[16,8,128]{2,1,0:T(8,128)S(1)} all-to-all(f32[16,8,128]{2,1,0:T(8,128)S(1)} %get-tuple-element.34), channel_id=1, replica_groups=mesh['group'=16,'slab'=32] {'group'}, dimensions={0} | all-to-all | bytes 131072 | tf_op jit(solution)/shard_map/all_to_all | solution.py:479
  80.6 1.0 %moments.1 = f32[32,8,128]{2,1,0:T(8,128)} custom-call(f32[128,128]{1,0:T(8,128)S(1)} %bitcast.11, f32[8,128]{1,0:T(8,128)S(1)} %get-tuple-element.35.own, f32[8,512]{1,0:T(8,128)S(1)} %get-tuple-element.36.given), custom_call_target="tpu_custom_call" | custom-call | tf_op jit(solution)/shard_map/moments/pallas_call | solution.py:385
  81.6 3.8 %all-to-all-start.2 = ((f32[32,8,128]{2,1,0:T(8,128)}), f32[32,8,128]{2,1,0:T(8,128)S(1)}, u32[]{:S(2)}, u32[]{:S(2)}) async-start(f32[32,8,128]{2,1,0:T(8,128)} %moments.1), calls=%async_computation.2 | async-start | bytes 262144 | tf_op jit(solution)/shard_map/all_to_all | solution.py:483
  85.4 9.8 %all-to-all-done.2.arrived = f32[32,8,128]{2,1,0:T(8,128)S(1)} async-done(((f32[32,8,128]{2,1,0:T(8,128)}), f32[32,8,128]{2,1,0:T(8,128)S(1)}, u32[]{:S(2)}, u32[]{:S(2)}) %all-to-all-start.2) | async-done | bytes 131104 | tf_op jit(solution)/shard_map/all_to_all | solution.py:483
  95.3 0.0 collective-permute-done.5.there
  95.3 1.7 %update.1 = f32[2,64,128]{2,1,0:T(8,128)} custom-call(s32[1]{0:T(128)} %bitcast.3.group, f32[32,8,128]{2,1,0:T(8,128)S(1)} %all-to-all-done.2.arrived, f32[16,64,128]{2,1,0:T(8,128)S(1)} %pad_maximum_fusion.here, f32[16,64,128]{2,1,0:T(8,128)S(1)} %collective-permute-done.5.there), custom_call_target="tpu_custom_call" | custom-call | tf_op jit(solution)/shard_map/update/pallas_call | solution.py:448
  (4 shorter events, 0.1 us)
Async XLA Ops:
  0.6 7.6 %collective-permute-start.2 = (f32[2,64,128]{2,1,0:T(8,128)}, f32[2,64,128]{2,1,0:T(8,128)S(1)}, u32[]{:S(2)}, u32[]{:S(2)}) collective-permute-start(f32[2,64,128]{2,1,0:T(8,128)} %bitcast.12), channel_id=1, source_target_pairs={{0,128},{32,160},{64,192},{96,224},{128,0},{160,32},{192,64},{224,... | collective-permute-start | bytes 196616 | tf_op jit(solution)/shard_map/ppermute | solution.py:467
  8.3 11.1 %collective-permute-start.3 = (f32[4,64,128]{2,1,0:T(8,128)S(1)}, f32[4,64,128]{2,1,0:T(8,128)S(1)}, u32[]{:S(2)}, u32[]{:S(2)}) collective-permute-start(f32[4,64,128]{2,1,0:T(8,128)S(1)} %pad_maximum_fusion.2), channel_id=1, source_target_pairs={{0,256},{32,288},{64,320},{96,352},{128,384},{160,416},{192,448},{... | collective-permute-start | bytes 393224 | tf_op jit(solution)/shard_map/ppermute | solution.py:467
  19.4 30.7 %collective-permute-start.4 = (f32[8,64,128]{2,1,0:T(8,128)S(1)}, f32[8,64,128]{2,1,0:T(8,128)S(1)}, u32[]{:S(2)}, u32[]{:S(2)}) collective-permute-start(f32[8,64,128]{2,1,0:T(8,128)S(1)} %pad_maximum_fusion.1), channel_id=1, source_target_pairs={{0,64},{32,96},{64,0},{96,32},{128,192},{160,224},{192,128},{224,1... | collective-permute-start | bytes 786440 | tf_op jit(solution)/shard_map/ppermute | solution.py:467
  22.4 5.9 %collective-permute-start = (f32[176,256]{1,0:T(8,128)S(1)}, f32[176,256]{1,0:T(8,128)S(1)}, u32[]{:S(2)}, u32[]{:S(2)}) collective-permute-start(f32[176,256]{1,0:T(8,128)S(1)} %get-tuple-element.20), channel_id=1, source_target_pairs={{0,1},{1,2},{2,3},{3,4},{4,5},{5,6},{6,7},{7,8},{8,9},{9,10},{10,1... | collective-permute-start | bytes 540680 | tf_op jit(solution)/shard_map/ppermute | solution.py:462
  25.8 6.5 %collective-permute-start.1 = (f32[176,256]{1,0:T(8,128)S(1)}, f32[176,256]{1,0:T(8,128)S(1)}, u32[]{:S(2)}, u32[]{:S(2)}) collective-permute-start(f32[176,256]{1,0:T(8,128)S(1)} %get-tuple-element.21), channel_id=1, source_target_pairs={{1,0},{2,1},{3,2},{4,3},{5,4},{6,5},{7,6},{8,7},{9,8},{10,9},{11,1... | collective-permute-start | bytes 540680 | tf_op jit(solution)/shard_map/ppermute | solution.py:463
  35.5 24.0 %all-to-all-start = ((f32[32,8,128]{2,1,0:T(8,128)}), f32[32,8,128]{2,1,0:T(8,128)S(1)}, u32[]{:S(2)}, u32[]{:S(2)}) async-start(f32[32,8,128]{2,1,0:T(8,128)} %get-tuple-element.32), calls=%async_computation | async-start | bytes 262144 | tf_op jit(solution)/shard_map/all_to_all | solution.py:475
  50.1 45.1 %collective-permute-start.5 = (f32[16,64,128]{2,1,0:T(8,128)S(1)}, f32[16,64,128]{2,1,0:T(8,128)S(1)}, u32[]{:S(2)}, u32[]{:S(2)}) collective-permute-start(f32[16,64,128]{2,1,0:T(8,128)S(1)} %pad_maximum_fusion.here), channel_id=1, source_target_pairs={{0,32},{32,0},{64,96},{96,64},{128,160},{160,128},{192,224},{224,1... | collective-permute-start | bytes 1572872 | tf_op jit(solution)/shard_map/ppermute | solution.py:485
  81.6 13.7 %all-to-all-start.2 = ((f32[32,8,128]{2,1,0:T(8,128)}), f32[32,8,128]{2,1,0:T(8,128)S(1)}, u32[]{:S(2)}, u32[]{:S(2)}) async-start(f32[32,8,128]{2,1,0:T(8,128)} %moments.1), calls=%async_computation.2 | async-start | bytes 262144 | tf_op jit(solution)/shard_map/all_to_all | solution.py:483

commit v10 on v9

--- a/solution.py
+++ b/solution.py
@@ -77,37 +77,41 @@
     )
 
 
-def pack_kernel(state, theta, forcing, first, last, sems):
+def pack_kernel(slab, state, theta, forcing, near, far, sems):
     copies = []
 
     def copy(src, dst):
         copies.append(pltpu.make_async_copy(src, dst, sems.at[len(copies)]))
 
-    for out, plane, coarse, force in ((first, 0, 0, 0), (last, PLANES - 2, COARSE - 1, PLANES - 1)):
+    even = slab[0] % 2 == 0
+    for out, is_last in ((near, even), (far, jnp.logical_not(even))):
+        plane = jnp.where(is_last, PLANES - 2, 0)
         for m in range(LOCAL):
             for p in range(2):
                 at = (m * 2 + p) * ROWS
                 copy(state.at[m, plane + p], out.at[pl.ds(at, ROWS), :])
+            coarse = jnp.where(is_last, COARSE - 1, 0)
             copy(theta.at[m, coarse], out.at[pl.ds(160, 16), pl.ds(m * 128, 128)])
-        copy(forcing.at[force], out.at[pl.ds(128, ROWS), :])
+        copy(forcing.at[jnp.where(is_last, PLANES - 1, 0)], out.at[pl.ds(128, ROWS), :])
     for c in copies:
         c.start()
     for c in copies:
         c.wait()
 
 
-def pack(state, theta, forcing):
+def pack(slab, state, theta, forcing):
     shape = jax.ShapeDtypeStruct((HALO_ROWS, COLS), F32)
     vmem = pl.BlockSpec(memory_space=pltpu.VMEM)
     return pl.pallas_call(
         pack_kernel,
         out_shape=(shape, shape),
-        in_specs=[pl.BlockSpec(memory_space=pltpu.HBM)] * 3,
+        in_specs=[pl.BlockSpec(memory_space=pltpu.SMEM)]
+        + [pl.BlockSpec(memory_space=pltpu.HBM)] * 3,
         out_specs=(vmem, vmem),
         compiler_params=pltpu.CompilerParams(vmem_limit_bytes=2 * MIB),
         scratch_shapes=[pltpu.SemaphoreType.DMA((14,))],
         name="pack",
-    )(*(pltpu.with_memory_space_constraint(a, pltpu.HBM) for a in (state, theta, forcing)))
+    )(slab, *(pltpu.with_memory_space_constraint(a, pltpu.HBM) for a in (state, theta, forcing)))
 
 
 def masks_kernel(
@@ -218,17 +222,25 @@
 
 
 def window_kernel(
-    slab, low, high, in_x, in_z, in_y, state, forcing, diff, mid, inner, inner_sums,
+    slab, near, far, in_x, in_z, in_y, state, forcing, diff, mid, inner, inner_sums,
     final, part, outer, edge, done, sems,
 ):
     middle = pltpu.make_async_copy(inner, final.at[:, pl.ds(2, 4)], sems.at[0])
     middle.start()
     s = slab[0]
+    even = s % 2 == 0
+
+    def low(rows, lanes=slice(None)):
+        return jnp.where(even, far[rows, lanes], near[rows, lanes])
+
+    def high(rows, lanes=slice(None)):
+        return jnp.where(even, near[rows, lanes], far[rows, lanes])
+
     pieces = []
     for m in range(LOCAL):
         for halo, inside in ((low, s > 0), (high, s < SLABS - 1)):
             keep = jnp.where(inside, 0.5, 0.0).astype(F32)
-            pieces.append(keep * jnp.exp(halo[160:176, m * 128 : (m + 1) * 128]))
+            pieces.append(keep * jnp.exp(halo(slice(160, 176), slice(m * 128, (m + 1) * 128))))
     spread_rows(outer, jnp.concatenate(pieces, axis=0), LOCAL * 2 * 16)
 
     def own(m, p):
@@ -236,14 +248,15 @@
 
     leaving = []
     for m in range(LOCAL):
-        below = [low[(m * 2 + p) * ROWS : (m * 2 + p + 1) * ROWS, :] for p in range(2)]
-        above = [high[(m * 2 + p) * ROWS : (m * 2 + p + 1) * ROWS, :] for p in range(2)]
+        below = [low(slice((m * 2 + p) * ROWS, (m * 2 + p + 1) * ROWS)) for p in range(2)]
+        above = [high(slice((m * 2 + p) * ROWS, (m * 2 + p + 1) * ROWS)) for p in range(2)]
         ahead = step(
-            below[0], below[1], state[m, 0], plane_of(outer, m * 2 * ROWS), low[128:160, :]
+            below[0], below[1], state[m, 0], plane_of(outer, m * 2 * ROWS),
+            low(slice(128, 160)),
         )
         behind = step(
             state[m, PLANES - 1], above[0], above[1], plane_of(outer, (m * 2 + 1) * ROWS),
-            high[128:160, :],
+            high(slice(128, 160)),
         )
         bottom = mid[m, 0] + STEP_SIZE * (own(m, 0) * below[1])
         top = mid[m, PLANES - 1] + STEP_SIZE * (own(m, PLANES - 1) * above[0])
@@ -458,9 +471,10 @@
 def local(state, theta, forcing, boxes, observed, noise_var, perturb):
     slab = lax.axis_index("slab").astype(jnp.int32).reshape(1)
     group = lax.axis_index("group").astype(jnp.int32).reshape(1)
-    first, last = pack(state, theta, forcing)
-    low = lax.ppermute(last, "slab", [(i, i + 1) for i in range(SLABS - 1)])
-    high = lax.ppermute(first, "slab", [(i + 1, i) for i in range(SLABS - 1)])
+    near, far = pack(slab, state, theta, forcing)
+    pairs = [(i, i + 1) for i in range(1, SLABS - 1, 2)]
+    far = lax.ppermute(far, "slab", pairs + [(j, i) for i, j in pairs])
+    near = lax.ppermute(near, "slab", [(i, i ^ 1) for i in range(SLABS)])
     field = theta.reshape(LOCAL, 64, 128)
 
     def from_chip(value, bit):
@@ -471,7 +485,7 @@
         slab, observed.reshape(1, BLOCK), noise_var.reshape(1, BLOCK), perturb, boxes,
         state, theta, forcing,
     )
-    final, part = window(slab, low, high, in_x, in_z, in_y, state, forcing, *inside)
+    final, part = window(slab, near, far, in_x, in_z, in_y, state, forcing, *inside)
     arrived = lax.all_to_all(part, "slab", 0, 0, tiled=True)
     pair = jnp.concatenate([here.reshape(field.shape), pair], axis=0)
     across = from_chip(pair, 4)

time: 97.4 us -> 96.6 us (level)
  waiting for transfers between devices: 18.5 us -> 15.5 us
  starting transfers between devices: 47.1 us -> 49.3 us
    ppermute x2, waiting for transfers between devices: 5.23 us -> 2.19 us  [the longest x1 2.19 us: local(): near = lax.ppermute(near, 'slab', [(i, i ^ 1) for i in range(SLABS)])]
    all_to_all x1, starting transfers between devices: 14.6 us -> 17.4 us  [local(): arrived = lax.all_to_all(part, 'slab', 0, 0, tiled=True)]
  transfers between devices with their start and end apart: 8 -> 8, of which waited for: 5 -> 4; matrix products, arithmetic and copies ran while one was open for 0% -> 0% of each run, Pallas kernels for 8% -> 8%
where the time goes in v10:
time: 96.6 us; the launch traced here: 96.1 us
  starting transfers between devices  49.3 us (51%)
  blocking collectives  21.1 us (22%)
  waiting for transfers between devices  15.5 us (16%)
  Pallas kernels  9.46 us (10%)
    all_to_all x1, blocking collectives, local(): lax.all_to_all(copies, 'group', 0, 0, tiled=True).reshape(GROUPS * 8, 128)  21.1 us
    all_to_all x1, starting transfers between devices, local(): arrived = lax.all_to_all(part, 'slab', 0, 0, tiled=True)  17.4 us
    ppermute x3, starting transfers between devices, from_chip(): lax.ppermute(value, 'group', [(i, i ^ 2 * bit) for i in range(GROUPS)])  15.7 us
    all_to_all x1, waiting for transfers between devices, local(): sums = lax.all_to_all(sums, 'slab', 0, 0, tiled=True)  9.84 us
    ppermute x1, starting transfers between devices, local(): there = lax.ppermute(here, 'group', [(i, i ^ 1) for i in range(GROUPS)])  8.2 us
    all_to_all x1, starting transfers between devices, local(): sums = lax.all_to_all(sums, 'slab', 0, 0, tiled=True)  3.84 us
    ppermute x1, starting transfers between devices, local(): near = lax.ppermute(near, 'slab', [(i, i ^ 1) for i in range(SLABS)])  3.43 us
    pallas_call x1, Pallas kernels, window(): pl.pallas_call(window_kernel, out_shape=(jax.ShapeDtypeStruct((LOCAL, PLA...  3.11 us
  transfers between devices with their start and end apart: 8, of which 4 were waited for; matrix products, arithmetic and copies ran while one was open for 0% of the time, Pallas kernels for 8%

profile of v10, /device:TPU:1, one launch (start us, length us, event | category | flops | bytes accessed | tf_op | source)
XLA Modules:
  0.0 96.1 jit_solution(14700338338621707166)
XLA Ops:
  0.6 5.0 %collective-permute-start.2 = (f32[2,64,128]{2,1,0:T(8,128)}, f32[2,64,128]{2,1,0:T(8,128)S(1)}, u32[]{:S(2)}, u32[]{:S(2)}) collective-permute-start(f32[2,64,128]{2,1,0:T(8,128)} %bitcast.12), channel_id=1, source_target_pairs={{0,128},{32,160},{64,192},{96,224},{128,0},{160,32},{192,64},{224,... | collective-permute-start | bytes 196616 | tf_op jit(solution)/shard_map/ppermute | solution.py:481
  5.7 2.6 %masks.1 = (bf16[64,16384]{1,0:T(8,128)(2,1)S(1)}, f32[8,16384]{1,0:T(8,128)S(1)}, f32[8,16384]{1,0:T(8,128)S(1)}, f32[8,128]{1,0:T(8,128)S(1)}, f32[8,512]{1,0:...) custom-call(s32[1]{0:T(128)} %bitcast.slab, ...), custom_call_target="tpu_custom_call" | custom-call | tf_op jit(solution)/shard_map/masks/pallas_call | solution.py:194
  8.2 0.0 collective-permute-done.2
  8.3 8.7 %collective-permute-start.3 = (f32[4,64,128]{2,1,0:T(8,128)S(1)}, f32[4,64,128]{2,1,0:T(8,128)S(1)}, u32[]{:S(2)}, u32[]{:S(2)}) collective-permute-start(f32[4,64,128]{2,1,0:T(8,128)S(1)} %pad_maximum_fusion.2), channel_id=1, source_target_pairs={{0,256},{32,288},{64,320},{96,352},{128,384},{160,416},{192,448},{... | collective-permute-start | bytes 393224 | tf_op jit(solution)/shard_map/ppermute | solution.py:481
  17.0 2.3 %collective-permute-done.3 = f32[4,64,128]{2,1,0:T(8,128)S(1)} collective-permute-done((f32[4,64,128]{2,1,0:T(8,128)S(1)}, f32[4,64,128]{2,1,0:T(8,128)S(1)}, u32[]{:S(2)}, u32[]{:S(2)}) %collective-permute-start.3) | collective-permute-done | bytes 131104 | tf_op jit(solution)/shard_map/ppermute | solution.py:481
  19.4 1.9 %collective-permute-start.4 = (f32[8,64,128]{2,1,0:T(8,128)S(1)}, f32[8,64,128]{2,1,0:T(8,128)S(1)}, u32[]{:S(2)}, u32[]{:S(2)}) collective-permute-start(f32[8,64,128]{2,1,0:T(8,128)S(1)} %pad_maximum_fusion.1), channel_id=1, source_target_pairs={{0,64},{32,96},{64,0},{96,32},{128,192},{160,224},{192,128},{224,1... | collective-permute-start | bytes 786440 | tf_op jit(solution)/shard_map/ppermute | solution.py:481
  21.3 1.1 %pack.1 = (f32[176,256]{1,0:T(8,128)S(1)}, f32[176,256]{1,0:T(8,128)S(1)}) custom-call(s32[1]{0:T(128)} %bitcast.slab, f32[2,8,32,256]{3,2,1,0:T(8,128)} %state.3, f32[2,4,16,128]{3,2,1,0:T(8,128)} %theta.3, f32[8,32,256]{2,1,0:T(8,128)} %forcing.3), custom_call_target="tpu_custom_call" | custom-call | tf_op jit(solution)/shard_map/pack/pallas_call | solution.py:105
  22.4 3.4 %collective-permute-start = (f32[176,256]{1,0:T(8,128)S(1)}, f32[176,256]{1,0:T(8,128)S(1)}, u32[]{:S(2)}, u32[]{:S(2)}) collective-permute-start(f32[176,256]{1,0:T(8,128)S(1)} %get-tuple-element.20), channel_id=1, source_target_pairs={{0,1},{1,0},{2,3},{3,2},{4,5},{5,4},{6,7},{7,6},{8,9},{9,8},{10,11... | collective-permute-start | bytes 540680 | tf_op jit(solution)/shard_map/ppermute | solution.py:477
  25.8 0.7 collective-permute-start.1
  26.5 2.2 %collective-permute-done.near = f32[176,256]{1,0:T(8,128)S(1)} collective-permute-done((f32[176,256]{1,0:T(8,128)S(1)}, f32[176,256]{1,0:T(8,128)S(1)}, u32[]{:S(2)}, u32[]{:S(2)}) %collective-permute-start) | collective-permute-done | bytes 180256 | tf_op jit(solution)/shard_map/ppermute | solution.py:477
  28.7 0.0 collective-permute-done.1.far
  28.7 3.1 %window.1 = (f32[2,8,32,256]{3,2,1,0:T(8,128)}, f32[32,8,128]{2,1,0:T(8,128)}) custom-call(s32[1]{0:T(128)} %bitcast.slab, f32[176,256]{1,0:T(8,128)S(1)} %collective-permute-done.near, f32[176,256]{1,0:T(8,128)S(1)} %collective-permute-done.1.far, bf16[64,16384]{1,0:T(8,128)(2,1)S(1)} %get-tuple-element.22.in_x, f32[8,16384]{1,0:T(8,128)S(1)} %get-tuple-element.23.in_z, ...), custom_call_target="tpu_custom_call" | custom-call | tf_op jit(solution)/shard_map/window/pallas_call | solution.py:329
  31.8 17.4 %all-to-all-start = ((f32[32,8,128]{2,1,0:T(8,128)}), f32[32,8,128]{2,1,0:T(8,128)S(1)}, u32[]{:S(2)}, u32[]{:S(2)}) async-start(f32[32,8,128]{2,1,0:T(8,128)} %get-tuple-element.32), calls=%async_computation | async-start | bytes 262144 | tf_op jit(solution)/shard_map/all_to_all | solution.py:489
  49.3 0.0 collective-permute-done.4
  49.3 8.2 %collective-permute-start.5 = (f32[16,64,128]{2,1,0:T(8,128)S(1)}, f32[16,64,128]{2,1,0:T(8,128)S(1)}, u32[]{:S(2)}, u32[]{:S(2)}) collective-permute-start(f32[16,64,128]{2,1,0:T(8,128)S(1)} %pad_maximum_fusion.here), channel_id=1, source_target_pairs={{0,32},{32,0},{64,96},{96,64},{128,160},{160,128},{192,224},{224,1... | collective-permute-start | bytes 1572872 | tf_op jit(solution)/shard_map/ppermute | solution.py:499
  57.5 1.1 %all-to-all-done.arrived = f32[32,8,128]{2,1,0:T(8,128)S(1)} async-done(((f32[32,8,128]{2,1,0:T(8,128)}), f32[32,8,128]{2,1,0:T(8,128)S(1)}, u32[]{:S(2)}, u32[]{:S(2)}) %all-to-all-start) | async-done | bytes 131104 | tf_op jit(solution)/shard_map/all_to_all | solution.py:489
  58.6 21.1 %all_to_all.15 = f32[16,8,128]{2,1,0:T(8,128)S(1)} all-to-all(f32[16,8,128]{2,1,0:T(8,128)S(1)} %get-tuple-element.34), channel_id=1, replica_groups=mesh['group'=16,'slab'=32] {'group'}, dimensions={0} | all-to-all | bytes 131072 | tf_op jit(solution)/shard_map/all_to_all | solution.py:493
  79.7 1.0 %moments.1 = f32[32,8,128]{2,1,0:T(8,128)} custom-call(f32[128,128]{1,0:T(8,128)S(1)} %bitcast.11, f32[8,128]{1,0:T(8,128)S(1)} %get-tuple-element.35.own, f32[8,512]{1,0:T(8,128)S(1)} %get-tuple-element.36.given), custom_call_target="tpu_custom_call" | custom-call | tf_op jit(solution)/shard_map/moments/pallas_call | solution.py:398
  80.7 3.8 %all-to-all-start.2 = ((f32[32,8,128]{2,1,0:T(8,128)}), f32[32,8,128]{2,1,0:T(8,128)S(1)}, u32[]{:S(2)}, u32[]{:S(2)}) async-start(f32[32,8,128]{2,1,0:T(8,128)} %moments.1), calls=%async_computation.2 | async-start | bytes 262144 | tf_op jit(solution)/shard_map/all_to_all | solution.py:497
  84.6 9.8 %all-to-all-done.2.arrived = f32[32,8,128]{2,1,0:T(8,128)S(1)} async-done(((f32[32,8,128]{2,1,0:T(8,128)}), f32[32,8,128]{2,1,0:T(8,128)S(1)}, u32[]{:S(2)}, u32[]{:S(2)}) %all-to-all-start.2) | async-done | bytes 131104 | tf_op jit(solution)/shard_map/all_to_all | solution.py:497
  94.4 0.0 collective-permute-done.5.there
  94.4 1.7 %update.1 = f32[2,64,128]{2,1,0:T(8,128)} custom-call(s32[1]{0:T(128)} %bitcast.3.group, f32[32,8,128]{2,1,0:T(8,128)S(1)} %all-to-all-done.2.arrived, f32[16,64,128]{2,1,0:T(8,128)S(1)} %pad_maximum_fusion.here, f32[16,64,128]{2,1,0:T(8,128)S(1)} %collective-permute-done.5.there), custom_call_target="tpu_custom_call" | custom-call | tf_op jit(solution)/shard_map/update/pallas_call | solution.py:461
  (4 shorter events, 0.1 us)
Async XLA Ops:
  0.6 7.6 %collective-permute-start.2 = (f32[2,64,128]{2,1,0:T(8,128)}, f32[2,64,128]{2,1,0:T(8,128)S(1)}, u32[]{:S(2)}, u32[]{:S(2)}) collective-permute-start(f32[2,64,128]{2,1,0:T(8,128)} %bitcast.12), channel_id=1, source_target_pairs={{0,128},{32,160},{64,192},{96,224},{128,0},{160,32},{192,64},{224,... | collective-permute-start | bytes 196616 | tf_op jit(solution)/shard_map/ppermute | solution.py:481
  8.3 11.1 %collective-permute-start.3 = (f32[4,64,128]{2,1,0:T(8,128)S(1)}, f32[4,64,128]{2,1,0:T(8,128)S(1)}, u32[]{:S(2)}, u32[]{:S(2)}) collective-permute-start(f32[4,64,128]{2,1,0:T(8,128)S(1)} %pad_maximum_fusion.2), channel_id=1, source_target_pairs={{0,256},{32,288},{64,320},{96,352},{128,384},{160,416},{192,448},{... | collective-permute-start | bytes 393224 | tf_op jit(solution)/shard_map/ppermute | solution.py:481
  19.4 29.9 %collective-permute-start.4 = (f32[8,64,128]{2,1,0:T(8,128)S(1)}, f32[8,64,128]{2,1,0:T(8,128)S(1)}, u32[]{:S(2)}, u32[]{:S(2)}) collective-permute-start(f32[8,64,128]{2,1,0:T(8,128)S(1)} %pad_maximum_fusion.1), channel_id=1, source_target_pairs={{0,64},{32,96},{64,0},{96,32},{128,192},{160,224},{192,128},{224,1... | collective-permute-start | bytes 786440 | tf_op jit(solution)/shard_map/ppermute | solution.py:481
  22.4 6.3 %collective-permute-start = (f32[176,256]{1,0:T(8,128)S(1)}, f32[176,256]{1,0:T(8,128)S(1)}, u32[]{:S(2)}, u32[]{:S(2)}) collective-permute-start(f32[176,256]{1,0:T(8,128)S(1)} %get-tuple-element.20), channel_id=1, source_target_pairs={{0,1},{1,0},{2,3},{3,2},{4,5},{5,4},{6,7},{7,6},{8,9},{9,8},{10,11... | collective-permute-start | bytes 540680 | tf_op jit(solution)/shard_map/ppermute | solution.py:477
  25.8 2.9 %collective-permute-start.1 = (f32[176,256]{1,0:T(8,128)S(1)}, f32[176,256]{1,0:T(8,128)S(1)}, u32[]{:S(2)}, u32[]{:S(2)}) collective-permute-start(f32[176,256]{1,0:T(8,128)S(1)} %get-tuple-element.21), channel_id=1, source_target_pairs={{1,2},{3,4},{5,6},{7,8},{9,10},{11,12},{13,14},{15,16},{17,18},{19... | collective-permute-start | bytes 540680 | tf_op jit(solution)/shard_map/ppermute | solution.py:476
  31.8 26.8 %all-to-all-start = ((f32[32,8,128]{2,1,0:T(8,128)}), f32[32,8,128]{2,1,0:T(8,128)S(1)}, u32[]{:S(2)}, u32[]{:S(2)}) async-start(f32[32,8,128]{2,1,0:T(8,128)} %get-tuple-element.32), calls=%async_computation | async-start | bytes 262144 | tf_op jit(solution)/shard_map/all_to_all | solution.py:489
  49.3 45.1 %collective-permute-start.5 = (f32[16,64,128]{2,1,0:T(8,128)S(1)}, f32[16,64,128]{2,1,0:T(8,128)S(1)}, u32[]{:S(2)}, u32[]{:S(2)}) collective-permute-start(f32[16,64,128]{2,1,0:T(8,128)S(1)} %pad_maximum_fusion.here), channel_id=1, source_target_pairs={{0,32},{32,0},{64,96},{96,64},{128,160},{160,128},{192,224},{224,1... | collective-permute-start | bytes 1572872 | tf_op jit(solution)/shard_map/ppermute | solution.py:499
  80.7 13.7 %all-to-all-start.2 = ((f32[32,8,128]{2,1,0:T(8,128)}), f32[32,8,128]{2,1,0:T(8,128)S(1)}, u32[]{:S(2)}, u32[]{:S(2)}) async-start(f32[32,8,128]{2,1,0:T(8,128)} %moments.1), calls=%async_computation.2 | async-start | bytes 262144 | tf_op jit(solution)/shard_map/all_to_all | solution.py:497

commit v11 on v10

--- a/solution.py
+++ b/solution.py
@@ -21,7 +21,7 @@
 BLOCK = 512
 OBS = SLABS * BLOCK
 MIB = 1 << 20
-PARTS = (0, 2, 4, 6, 1, 3, 5, 7)
+PARTS = (0, 1, 4, 5, 2, 3, 6, 7)
 HALO_ROWS = 176
 
 
@@ -480,7 +480,7 @@
     def from_chip(value, bit):
         return lax.ppermute(value, "group", [(i, i ^ (2 * bit)) for i in range(GROUPS)])
 
-    pair = from_chip(field, 2)
+    pair = from_chip(field, 1)
     in_x, in_z, in_y, count, given, state, here, forcing, *inside = masks(
         slab, observed.reshape(1, BLOCK), noise_var.reshape(1, BLOCK), perturb, boxes,
         state, theta, forcing,
@@ -492,7 +492,7 @@
     copies, own = own_predictions(arrived, count)
     preds = lax.all_to_all(copies, "group", 0, 0, tiled=True).reshape(GROUPS * 8, 128)
     even = jnp.concatenate([pair, across], axis=0)
-    odd = from_chip(even, 1)
+    odd = from_chip(even, 2)
     sums = moments(preds, own, given)
     sums = lax.all_to_all(sums, "slab", 0, 0, tiled=True)
     here = jnp.concatenate([even, odd], axis=0)

time: 96.6 us -> 95.8 us (level)
  blocking collectives: 21.1 us -> 16.4 us
  waiting for transfers between devices: 15.5 us -> 20 us
    all_to_all x1, blocking collectives: 21.1 us -> 16.4 us  [local(): lax.all_to_all(copies, 'group', 0, 0, tiled=True).reshape(GROUPS * 8, 128)]
    all_to_all x1, waiting for transfers between devices: 1.07 us -> 4.83 us  [local(): arrived = lax.all_to_all(part, 'slab', 0, 0, tiled=True)]
    ppermute x1, starting transfers between devices: 8.2 us -> 4.45 us  [local(): there = lax.ppermute(here, 'group', [(i, i ^ 1) for i in range(GROUPS)])]
    ppermute x3, starting transfers between devices: 15.7 us -> 17.4 us  [from_chip(): lax.ppermute(value, 'group', [(i, i ^ 2 * bit) for i in range(GROUPS)])]
    ppermute x1, starting transfers between devices: 3.43 us -> 4.75 us  [local(): near = lax.ppermute(near, 'slab', [(i, i ^ 1) for i in range(SLABS)])]
where the time goes in v11:
time: 95.8 us; the launch traced here: 95.3 us
  starting transfers between devices  48.6 us (51%)
  waiting for transfers between devices  20 us (21%)
  blocking collectives  16.4 us (17%)
  Pallas kernels  9.46 us (10%)
    all_to_all x1, starting transfers between devices, local(): arrived = lax.all_to_all(part, 'slab', 0, 0, tiled=True)  17.5 us
    ppermute x3, starting transfers between devices, from_chip(): lax.ppermute(value, 'group', [(i, i ^ 2 * bit) for i in range(GROUPS)])  17.4 us
    all_to_all x1, blocking collectives, local(): lax.all_to_all(copies, 'group', 0, 0, tiled=True).reshape(GROUPS * 8, 128)  16.4 us
    all_to_all x1, waiting for transfers between devices, local(): sums = lax.all_to_all(sums, 'slab', 0, 0, tiled=True)  9.84 us
    all_to_all x1, waiting for transfers between devices, local(): arrived = lax.all_to_all(part, 'slab', 0, 0, tiled=True)  4.83 us
    ppermute x1, starting transfers between devices, local(): near = lax.ppermute(near, 'slab', [(i, i ^ 1) for i in range(SLABS)])  4.75 us
    ppermute x1, starting transfers between devices, local(): there = lax.ppermute(here, 'group', [(i, i ^ 1) for i in range(GROUPS)])  4.45 us
    all_to_all x1, starting transfers between devices, local(): sums = lax.all_to_all(sums, 'slab', 0, 0, tiled=True)  3.84 us
  transfers between devices with their start and end apart: 8, of which 4 were waited for; matrix products, arithmetic and copies ran while one was open for 0% of the time, Pallas kernels for 8%

profile of v11, /device:TPU:1, one launch (start us, length us, event | category | flops | bytes accessed | tf_op | source)
XLA Modules:
  0.0 95.3 jit_solution(17246072128723610112)
XLA Ops:
  0.6 4.0 %collective-permute-start.2 = (f32[2,64,128]{2,1,0:T(8,128)}, f32[2,64,128]{2,1,0:T(8,128)S(1)}, u32[]{:S(2)}, u32[]{:S(2)}) collective-permute-start(f32[2,64,128]{2,1,0:T(8,128)} %bitcast.12), channel_id=1, source_target_pairs={{0,64},{32,96},{64,0},{96,32},{128,192},{160,224},{192,128},{224,1... | collective-permute-start | bytes 196616 | tf_op jit(solution)/shard_map/ppermute | solution.py:481
  4.7 2.6 %masks.1 = (bf16[64,16384]{1,0:T(8,128)(2,1)S(1)}, f32[8,16384]{1,0:T(8,128)S(1)}, f32[8,16384]{1,0:T(8,128)S(1)}, f32[8,128]{1,0:T(8,128)S(1)}, f32[8,512]{1,0:...) custom-call(s32[1]{0:T(128)} %bitcast.slab, ...), custom_call_target="tpu_custom_call" | custom-call | tf_op jit(solution)/shard_map/masks/pallas_call | solution.py:194
  7.2 0.0 collective-permute-done.2
  7.3 6.9 %collective-permute-start.3 = (f32[4,64,128]{2,1,0:T(8,128)S(1)}, f32[4,64,128]{2,1,0:T(8,128)S(1)}, u32[]{:S(2)}, u32[]{:S(2)}) collective-permute-start(f32[4,64,128]{2,1,0:T(8,128)S(1)} %pad_maximum_fusion.2), channel_id=1, source_target_pairs={{0,256},{32,288},{64,320},{96,352},{128,384},{160,416},{192,448},{... | collective-permute-start | bytes 393224 | tf_op jit(solution)/shard_map/ppermute | solution.py:481
  14.1 2.8 %collective-permute-done.3 = f32[4,64,128]{2,1,0:T(8,128)S(1)} collective-permute-done((f32[4,64,128]{2,1,0:T(8,128)S(1)}, f32[4,64,128]{2,1,0:T(8,128)S(1)}, u32[]{:S(2)}, u32[]{:S(2)}) %collective-permute-start.3) | collective-permute-done | bytes 131104 | tf_op jit(solution)/shard_map/ppermute | solution.py:481
  17.0 6.5 %collective-permute-start.4 = (f32[8,64,128]{2,1,0:T(8,128)S(1)}, f32[8,64,128]{2,1,0:T(8,128)S(1)}, u32[]{:S(2)}, u32[]{:S(2)}) collective-permute-start(f32[8,64,128]{2,1,0:T(8,128)S(1)} %pad_maximum_fusion.1), channel_id=1, source_target_pairs={{0,128},{32,160},{64,192},{96,224},{128,0},{160,32},{192,64},{224,... | collective-permute-start | bytes 786440 | tf_op jit(solution)/shard_map/ppermute | solution.py:481
  23.5 1.1 %pack.1 = (f32[176,256]{1,0:T(8,128)S(1)}, f32[176,256]{1,0:T(8,128)S(1)}) custom-call(s32[1]{0:T(128)} %bitcast.slab, f32[2,8,32,256]{3,2,1,0:T(8,128)} %state.3, f32[2,4,16,128]{3,2,1,0:T(8,128)} %theta.3, f32[8,32,256]{2,1,0:T(8,128)} %forcing.3), custom_call_target="tpu_custom_call" | custom-call | tf_op jit(solution)/shard_map/pack/pallas_call | solution.py:105
  24.6 4.8 %collective-permute-start = (f32[176,256]{1,0:T(8,128)S(1)}, f32[176,256]{1,0:T(8,128)S(1)}, u32[]{:S(2)}, u32[]{:S(2)}) collective-permute-start(f32[176,256]{1,0:T(8,128)S(1)} %get-tuple-element.20), channel_id=1, source_target_pairs={{0,1},{1,0},{2,3},{3,2},{4,5},{5,4},{6,7},{7,6},{8,9},{9,8},{10,11... | collective-permute-start | bytes 540680 | tf_op jit(solution)/shard_map/ppermute | solution.py:477
  29.3 0.7 collective-permute-start.1
  30.0 2.5 %collective-permute-done.near = f32[176,256]{1,0:T(8,128)S(1)} collective-permute-done((f32[176,256]{1,0:T(8,128)S(1)}, f32[176,256]{1,0:T(8,128)S(1)}, u32[]{:S(2)}, u32[]{:S(2)}) %collective-permute-start) | collective-permute-done | bytes 180256 | tf_op jit(solution)/shard_map/ppermute | solution.py:477
  32.5 0.0 collective-permute-done.1.far
  32.5 3.1 %window.1 = (f32[2,8,32,256]{3,2,1,0:T(8,128)}, f32[32,8,128]{2,1,0:T(8,128)}) custom-call(s32[1]{0:T(128)} %bitcast.slab, f32[176,256]{1,0:T(8,128)S(1)} %collective-permute-done.near, f32[176,256]{1,0:T(8,128)S(1)} %collective-permute-done.1.far, bf16[64,16384]{1,0:T(8,128)(2,1)S(1)} %get-tuple-element.22.in_x, f32[8,16384]{1,0:T(8,128)S(1)} %get-tuple-element.23.in_z, ...), custom_call_target="tpu_custom_call" | custom-call | tf_op jit(solution)/shard_map/window/pallas_call | solution.py:329
  35.6 17.5 %all-to-all-start = ((f32[32,8,128]{2,1,0:T(8,128)}), f32[32,8,128]{2,1,0:T(8,128)S(1)}, u32[]{:S(2)}, u32[]{:S(2)}) async-start(f32[32,8,128]{2,1,0:T(8,128)} %get-tuple-element.32), calls=%async_computation | async-start | bytes 262144 | tf_op jit(solution)/shard_map/all_to_all | solution.py:489
  53.1 0.0 collective-permute-done.4
  53.2 4.5 %collective-permute-start.5 = (f32[16,64,128]{2,1,0:T(8,128)S(1)}, f32[16,64,128]{2,1,0:T(8,128)S(1)}, u32[]{:S(2)}, u32[]{:S(2)}) collective-permute-start(f32[16,64,128]{2,1,0:T(8,128)S(1)} %pad_maximum_fusion.here), channel_id=1, source_target_pairs={{0,32},{32,0},{64,96},{96,64},{128,160},{160,128},{192,224},{224,1... | collective-permute-start | bytes 1572872 | tf_op jit(solution)/shard_map/ppermute | solution.py:499
  57.6 4.8 %all-to-all-done.arrived = f32[32,8,128]{2,1,0:T(8,128)S(1)} async-done(((f32[32,8,128]{2,1,0:T(8,128)}), f32[32,8,128]{2,1,0:T(8,128)S(1)}, u32[]{:S(2)}, u32[]{:S(2)}) %all-to-all-start) | async-done | bytes 131104 | tf_op jit(solution)/shard_map/all_to_all | solution.py:489
  62.5 16.4 %all_to_all.15 = f32[16,8,128]{2,1,0:T(8,128)S(1)} all-to-all(f32[16,8,128]{2,1,0:T(8,128)S(1)} %get-tuple-element.34), channel_id=1, replica_groups=mesh['group'=16,'slab'=32] {'group'}, dimensions={0} | all-to-all | bytes 131072 | tf_op jit(solution)/shard_map/all_to_all | solution.py:493
  78.9 1.0 %moments.1 = f32[32,8,128]{2,1,0:T(8,128)} custom-call(f32[128,128]{1,0:T(8,128)S(1)} %bitcast.11, f32[8,128]{1,0:T(8,128)S(1)} %get-tuple-element.35.own, f32[8,512]{1,0:T(8,128)S(1)} %get-tuple-element.36.given), custom_call_target="tpu_custom_call" | custom-call | tf_op jit(solution)/shard_map/moments/pallas_call | solution.py:398
  79.9 3.8 %all-to-all-start.2 = ((f32[32,8,128]{2,1,0:T(8,128)}), f32[32,8,128]{2,1,0:T(8,128)S(1)}, u32[]{:S(2)}, u32[]{:S(2)}) async-start(f32[32,8,128]{2,1,0:T(8,128)} %moments.1), calls=%async_computation.2 | async-start | bytes 262144 | tf_op jit(solution)/shard_map/all_to_all | solution.py:497
  83.7 9.8 %all-to-all-done.2.arrived = f32[32,8,128]{2,1,0:T(8,128)S(1)} async-done(((f32[32,8,128]{2,1,0:T(8,128)}), f32[32,8,128]{2,1,0:T(8,128)S(1)}, u32[]{:S(2)}, u32[]{:S(2)}) %all-to-all-start.2) | async-done | bytes 131104 | tf_op jit(solution)/shard_map/all_to_all | solution.py:497
  93.6 0.0 collective-permute-done.5.there
  93.6 1.7 %update.1 = f32[2,64,128]{2,1,0:T(8,128)} custom-call(s32[1]{0:T(128)} %bitcast.3.group, f32[32,8,128]{2,1,0:T(8,128)S(1)} %all-to-all-done.2.arrived, f32[16,64,128]{2,1,0:T(8,128)S(1)} %pad_maximum_fusion.here, f32[16,64,128]{2,1,0:T(8,128)S(1)} %collective-permute-done.5.there), custom_call_target="tpu_custom_call" | custom-call | tf_op jit(solution)/shard_map/update/pallas_call | solution.py:461
  (4 shorter events, 0.1 us)
Async XLA Ops:
  0.6 6.6 %collective-permute-start.2 = (f32[2,64,128]{2,1,0:T(8,128)}, f32[2,64,128]{2,1,0:T(8,128)S(1)}, u32[]{:S(2)}, u32[]{:S(2)}) collective-permute-start(f32[2,64,128]{2,1,0:T(8,128)} %bitcast.12), channel_id=1, source_target_pairs={{0,64},{32,96},{64,0},{96,32},{128,192},{160,224},{192,128},{224,1... | collective-permute-start | bytes 196616 | tf_op jit(solution)/shard_map/ppermute | solution.py:481
  7.3 9.7 %collective-permute-start.3 = (f32[4,64,128]{2,1,0:T(8,128)S(1)}, f32[4,64,128]{2,1,0:T(8,128)S(1)}, u32[]{:S(2)}, u32[]{:S(2)}) collective-permute-start(f32[4,64,128]{2,1,0:T(8,128)S(1)} %pad_maximum_fusion.2), channel_id=1, source_target_pairs={{0,256},{32,288},{64,320},{96,352},{128,384},{160,416},{192,448},{... | collective-permute-start | bytes 393224 | tf_op jit(solution)/shard_map/ppermute | solution.py:481
  17.0 36.1 %collective-permute-start.4 = (f32[8,64,128]{2,1,0:T(8,128)S(1)}, f32[8,64,128]{2,1,0:T(8,128)S(1)}, u32[]{:S(2)}, u32[]{:S(2)}) collective-permute-start(f32[8,64,128]{2,1,0:T(8,128)S(1)} %pad_maximum_fusion.1), channel_id=1, source_target_pairs={{0,128},{32,160},{64,192},{96,224},{128,0},{160,32},{192,64},{224,... | collective-permute-start | bytes 786440 | tf_op jit(solution)/shard_map/ppermute | solution.py:481
  24.6 7.9 %collective-permute-start = (f32[176,256]{1,0:T(8,128)S(1)}, f32[176,256]{1,0:T(8,128)S(1)}, u32[]{:S(2)}, u32[]{:S(2)}) collective-permute-start(f32[176,256]{1,0:T(8,128)S(1)} %get-tuple-element.20), channel_id=1, source_target_pairs={{0,1},{1,0},{2,3},{3,2},{4,5},{5,4},{6,7},{7,6},{8,9},{9,8},{10,11... | collective-permute-start | bytes 540680 | tf_op jit(solution)/shard_map/ppermute | solution.py:477
  29.3 3.2 %collective-permute-start.1 = (f32[176,256]{1,0:T(8,128)S(1)}, f32[176,256]{1,0:T(8,128)S(1)}, u32[]{:S(2)}, u32[]{:S(2)}) collective-permute-start(f32[176,256]{1,0:T(8,128)S(1)} %get-tuple-element.21), channel_id=1, source_target_pairs={{1,2},{3,4},{5,6},{7,8},{9,10},{11,12},{13,14},{15,16},{17,18},{19... | collective-permute-start | bytes 540680 | tf_op jit(solution)/shard_map/ppermute | solution.py:476
  35.6 26.9 %all-to-all-start = ((f32[32,8,128]{2,1,0:T(8,128)}), f32[32,8,128]{2,1,0:T(8,128)S(1)}, u32[]{:S(2)}, u32[]{:S(2)}) async-start(f32[32,8,128]{2,1,0:T(8,128)} %get-tuple-element.32), calls=%async_computation | async-start | bytes 262144 | tf_op jit(solution)/shard_map/all_to_all | solution.py:489
  53.2 40.4 %collective-permute-start.5 = (f32[16,64,128]{2,1,0:T(8,128)S(1)}, f32[16,64,128]{2,1,0:T(8,128)S(1)}, u32[]{:S(2)}, u32[]{:S(2)}) collective-permute-start(f32[16,64,128]{2,1,0:T(8,128)S(1)} %pad_maximum_fusion.here), channel_id=1, source_target_pairs={{0,32},{32,0},{64,96},{96,64},{128,160},{160,128},{192,224},{224,1... | collective-permute-start | bytes 1572872 | tf_op jit(solution)/shard_map/ppermute | solution.py:499
  79.9 13.7 %all-to-all-start.2 = ((f32[32,8,128]{2,1,0:T(8,128)}), f32[32,8,128]{2,1,0:T(8,128)S(1)}, u32[]{:S(2)}, u32[]{:S(2)}) async-start(f32[32,8,128]{2,1,0:T(8,128)} %moments.1), calls=%async_computation.2 | async-start | bytes 262144 | tf_op jit(solution)/shard_map/all_to_all | solution.py:497
